TPU v7x, 128 devices: a whole 4x4x4 slice. The times are simulated.
128 devices in a mesh: dp: 2 (over z_hi), expert: 64 (over z_lo, y, x, core).
Axes of the slice: x: 4, y: 4, z: 4 (z_hi: 2, z_lo: 2; z = z_hi * 2 + z_lo), core: 2. Of those that a mesh axis runs over, the one named last changes fastest.
Arguments:
- tokens_in: bfloat16 [16384, 2880], P(('dp', 'expert')), may hold values from -6 to 6
- grad_out: bfloat16 [16384, 2880], P(('dp', 'expert')), may hold values from -6 to 6
- expert_ids: int32 [16384, 4], P(('dp', 'expert')), may hold values from 0 to 63, all different within a row; in each aligned block of 128 rows (0 to 127, 128 to 255, ...) at most 10 rows name the same one
- combine_weights: float32 [16384, 4], P(('dp', 'expert')), may hold values from 0.1 to 1
- up_weight: bfloat16 [64, 2880, 1440], P('expert'), may hold values from -0.109375 to 0.109375
- down_weight: bfloat16 [64, 1440, 2880], P('expert'), may hold values from -0.15625 to 0.15625
Outputs:
- grad_input: bfloat16 [16384, 2880], P(('dp', 'expert'))
- grad_up: bfloat16 [64, 2880, 1440], P('expert', 'dp')
- grad_down: bfloat16 [64, 1440, 2880], P('expert', 'dp')
Inputs may be any that keep to these rules, and one draw needn't show every extreme that they name: `expert_ids`: each row names 4 different experts; in the rows of one device no expert is named by more than 10 rows, a bound that some block reaches.
All inputs are finite; a program needn't handle non-finite values.
Results may differ from a plain program's by a relative error of at most 0.0064.
Values may be sent and summed in bfloat16 or wider, within the bound.
No kernel may reach another device: no remote copies, remote signals or barrier semaphores. Data moves between devices by JAX's collectives and lax.ppermute only.
A program may use at most 192 MiB of HBM per device.

v0:
```python
import jax
import jax.numpy as jnp
from jax import lax
from jax.sharding import PartitionSpec as P


def silu_parts(preact):
    logistic = jax.nn.sigmoid(preact)
    return (preact * logistic, logistic * (1.0 + preact * (1.0 - logistic)))


def contract_rows(left, right):
    return lax.dot_general(
        left, right, (((0,), (0,)), ((), ())), preferred_element_type=jnp.float32
    )


def contract_cols(left, right):
    return lax.dot_general(
        left, right, (((1,), (1,)), ((), ())), preferred_element_type=jnp.float32
    )


def local(tokens_in, grad_out, expert_ids, combine_weights, up_weight, down_weight):
    token_count, model_width = tokens_in.shape
    top_count = expert_ids.shape[1]
    expert_group = lax.axis_size("expert")
    experts_all = expert_group * up_weight.shape[0]
    capacity = 5 * token_count * top_count // (4 * experts_all)
    routed = token_count * top_count
    flat_ids = expert_ids.reshape(-1)
    one_hot = (flat_ids[:, None] == jnp.arange(experts_all, dtype=jnp.int32)[None, :]).astype(
        jnp.int32
    )
    slot_rank = jnp.sum((jnp.cumsum(one_hot, axis=0) - one_hot) * one_hot, axis=1)
    position = flat_ids * capacity + slot_rank
    slot_table = (
        jnp.full((experts_all * capacity,), routed, jnp.int32)
        .at[position]
        .set(jnp.arange(routed, dtype=jnp.int32))
    )
    source_token = slot_table // top_count
    padded_x = jnp.concatenate([tokens_in, jnp.zeros((1, model_width), tokens_in.dtype)], axis=0)
    padded_dy = jnp.concatenate([grad_out, jnp.zeros((1, model_width), grad_out.dtype)], axis=0)
    padded_weight = jnp.concatenate(
        [combine_weights.reshape(-1), jnp.zeros((1,), jnp.float32)], axis=0
    )
    send_x = padded_x[source_token].reshape(experts_all, capacity, model_width)
    send_grad = (
        padded_weight[slot_table][:, None] * padded_dy[source_token].astype(jnp.float32)
    ).astype(jnp.bfloat16)
    send_grad = send_grad.reshape(experts_all, capacity, model_width)
    w_up = up_weight[0]
    w_down = down_weight[0]
    hidden_width = w_up.shape[1]
    slot_x = lax.all_to_all(send_x, "expert", split_axis=0, concat_axis=0, tiled=True)
    slot_grad = lax.all_to_all(send_grad, "expert", split_axis=0, concat_axis=0, tiled=True)
    sources = slot_x.shape[0]
    slot_count = slot_x.shape[1]
    rows_x = slot_x.reshape(-1, model_width)
    rows_grad = slot_grad.reshape(-1, model_width)
    preact = jnp.dot(rows_x, w_up, preferred_element_type=jnp.float32)
    activated, slope = silu_parts(preact)
    activated = activated.astype(jnp.bfloat16)
    grad_act = contract_cols(rows_grad, w_down)
    grad_pre = (grad_act * slope).astype(jnp.bfloat16)
    grad_rows = (
        contract_cols(grad_pre, w_up).astype(jnp.bfloat16).reshape(sources, slot_count, model_width)
    )
    returned = lax.all_to_all(grad_rows, "expert", split_axis=0, concat_axis=0, tiled=True)
    returned, activated, grad_pre, slot_x, slot_grad = (
        returned,
        activated.reshape(sources, slot_count, hidden_width),
        grad_pre.reshape(sources, slot_count, hidden_width),
        slot_x,
        slot_grad,
    )
    picked = returned.reshape(-1, model_width)[position].reshape(
        token_count, top_count, model_width
    )
    grad_input = jnp.sum(picked.astype(jnp.float32), axis=1).astype(jnp.bfloat16)
    rows_x = slot_x.reshape(-1, model_width)
    rows_grad = slot_grad.reshape(-1, model_width)
    activated = activated.reshape(-1, hidden_width)
    grad_pre = grad_pre.reshape(-1, hidden_width)
    column_x, column_act = (
        lax.all_to_all(rows_x, "dp", split_axis=1, concat_axis=0, tiled=True),
        lax.all_to_all(activated, "dp", split_axis=1, concat_axis=0, tiled=True),
    )
    every_pre, every_grad = (
        lax.all_gather(grad_pre, "dp", axis=0, tiled=True),
        lax.all_gather(rows_grad, "dp", axis=0, tiled=True),
    )
    grad_up = contract_rows(column_x, every_pre)
    grad_down = contract_rows(column_act, every_grad)
    return (grad_input, grad_up.astype(jnp.bfloat16)[None], grad_down.astype(jnp.bfloat16)[None])


def solution(mesh):
    return jax.shard_map(
        local,
        mesh=mesh,
        in_specs=(
            P(("dp", "expert"), None),
            P(("dp", "expert"), None),
            P(("dp", "expert"), None),
            P(("dp", "expert"), None),
            P("expert", None, None),
            P("expert", None, None),
        ),
        out_specs=(P(("dp", "expert"), None), P("expert", "dp", None), P("expert", "dp", None)),
        check_vma=False,
    )
```

profile of v0, /device:TPU:1, one launch (start us, length us, event | category | flops | bytes accessed | tf_op | source)
XLA Modules:
  0.0 488.0 jit_solution(5856224476482001629)
XLA Ops:
  7.2 0.8 copy.24
  8.2 0.7 broadcast_multiply_fusion
  8.9 1.2 reduce-window.6
  10.1 0.2 slice_reduce_fusion
  10.4 0.1 copy.23
  10.6 0.1 fusion.19
  10.7 2.4 scatter_custom_fusion
  13.2 1.5 copy.28
  14.7 4.6 gather_fusion.2
  19.3 7.3 %reshape.95 = bf16[64,10,2880]{2,1,0:T(8,128)(2,1)} reshape(bf16[640,2880]{1,0:T(8,128)(2,1)} %gather_fusion.2) | data formatting | bytes 7372800 | tf_op jit(solution)/shard_map/reshape | solution.py:48
  26.6 10.6 %all-to-all-start.1 = ((bf16[64,10,2880]{2,1,0:T(8,128)(2,1)}), bf16[64,10,2880]{2,1,0:T(8,128)(2,1)}, u32[]{:S(2)}, u32[]{:S(2)}) async-start(bf16[64,10,2880]{2,1,0:T(8,128)(2,1)} %reshape.95), calls=%async_computation.1 | async-start | bytes 12058624 | tf_op jit(solution)/shard_map/all_to_all | solution.py:56
  37.2 0.3 copy.27
  37.7 4.6 gather_fusion.1
  42.2 7.9 %reshape.100 = f32[64,10,2880]{2,1,0:T(8,128)} reshape(bf16[640,2880]{1,0:T(8,128)(2,1)} %gather_fusion.1) | data formatting | bytes 11059200 | tf_op jit(solution)/shard_map/convert_element_type | solution.py:50
  50.2 0.1 copy.22
  50.4 2.8 gather_fusion
  53.2 0.1 mul.46
  53.3 8.4 %multiply_convert_fusion = bf16[64,10,2880]{2,1,0:T(8,128)(2,1)} fusion(f32[64,10,2880]{2,1,0:T(8,128)} %reshape.100, f32[64,10]{1,0:T(8,128)S(1)} %mul.46), kind=kLoop, calls=%fused_computation.5 | loop fusion | flops 3686400 | bytes 11061760 | tf_op jit(solution)/shard_map/convert_element_type | solution.py:51
  61.7 50.2 %all-to-all-done.1 = bf16[64,10,2880]{2,1,0:T(8,128)(2,1)} async-done(((bf16[64,10,2880]{2,1,0:T(8,128)(2,1)}), bf16[64,10,2880]{2,1,0:T(8,128)(2,1)}, u32[]{:S(2)}, u32[]{:S(2)}) %all-to-all-start.1) | async-done | bytes 3686432 | tf_op jit(solution)/shard_map/all_to_all | solution.py:56
  111.9 10.6 %all-to-all-start = ((bf16[64,10,2880]{2,1,0:T(8,128)(2,1)}), bf16[64,10,2880]{2,1,0:T(8,128)(2,1)}, u32[]{:S(2)}, u32[]{:S(2)}) async-start(bf16[64,10,2880]{2,1,0:T(8,128)(2,1)} %multiply_convert_fusion), calls=%async_computation | async-start | bytes 12058624 | tf_op jit(solution)/shard_map/all_to_all | solution.py:57
  122.5 0.2 all-gather.3.cloned.1.call-start
  122.7 7.8 %reshape.96 = bf16[640,2880]{1,0:T(8,128)(2,1)} reshape(bf16[64,10,2880]{2,1,0:T(8,128)(2,1)} %all-to-all-done.1) | data formatting | bytes 7372800 | tf_op jit(solution)/shard_map/reshape | solution.py:60
  130.5 12.3 %multiply_convert_fusion.1 = (bf16[640,1440]{0,1:T(8,128)(2,1)}, f32[640,1440]{0,1:T(8,128)}) fusion(bf16[640,2880]{1,0:T(8,128)(2,1)} %reshape.96, bf16[1,2880,1440]{1,2,0:T(8,128)(2,1)} %param.10), kind=kOutput, calls=%fused_computation.18 | convolution fusion | flops 5313024000 | bytes 17510400 | tf_op jit(solution)/shard_map/dot_general | solution.py:62
  142.8 54.4 %all-to-all-done = bf16[64,10,2880]{2,1,0:T(8,128)(2,1)} async-done(((bf16[64,10,2880]{2,1,0:T(8,128)(2,1)}), bf16[64,10,2880]{2,1,0:T(8,128)(2,1)}, u32[]{:S(2)}, u32[]{:S(2)}) %all-to-all-start) | async-done | bytes 3686432 | tf_op jit(solution)/shard_map/all_to_all | solution.py:57
  197.2 7.8 %reshape.94 = bf16[640,2880]{1,0:T(8,128)(2,1)} reshape(bf16[64,10,2880]{2,1,0:T(8,128)(2,1)} %all-to-all-done) | data formatting | bytes 7372800 | tf_op jit(solution)/shard_map/reshape | solution.py:61
  205.0 12.4 %fusion.14 = bf16[640,1440]{0,1:T(8,128)(2,1)} fusion(f32[640,1440]{0,1:T(8,128)} %get-tuple-element.9, bf16[640,2880]{1,0:T(8,128)(2,1)} %reshape.94, bf16[1,1440,2880]{2,1,0:T(8,128)(2,1)} %param.11), kind=kOutput, calls=%fused_computation.20 | convolution fusion | flops 5316710400 | bytes 17510400 | tf_op jit(solution)/shard_map/dot_general | solution.py:19
  217.5 4.6 all-to-all-start.4
  222.0 0.7 all-gather.5.cloned.1.call-update
  222.8 12.6 %all_to_all.40 = bf16[640,2,1440]{2,1,0:T(2,128)(2,1)} reshape(bf16[64,10,2880]{2,1,0:T(8,128)(2,1)} %all-to-all-done.1) | data formatting | bytes 7372800 | tf_op jit(solution)/shard_map/all_to_all | solution.py:87
  235.4 10.6 %copy.30 = bf16[640,2,1440]{0,2,1:T(8,128)(2,1)} copy(bf16[640,2,1440]{2,1,0:T(2,128)(2,1)} %all_to_all.40) | data formatting | bytes 7372800 | tf_op jit(solution)/shard_map/all_to_all | solution.py:87
  246.0 4.9 %all-to-all-done.4 = bf16[640,2,720]{0,2,1:T(8,128)(2,1)S(1)} async-done(((bf16[640,2,720]{0,2,1:T(8,128)(2,1)}), bf16[640,2,720]{0,2,1:T(8,128)(2,1)S(1)}, u32[]{:S(2)}, u32[]{:S(2)}) %all-to-all-start.4) | async-done | bytes 1843232 | tf_op jit(solution)/shard_map/all_to_all | solution.py:88
  250.9 5.5 %all-to-all-start.3 = ((bf16[640,2,1440]{0,2,1:T(8,128)(2,1)}), bf16[640,2,1440]{0,2,1:T(8,128)(2,1)}, u32[]{:S(2)}, u32[]{:S(2)}) async-start(bf16[640,2,1440]{0,2,1:T(8,128)(2,1)} %copy.30), calls=%async_computation.3 | async-start | bytes 7372800 | tf_op jit(solution)/shard_map/all_to_all | solution.py:87
  256.4 11.8 %fusion.7 = bf16[640,2880]{0,1:T(8,128)(2,1)} fusion(bf16[640,1440]{0,1:T(8,128)(2,1)} %fusion.14, bf16[1,2880,1440]{1,2,0:T(8,128)(2,1)} %param.10), kind=kOutput, calls=%fused_computation.15 | convolution fusion | flops 5310259200 | bytes 13824000 | tf_op jit(solution)/shard_map/dot_general | solution.py:19
  268.3 6.2 %copy.29 = bf16[640,2880]{1,0:T(8,128)(2,1)} copy(bf16[640,2880]{0,1:T(8,128)(2,1)} %fusion.7) | data formatting | bytes 7372800 | tf_op jit(solution)/shard_map/convert_element_type | solution.py:68
  274.4 7.3 %reshape.97 = bf16[64,10,2880]{2,1,0:T(8,128)(2,1)} reshape(bf16[640,2880]{1,0:T(8,128)(2,1)} %copy.29) | data formatting | bytes 7372800 | tf_op jit(solution)/shard_map/reshape | solution.py:68
  281.7 41.0 %all-to-all-done.3 = bf16[640,2,1440]{0,2,1:T(8,128)(2,1)} async-done(((bf16[640,2,1440]{0,2,1:T(8,128)(2,1)}), bf16[640,2,1440]{0,2,1:T(8,128)(2,1)}, u32[]{:S(2)}, u32[]{:S(2)}) %all-to-all-start.3) | async-done | bytes 3686432 | tf_op jit(solution)/shard_map/all_to_all | solution.py:87
  322.7 14.4 %all-to-all-start.2 = ((bf16[64,10,2880]{2,1,0:T(8,128)(2,1)}), bf16[64,10,2880]{2,1,0:T(8,128)(2,1)}, u32[]{:S(2)}, u32[]{:S(2)}) async-start(bf16[64,10,2880]{2,1,0:T(8,128)(2,1)} %reshape.97), calls=%async_computation.2 | async-start | bytes 12058624 | tf_op jit(solution)/shard_map/all_to_all | solution.py:70
  337.1 1.4 copy.36
  338.5 4.3 copy.35
  342.7 69.0 %all-to-all-done.2 = bf16[64,10,2880]{2,1,0:T(8,128)(2,1)} async-done(((bf16[64,10,2880]{2,1,0:T(8,128)(2,1)}), bf16[64,10,2880]{2,1,0:T(8,128)(2,1)}, u32[]{:S(2)}, u32[]{:S(2)}) %all-to-all-start.2) | async-done | bytes 3686432 | tf_op jit(solution)/shard_map/all_to_all | solution.py:70
  411.7 7.8 %reshape.98 = bf16[640,2880]{1,0:T(8,128)(2,1)} reshape(bf16[64,10,2880]{2,1,0:T(8,128)(2,1)} %all-to-all-done.2) | data formatting | bytes 7372800 | tf_op jit(solution)/shard_map/reshape | solution.py:78
  419.5 9.3 %gather_fusion.3 = bf16[512,2880]{1,0:T(8,128)(2,1)} fusion(bf16[640,2880]{1,0:T(8,128)(2,1)} %reshape.98, s32[1024]{0:T(1024)S(1)} %pad_clamp_fusion), kind=kCustom, calls=%fused_computation.3 | custom fusion | bytes 5900288 | tf_op jit(solution)/shard_map/gather | solution.py:78
  428.8 4.7 reshape.99
  433.5 4.9 %reduce_sum.25 = bf16[128,2880]{1,0:T(8,128)(2,1)} reduce(bf16[128,4,2880]{2,1,0:T(4,128)(2,1)S(1)} %reshape.99, bf16[]{:T(256)} %constant.34.clone.1), dimensions={1}, to_apply=%region_4.5 | reduce | flops 1105920 | bytes 3686402 | tf_op jit(solution)/shard_map/reduce_sum | solution.py:81
  438.4 2.3 copy.33
  440.7 10.2 %fusion.6 = bf16[1,1440,1440]{2,1,0:T(8,128)(2,1)} fusion(bf16[1280,1440]{0,1:T(8,128)(2,1)} %bitcast.56, bf16[1280,1440]{0,1:T(8,128)(2,1)} %all-gather.3.cloned.1.call-done), kind=kOutput, calls=%fused_computation.13 | convolution fusion | flops 5310489600 | bytes 11520000 | tf_op jit(solution)/shard_map/dot_general | solution.py:13
  450.9 19.7 %all-gather.5.cloned.1.call-done = bf16[1280,2880]{1,0:T(8,128)(2,1)} async-done(((bf16[640,2880]{1,0:T(8,128)(2,1)}), bf16[1280,2880]{1,0:T(8,128)(2,1)}) %all-gather.5.cloned.1.call-update) | async-done | bytes 7372816 | tf_op jit(solution)/shard_map/all_gather | solution.py:92
  470.6 10.6 %fusion.10 = bf16[1,720,2880]{2,1,0:T(8,128)(2,1)} fusion(bf16[1280,720]{0,1:T(8,128)(2,1)S(1)} %bitcast.58, bf16[1280,2880]{1,0:T(8,128)(2,1)} %all-gather.5.cloned.1.call-done), kind=kOutput, calls=%fused_computation.16 | convolution fusion | flops 5310489600 | bytes 13363200 | tf_op jit(solution)/shard_map/dot_general | solution.py:13
  (24 shorter events, 0.7 us)
Async XLA Ops:
  26.6 10.6 %copy-start.1 = (bf16[128,2880]{0,1:T(8,128)(2,1)S(1)}, bf16[128,2880]{0,1:T(8,128)(2,1)}, u32[]{:S(2)}) copy-start(bf16[128,2880]{0,1:T(8,128)(2,1)} %param.7) | copy-start | bytes 2211844
  26.6 85.3 %all-to-all-start.1 = ((bf16[64,10,2880]{2,1,0:T(8,128)(2,1)}), bf16[64,10,2880]{2,1,0:T(8,128)(2,1)}, u32[]{:S(2)}, u32[]{:S(2)}) async-start(bf16[64,10,2880]{2,1,0:T(8,128)(2,1)} %reshape.95), calls=%async_computation.1 | async-start | bytes 12058624 | tf_op jit(solution)/shard_map/all_to_all | solution.py:56
  42.2 7.9 %copy-start.2 = (f32[128,4]{0,1:T(4,128)S(1)}, f32[128,4]{0,1:T(4,128)}, u32[]{:S(2)}) copy-start(f32[128,4]{0,1:T(4,128)} %param.9) | copy-start | bytes 6148
  111.9 85.3 %all-to-all-start = ((bf16[64,10,2880]{2,1,0:T(8,128)(2,1)}), bf16[64,10,2880]{2,1,0:T(8,128)(2,1)}, u32[]{:S(2)}, u32[]{:S(2)}) async-start(bf16[64,10,2880]{2,1,0:T(8,128)(2,1)} %multiply_convert_fusion), calls=%async_computation | async-start | bytes 12058624 | tf_op jit(solution)/shard_map/all_to_all | solution.py:57
  122.5 318.1 %all-gather.3.cloned.1.call-start = ((), (), s32[]{:S(2)}) async-start(), calls=%async_computation.5 | async-start | bytes 5529600 | tf_op jit(solution)/shard_map/all_gather | solution.py:91
  217.5 33.5 %all-to-all-start.4 = ((bf16[640,2,720]{0,2,1:T(8,128)(2,1)}), bf16[640,2,720]{0,2,1:T(8,128)(2,1)S(1)}, u32[]{:S(2)}, u32[]{:S(2)}) async-start(bf16[640,2,720]{0,2,1:T(8,128)(2,1)} %bitcast.57), calls=%async_computation.4 | async-start | bytes 3686400 | tf_op jit(solution)/shard_map/all_to_all | solution.py:88
  222.0 248.5 %all-gather.5.cloned.1.call-start = ((), (), s32[]{:S(2)}) async-start(), calls=%async_computation.6 | async-start | bytes 11304960 | tf_op jit(solution)/shard_map/all_gather | solution.py:92
  250.9 71.7 %all-to-all-start.3 = ((bf16[640,2,1440]{0,2,1:T(8,128)(2,1)}), bf16[640,2,1440]{0,2,1:T(8,128)(2,1)}, u32[]{:S(2)}, u32[]{:S(2)}) async-start(bf16[640,2,1440]{0,2,1:T(8,128)(2,1)} %copy.30), calls=%async_computation.3 | async-start | bytes 7372800 | tf_op jit(solution)/shard_map/all_to_all | solution.py:87
  322.7 89.1 %all-to-all-start.2 = ((bf16[64,10,2880]{2,1,0:T(8,128)(2,1)}), bf16[64,10,2880]{2,1,0:T(8,128)(2,1)}, u32[]{:S(2)}, u32[]{:S(2)}) async-start(bf16[64,10,2880]{2,1,0:T(8,128)(2,1)} %reshape.97), calls=%async_computation.2 | async-start | bytes 12058624 | tf_op jit(solution)/shard_map/all_to_all | solution.py:70
  440.7 29.9 %copy-start = (bf16[2,90,8,640]{3,2,0,1:T(8,128)(2,1)S(1)}, bf16[2,90,8,640]{3,2,0,1:T(8,128)(2,1)}, u32[]{:S(2)}) copy-start(bf16[2,90,8,640]{3,2,0,1:T(8,128)(2,1)} %copy.36) | copy-start | bytes 5529604
Sparse Core Ops, SparseCore 0:
  217.6 90.2 all-gather.2
  309.5 161.0 all-gather.4
where the time goes:
time: 492 us; the launch traced here: 488 us
  waiting for transfers between devices  240 us (49%)
  local copies, waits for them, and re-layouts  115 us (23%)
  matrix products  57.3 us (12%)
  starting transfers between devices  45.9 us (9%)
  other arithmetic  15.4 us (3%)
  between operations  14.2 us (3%)
    all_to_all x1, waiting for transfers between devices, local(): lax.all_to_all(grad_rows, 'expert', split_axis=0, concat_axis=0, tiled=True)  69 us
    all_to_all x1, waiting for transfers between devices, local(): lax.all_to_all(send_grad, 'expert', split_axis=0, concat_axis=0, tiled=True)  54.4 us
    all_to_all x1, waiting for transfers between devices, local(): lax.all_to_all(send_x, 'expert', split_axis=0, concat_axis=0, tiled=True)  50.2 us
    all_to_all x1, waiting for transfers between devices, local(): lax.all_to_all(rows_x, 'dp', split_axis=1, concat_axis=0, tiled=True)  41 us
    all_to_all x3, local copies, waits for them, and re-layouts, local(): lax.all_to_all(rows_x, 'dp', split_axis=1, concat_axis=0, tiled=True)  27.5 us
    dot_general x2, matrix products, contract_cols(): lax.dot_general(left, right, (((1,), (1,)), ((), ())), preferred_element_...  24.2 us
    dot_general x2, matrix products, contract_rows(): lax.dot_general(left, right, (((0,), (0,)), ((), ())), preferred_element_...  20.8 us
    all_gather x1, waiting for transfers between devices, local(): lax.all_gather(rows_grad, 'dp', axis=0, tiled=True)  19.7 us
  transfers between devices with their start and end apart: 7, of which 6 were waited for; matrix products, arithmetic and copies ran while one was open for 26% of the time, Pallas kernels for 0%

commit v1 on v0

v1 whole, which is shorter than its diff:
```python
import functools

import jax
import jax.numpy as jnp
from jax import lax
from jax.experimental import pallas as pl
from jax.experimental.pallas import tpu as pltpu
from jax.sharding import Mesh, PartitionSpec as P

LW = 1536
QW = 768
BF = jnp.bfloat16
F32 = jnp.float32
ALL = ("dp", "zl", "y", "x", "core")
GROUP = ("zl", "y", "x", "core")
PLANE = ("y", "x", "core")
ANY = pl.BlockSpec(memory_space=pl.ANY)
SMEM = pl.BlockSpec(memory_space=pltpu.SMEM)
VLIMIT = 62 * 1024 * 1024


def iota(shape, dim):
    return lax.broadcasted_iota(jnp.int32, shape, dim)


def onehot(cond):
    return jnp.where(cond, 1.0, 0.0).astype(BF)


def dot_nn(left, right):
    return lax.dot_general(left, right, (((1,), (0,)), ((), ())), preferred_element_type=F32)


def dot_nt(left, right):
    return lax.dot_general(left, right, (((1,), (1,)), ((), ())), preferred_element_type=F32)


def dot_tn(left, right):
    return lax.dot_general(left, right, (((0,), (0,)), ((), ())), preferred_element_type=F32)


def rank_rows(ids, weights, first, experts):
    top, tokens = ids.shape
    index = iota((experts, tokens), 0) + first
    member = jnp.zeros((experts, tokens), F32)
    weight = jnp.zeros((experts, tokens), F32)
    for k in range(top):
        hit = ids[k : k + 1, :] == index
        member = member + jnp.where(hit, 1.0, 0.0)
        weight = weight + jnp.where(hit, weights[k : k + 1, :], 0.0)
    before = onehot(iota((tokens, tokens), 0) < iota((tokens, tokens), 1))
    rank = member * (dot_nn(member.astype(BF), before) + 1.0)
    spread = onehot(iota((experts * 8, experts), 0) // 8 == iota((experts * 8, experts), 1))
    w1 = weight.astype(BF)
    rest = weight - w1.astype(F32)
    w2 = rest.astype(BF)
    w3 = (rest - w2.astype(F32)).astype(BF)
    low = dot_nn(spread, w2) + dot_nn(spread, w3)
    return dot_nn(spread, rank.astype(BF)), dot_nn(spread, w1) + low


def padded(piece):
    if piece.shape[0] == LW:
        return piece
    return jnp.concatenate([piece, jnp.zeros((LW - piece.shape[0], piece.shape[1]), piece.dtype)], axis=0)


def row_weight(hit, weight):
    return jnp.sum(jnp.where(hit, weight, 0.0), axis=1, keepdims=True)


def pack_own_body(ids_ref, w_ref, x_ref, dy_ref, out_ref, rank_ref, weight_s):
    step = pl.program_id(0)
    rows, tokens = rank_ref.shape
    width = x_ref.shape[0]

    @pl.when(step == 0)
    def _():
        rank, weight = rank_rows(ids_ref[...], w_ref[...], 0, rows // 8)
        rank_ref[...] = rank
        weight_s[...] = weight

    slot = iota((rows, tokens), 0) % 8
    pieces = ((x_ref, 0, LW), (x_ref, LW, width - LW), (dy_ref, 0, LW), (dy_ref, LW, width - LW))
    for g in range(4):

        @pl.when(step == g)
        def _(g=g):
            ref, start, size = pieces[g]
            hit = rank_ref[...] == (slot + 1).astype(F32)
            value = dot_nt(onehot(hit), padded(ref[pl.ds(start, size), :]))
            if g >= 2:
                value = value * row_weight(hit, weight_s[...])
            out_ref[...] = value.reshape(rows // 8, 1, 8, LW).astype(BF)

    @pl.when(step == 4)
    def _():
        hit = rank_ref[...] == (slot % 2 + 9).astype(F32)
        which = slot // 2
        picks = jnp.concatenate([onehot(hit & (which == c)) for c in range(4)], axis=1)
        source = jnp.concatenate([padded(ref[pl.ds(start, size), :]) for ref, start, size in pieces], axis=1)
        value = dot_nt(picks, source)
        scale = jnp.where(which[:, :1] >= 2, row_weight(hit, weight_s[...]), 1.0)
        out_ref[...] = (value * scale).reshape(rows // 8, 1, 8, LW).astype(BF)


def pack_own(ids, weights, x, dy, peers):
    tokens = ids.shape[1]
    whole = lambda a: pl.BlockSpec(a.shape, lambda g: (0, 0))
    return pl.pallas_call(
        pack_own_body,
        grid=(5,),
        in_specs=[whole(ids), whole(weights), whole(x), whole(dy)],
        out_specs=[
            pl.BlockSpec((peers, 1, 8, LW), lambda g: (0, g, 0, 0)),
            pl.BlockSpec((peers * 8, tokens), lambda g: (0, 0)),
        ],
        out_shape=[
            jax.ShapeDtypeStruct((peers, 5, 8, LW), BF),
            jax.ShapeDtypeStruct((peers * 8, tokens), F32),
        ],
        scratch_shapes=[pltpu.VMEM((peers * 8, tokens), F32)],
        compiler_params=pltpu.CompilerParams(vmem_limit_bytes=VLIMIT),
        name="pack_own",
    )(ids, weights, x, dy)


def pack_other_body(zl_ref, pa_ref, pb_ref, ma_ref, mb_ref, out_ref, rank_s, weight_s):
    step = pl.program_id(0)
    _, rows, tokens = rank_s.shape
    top = ma_ref.shape[0] // 2
    half = pa_ref.shape[0] // 3

    @pl.when(step == 0)
    def _():
        for s, meta in enumerate((ma_ref, mb_ref)):
            ids = meta[pl.ds(0, top), :].astype(jnp.int32)
            rank, weight = rank_rows(ids, meta[pl.ds(top, top), :], zl_ref[0] * (rows // 8), rows // 8)
            rank_s[s] = rank
            weight_s[s] = weight

    slot = iota((rows, tokens), 0) % 8
    spans = ((half, LW), (half + LW, 2 * half - LW), (0, half))
    pays = (pa_ref, pb_ref)
    for c in range(3):
        for s in range(2):

            @pl.when(step == c * 2 + s)
            def _(c=c, s=s):
                start, size = spans[c]
                hit = rank_s[s] == (slot + 1).astype(F32)
                value = dot_nt(onehot(hit), padded(pays[s][pl.ds(start, size), :]))
                if c < 2:
                    value = value * row_weight(hit, weight_s[s])
                out_ref[...] = value.reshape(rows // 8, 1, 8, LW).astype(BF)

    def remainder(pieces, per_piece):
        picks, source = [], []
        scale = jnp.zeros((rows, 1), F32)
        for s in range(2):
            hit = rank_s[s] == (slot % 2 + 9).astype(F32)
            scale = scale + jnp.where((slot[:, :1] // 2) % 2 == s, row_weight(hit, weight_s[s]), 0.0)
            for n, c in enumerate(pieces):
                mine = hit & (slot // 2 == n * 2 + s)
                picks.append(onehot(mine))
                start, size = spans[c]
                source.append(padded(pays[s][pl.ds(start, size), :]))
        value = dot_nt(jnp.concatenate(picks, axis=1), jnp.concatenate(source, axis=1))
        if per_piece:
            value = value * scale
        out_ref[...] = value.reshape(rows // 8, 1, 8, LW).astype(BF)

    @pl.when(step == 6)
    def _():
        remainder((0, 1), True)

    @pl.when(step == 7)
    def _():
        remainder((2,), False)


def pack_other(zl, pay_a, pay_b, meta_a, meta_b, peers):
    tokens = meta_a.shape[1]
    whole = lambda a: pl.BlockSpec(a.shape, lambda g: (0, 0))
    return pl.pallas_call(
        pack_other_body,
        grid=(8,),
        in_specs=[SMEM, whole(pay_a), whole(pay_b), whole(meta_a), whole(meta_b)],
        out_specs=pl.BlockSpec((peers, 1, 8, LW), lambda g: (0, g, 0, 0)),
        out_shape=jax.ShapeDtypeStruct((peers, 8, 8, LW), BF),
        scratch_shapes=[pltpu.VMEM((2, peers * 8, tokens), F32), pltpu.VMEM((2, peers * 8, tokens), F32)],
        compiler_params=pltpu.CompilerParams(vmem_limit_bytes=VLIMIT),
        name="pack_other",
    )(zl, pay_a, pay_b, meta_a, meta_b)


def blocks(total, size):
    return [(start, min(size, total - start)) for start in range(0, total, size)]


def expert_body(
    dp_ref, slab, wup, wdn, ret_o, gp_o, keep_o, send_o, xh_o, dy_o,
    x3, dy3, xr, dyr, rem, wu, wd, act_s, gp_s, keep_s, send_s, xh_s, ret, rest, sems, osems,
):
    peers = slab.shape[0]
    main = peers * 8
    rows = main + peers * 2
    hidden, width = wu.shape
    copies = [
        pltpu.make_async_copy(src, dst, sems.at[i])
        for i, (src, dst) in enumerate(
            (
                (slab.at[:, 0], x3.at[pl.ds(0, peers), :, pl.ds(0, LW)]),
                (slab.at[:, 1], xr),
                (slab.at[:, 4], rem),
                (wup, wu),
                (slab.at[:, 2], dy3.at[pl.ds(0, peers), :, pl.ds(0, LW)]),
                (slab.at[:, 3], dyr),
                (wdn, wd),
            )
        )
    ]
    for copy in copies:
        copy.start()
    right = width - LW
    for i in range(3):
        copies[i].wait()
    x3[pl.ds(0, peers), :, pl.ds(LW, right)] = xr[:, :, pl.ds(0, right)]
    last = rem[...].reshape(main, LW)
    r_i = iota((peers * 2, main), 0)
    c_i = iota((peers * 2, main), 1)
    for c in range(4):
        pick = onehot(c_i == (r_i // 2) * 8 + 2 * c + r_i % 2)
        dst = (x3, dy3)[c // 2]
        start, size = ((0, LW), (LW, right))[c % 2]
        value = dot_nn(pick, last[:, :size])
        dst[pl.ds(peers, peers // 4), :, pl.ds(start, size)] = value.reshape(peers // 4, 8, size).astype(BF)
    for i in range(3, 7):
        copies[i].wait()
    dy3[pl.ds(0, peers), :, pl.ds(LW, right)] = dyr[:, :, pl.ds(0, right)]
    out_dy = pltpu.make_async_copy(dy3, dy_o, osems.at[0])
    out_dy.start()
    for start, size in blocks(hidden, 512):
        pre = dot_nt(x3[...].reshape(rows, width), wu[pl.ds(start, size), :])
        s = jax.nn.sigmoid(pre)
        act_s[:, pl.ds(start, size)] = (pre * s).astype(BF)
        slope = s * (1.0 + pre * (1.0 - s))
        grad = dot_nt(dy3[...].reshape(rows, width), wd[pl.ds(start, size), :])
        gp_s[:, pl.ds(start, size)] = (grad * slope).astype(BF)
    out_gp = pltpu.make_async_copy(gp_s, gp_o, osems.at[1])
    out_gp.start()
    first = dp_ref[0] == 0
    a0 = act_s[:, pl.ds(0, hidden // 2)]
    a1 = act_s[:, pl.ds(hidden // 2, hidden // 2)]
    keep_s[...] = jnp.where(first, a0, a1)
    send_s[...] = jnp.where(first, a1, a0)
    out_keep = pltpu.make_async_copy(keep_s, keep_o, osems.at[2])
    out_send = pltpu.make_async_copy(send_s, send_o, osems.at[3])
    out_keep.start()
    out_send.start()
    x0 = x3[:, :, pl.ds(0, width // 2)]
    x1 = x3[:, :, pl.ds(width // 2, width // 2)]
    xh_s[...] = jnp.where(first, x0, x1)
    out_xh = pltpu.make_async_copy(xh_s, xh_o, osems.at[4])
    out_xh.start()
    outs = [out_dy, out_gp, out_keep, out_send, out_xh]
    rest[...] = jnp.zeros(rest.shape, F32)
    r_j = iota((main, peers * 2), 0)
    c_j = iota((main, peers * 2), 1)
    for q, (start, size) in enumerate(blocks(width, QW)):
        value = dot_nn(gp_s[...], wu[:, pl.ds(start, size)]).astype(BF)
        head = value[:main].reshape(peers, 8, size)
        if size < QW:
            ret[:, q] = jnp.zeros((peers, 8, QW), BF)
        ret[:, q, :, pl.ds(0, size)] = head
        place = onehot(((r_j % 8) // 2 == q) & (c_j == (r_j // 8) * 2 + r_j % 2))
        rest[:, pl.ds(0, size)] = rest[:, pl.ds(0, size)] + dot_nn(place, value[main:])
        copy = pltpu.make_async_copy(ret.at[:, q], ret_o.at[:, q], osems.at[5 + q])
        copy.start()
        outs.append(copy)
    ret[:, 4] = rest[...].reshape(peers, 8, QW).astype(BF)
    copy = pltpu.make_async_copy(ret.at[:, 4], ret_o.at[:, 4], osems.at[9])
    copy.start()
    outs.append(copy)
    for copy in outs:
        copy.wait()


def expert(dp, slab, wup, wdn):
    peers = slab.shape[0]
    hidden, width = wup.shape
    rows = peers * 10
    tiles = rows // 8
    sds = jax.ShapeDtypeStruct
    return pl.pallas_call(
        expert_body,
        in_specs=[SMEM, ANY, ANY, ANY],
        out_specs=[ANY] * 6,
        out_shape=[
            sds((peers, 5, 8, QW), BF),
            sds((rows, hidden), BF),
            sds((rows, hidden // 2), BF),
            sds((rows, hidden // 2), BF),
            sds((tiles, 8, width // 2), BF),
            sds((tiles, 8, width), BF),
        ],
        scratch_shapes=[
            pltpu.VMEM((tiles, 8, width), BF),
            pltpu.VMEM((tiles, 8, width), BF),
            pltpu.VMEM((peers, 8, LW), BF),
            pltpu.VMEM((peers, 8, LW), BF),
            pltpu.VMEM((peers, 8, LW), BF),
            pltpu.VMEM((hidden, width), BF),
            pltpu.VMEM((hidden, width), BF),
            pltpu.VMEM((rows, hidden), BF),
            pltpu.VMEM((rows, hidden), BF),
            pltpu.VMEM((rows, hidden // 2), BF),
            pltpu.VMEM((rows, hidden // 2), BF),
            pltpu.VMEM((tiles, 8, width // 2), BF),
            pltpu.VMEM((peers, 5, 8, QW), BF),
            pltpu.VMEM((peers * 8, QW), F32),
            pltpu.SemaphoreType.DMA((7,)),
            pltpu.SemaphoreType.DMA((10,)),
        ],
        compiler_params=pltpu.CompilerParams(vmem_limit_bytes=VLIMIT),
        cost_estimate=pl.CostEstimate(flops=6 * rows * hidden * width, transcendentals=rows * hidden, bytes_accessed=40_000_000),
        name="expert",
    )(dp, slab, wup, wdn)


def unpack_body(zl_ref, slab, dy_o, xh_o, dy3, xh3, dyr, xhr, r6, r7, sems):
    plane = slab.shape[0]
    peers = plane * 2
    width = dy3.shape[2]
    half = width // 2
    right = width - LW
    zl = zl_ref[0]
    copies = []
    for z in range(2):
        rel = lax.bitwise_xor(zl, z)
        span = pl.ds(z * plane, plane)
        copies.append(pltpu.make_async_copy(slab.at[:, rel], dy3.at[span, :, pl.ds(0, LW)], sems.at[3 * z]))
        copies.append(pltpu.make_async_copy(slab.at[:, 2 + rel], dyr.at[span], sems.at[3 * z + 1]))
        copies.append(pltpu.make_async_copy(slab.at[:, 4 + rel], xhr.at[span], sems.at[3 * z + 2]))
    copies.append(pltpu.make_async_copy(slab.at[:, 6], r6, sems.at[6]))
    copies.append(pltpu.make_async_copy(slab.at[:, 7], r7, sems.at[7]))
    for copy in copies:
        copy.start()
    for copy in copies:
        copy.wait()
    dy3[pl.ds(0, peers), :, pl.ds(LW, right)] = dyr[:, :, pl.ds(0, right)]
    xh3[pl.ds(0, peers)] = xhr[:, :, pl.ds(0, half)]
    r_i = iota((peers * 2, plane * 8), 0)
    c_i = iota((peers * 2, plane * 8), 1)
    rel = lax.bitwise_xor(r_i // peers, zl)
    base = ((r_i // 2) % plane) * 8 + rel * 2 + r_i % 2
    for c in range(3):
        source = (r6 if c < 2 else r7)[...].reshape(plane * 8, LW)
        size = (LW, right, half)[c]
        value = dot_nn(onehot(c_i == base + (4 if c == 1 else 0)), source[:, :size])
        value = value.reshape(peers // 4, 8, size).astype(BF)
        if c < 2:
            dy3[pl.ds(peers, peers // 4), :, pl.ds(c * LW, size)] = value
        else:
            xh3[pl.ds(peers, peers // 4)] = value
    outs = [
        pltpu.make_async_copy(dy3, dy_o, sems.at[8]),
        pltpu.make_async_copy(xh3, xh_o, sems.at[9]),
    ]
    for copy in outs:
        copy.start()
    for copy in outs:
        copy.wait()


def unpack_other(zl, slab, width):
    plane = slab.shape[0]
    peers = plane * 2
    tiles = peers * 10 // 8
    sds = jax.ShapeDtypeStruct
    return pl.pallas_call(
        unpack_body,
        in_specs=[SMEM, ANY],
        out_specs=[ANY, ANY],
        out_shape=[sds((tiles, 8, width), BF), sds((tiles, 8, width // 2), BF)],
        scratch_shapes=[
            pltpu.VMEM((tiles, 8, width), BF),
            pltpu.VMEM((tiles, 8, width // 2), BF),
            pltpu.VMEM((peers, 8, LW), BF),
            pltpu.VMEM((peers, 8, LW), BF),
            pltpu.VMEM((plane, 8, LW), BF),
            pltpu.VMEM((plane, 8, LW), BF),
            pltpu.SemaphoreType.DMA((10,)),
        ],
        compiler_params=pltpu.CompilerParams(vmem_limit_bytes=VLIMIT),
        name="unpack_other",
    )(zl, slab)


def combine_body(rank_ref, ret_ref, out_ref):
    peers = ret_ref.shape[0]
    rows, tokens = rank_ref.shape
    width = out_ref.shape[0]
    slot = iota((rows, tokens), 0) % 8
    rank = rank_ref[...]
    main = onehot(rank == (slot + 1).astype(F32))
    last = rank == (slot % 2 + 9).astype(F32)
    for q, (start, size) in enumerate(blocks(width, QW)):
        pick = jnp.concatenate([main, onehot(last & (slot // 2 == q))], axis=0)
        got = jnp.concatenate([ret_ref[:, q].reshape(rows, QW), ret_ref[:, 4].reshape(rows, QW)], axis=0)
        value = dot_tn(pick, got[:, :size])
        out_ref[pl.ds(start, size), :] = value.T.astype(BF)


def combine(rank, ret, width):
    return pl.pallas_call(
        combine_body,
        out_shape=jax.ShapeDtypeStruct((width, rank.shape[1]), BF),
        compiler_params=pltpu.CompilerParams(vmem_limit_bytes=VLIMIT),
        name="combine",
    )(rank, ret)


def local(sizes, tokens_in, grad_out, expert_ids, combine_weights, up_weight, down_weight):
    n_dp, n_zl, n_plane = sizes
    peers = n_zl * n_plane
    width = tokens_in.shape[1]
    half = width // 2
    x = tokens_in.T
    dy = grad_out.T
    ids = expert_ids.T
    weights = combine_weights.T
    dp = lax.axis_index("dp").astype(jnp.int32)
    zl = lax.axis_index("zl").astype(jnp.int32)

    def other(value, flip):
        pairs = []
        for i in range(n_dp * peers):
            d, z, p = i // peers, (i // n_plane) % n_zl, i % n_plane
            pairs.append((i, ((1 - d) * n_zl + (z ^ flip)) * n_plane + p))
        return lax.ppermute(value, ALL, pairs)

    pay = jnp.concatenate([lax.dynamic_slice_in_dim(x, (1 - dp) * half, half, 0), dy], axis=0)
    meta = jnp.concatenate([ids.astype(F32), weights], axis=0)
    meta_a, meta_b = other(meta, 0), other(meta, 1)
    pay_a, pay_b = other(pay, 0), other(pay, 1)

    slab, rank = pack_own(ids, weights, x, dy, peers)
    got = lax.all_to_all(slab, GROUP, 0, 0, tiled=True)
    slab_other = pack_other(zl[None], pay_a, pay_b, meta_a, meta_b, n_plane)
    got_other = lax.all_to_all(slab_other, PLANE, 0, 0, tiled=True)

    ret, gp, act, act_send, xh, dyr = expert(dp[None], got, up_weight[0].T, down_weight[0])
    back = lax.all_to_all(ret, GROUP, 0, 0, tiled=True)
    gp_other = other(gp, 0)
    act_other = other(act_send, 0)
    dy_other, xh_other = unpack_other(zl[None], got_other, width)

    flat = lambda a: a.reshape(-1, a.shape[-1])
    grad_up = dot_tn(flat(xh), gp) + dot_tn(flat(xh_other), gp_other)
    grad_down = dot_tn(act, flat(dyr)) + dot_tn(act_other, flat(dy_other))
    grad_input = combine(rank, back, width).T
    return (grad_input, grad_up.astype(BF)[None], grad_down.astype(BF)[None])


def build(devices, shape):
    n_dp, n_zl, n_y, n_x, n_core = shape
    fine = Mesh(devices.reshape(shape), ALL)
    token = P(ALL, None)
    weight = P(GROUP, None, None)
    return jax.shard_map(
        functools.partial(local, (n_dp, n_zl, n_y * n_x * n_core)),
        mesh=fine,
        in_specs=(token, token, token, token, weight, weight),
        out_specs=(token, P(GROUP, "dp", None), P(GROUP, "dp", None)),
        check_vma=False,
    )


def solution(mesh):
    return build(mesh.devices, (2, 2, 4, 4, 2))
```

time: 492 us -> 352 us (0.72)
  local copies, waits for them, and re-layouts: 115 us -> 5.22 us
  Pallas kernels: 0 us -> 67.5 us
  matrix products: 57.3 us -> 20.9 us
  waiting for transfers between devices: 240 us -> 212 us
  other arithmetic: 15.4 us -> 1.07 us
  between operations: 14.2 us -> 1.02 us
  starting transfers between devices: 45.9 us -> 37.6 us
    all_to_all x5 -> x3, waiting for transfers between devices: 219 us -> 32.2 us  [the longest x1 32.2 us: local(): got_other = lax.all_to_all(slab_other, PLANE, 0, 0, tiled=True)]
    ppermute x0 -> x6, waiting for transfers between devices: none -> 179 us  [other(): return lax.ppermute(value, ALL, pairs)]
    pallas_call x0 -> x5, Pallas kernels: none -> 67.5 us  [the longest x1 41.2 us: expert(): pl.pallas_call(expert_body, in_specs=[SMEM, ANY, ANY, ANY], out_specs=[AN...]
    reshape x7 -> x0, local copies, waits for them, and re-layouts: 42.7 us -> none  [the longest x2 12.4 us: local(): returned.reshape(-1, model_width)[position]]
    dot_general x5 -> x4, matrix products: 57.3 us -> 20.9 us  [dot_tn(): lax.dot_general(left, right, (((0,), (0,)), ((), ())), preferred_element_...]
    all_to_all x4 -> x0, local copies, waits for them, and re-layouts: 28.9 us -> none  [the longest x3 27.5 us: local(): lax.all_to_all(rows_x, 'dp', split_axis=1, concat_axis=0, tiled=True)]
    gather x4 -> x0, local copies, waits for them, and re-layouts: 21.2 us -> none  [the longest x1 9.28 us: local(): returned.reshape(-1, model_width)[position]]
    all_gather x2 -> x0, waiting for transfers between devices: 19.7 us -> none  [the longest x1 19.7 us: local(): lax.all_gather(rows_grad, 'dp', axis=0, tiled=True)]
  transfers between devices with their start and end apart: 7 -> 9, of which waited for: 6 -> 5; matrix products, arithmetic and copies ran while one was open for 26% -> 8% of each run, Pallas kernels for 0% -> 16%
where the time goes in v1:
time: 352 us; the launch traced here: 345 us
  waiting for transfers between devices  212 us (60%)
  Pallas kernels  67.5 us (19%)
  starting transfers between devices  37.6 us (11%)
  matrix products  20.9 us (6%)
  local copies, waits for them, and re-layouts  5.22 us (1%)
    ppermute x6, waiting for transfers between devices, other(): return lax.ppermute(value, ALL, pairs)  179 us
    pallas_call x1, Pallas kernels, expert(): pl.pallas_call(expert_body, in_specs=[SMEM, ANY, ANY, ANY], out_specs=[AN...  41.2 us
    all_to_all x1, waiting for transfers between devices, local(): got_other = lax.all_to_all(slab_other, PLANE, 0, 0, tiled=True)  32.2 us
    dot_general x4, matrix products, dot_tn(): lax.dot_general(left, right, (((0,), (0,)), ((), ())), preferred_element_...  20.9 us
    all_to_all x1, starting transfers between devices, local(): got = lax.all_to_all(slab, GROUP, 0, 0, tiled=True)  10.6 us
    ppermute x6, starting transfers between devices, other(): return lax.ppermute(value, ALL, pairs)  9.73 us
    all_to_all x1, starting transfers between devices, local(): back = lax.all_to_all(ret, GROUP, 0, 0, tiled=True)  9.54 us
    pallas_call x1, Pallas kernels, pack_other(): pl.pallas_call(pack_other_body, grid=(8,), in_specs=[SMEM, whole(pay_a),...  8.07 us
  transfers between devices with their start and end apart: 9, of which 5 were waited for; matrix products, arithmetic and copies ran while one was open for 8% of the time, Pallas kernels for 16%

profile of v1, /device:TPU:1, one launch (start us, length us, event | category | flops | bytes accessed | tf_op | source)
XLA Modules:
  0.0 345.0 jit_solution(11119921322798876839)
XLA Ops:
  0.6 7.8 %pack_own.1 = (bf16[64,5,8,1536]{3,2,1,0:T(8,128)(2,1)}, f32[512,128]{1,0:T(8,128)}) custom-call(s32[4,128]{1,0:T(4,128)} %bitcast.38, f32[4,128]{1,0:T(4,128)} %bitcast.39, bf16[2880,128]{1,0:T(8,128)(2,1)} %bitcast.36, bf16[2880,128]{1,0:T(8,128)(2,1)} %bitcast.34), custom_call_target="tpu_custom_call" | custom-call | tf_op jit(solution)/shard_map/pack_own/pallas_call | solution.py:110
  8.5 0.0 copy-start.3
  8.5 0.0 copy-start.1
  8.5 0.0 copy-start.6
  8.5 0.0 copy-start.7
  8.5 10.6 %all-to-all-start = ((bf16[64,5,8,1536]{3,2,1,0:T(8,128)(2,1)}), bf16[64,5,8,1536]{3,2,1,0:T(8,128)(2,1)}, u32[]{:S(2)}, u32[]{:S(2)}) async-start(bf16[64,5,8,1536]{3,2,1,0:T(8,128)(2,1)} %get-tuple-element.14), calls=%async_computation | async-start | bytes 15728640 | tf_op jit(solution)/shard_map/all_to_all | solution.py:449
  19.2 0.0 copy-done.3
  19.2 0.0 copy-done.1
  19.2 1.1 pad_maximum_fusion
  20.3 3.6 %collective-permute-start.1 = (bf16[4320,128]{1,0:T(8,128)(2,1)}, bf16[4320,128]{1,0:T(8,128)(2,1)S(1)}, u32[]{:S(2)}, u32[]{:S(2)}) collective-permute-start(bf16[4320,128]{1,0:T(8,128)(2,1)} %pad_maximum_fusion), channel_id=1, source_target_pairs={{0,96},{1,97},{2,98},{3,99},{4,100},{5,101},{6,102},{7,103},{8,104... | collective-permute-start | bytes 3317768 | tf_op jit(solution)/shard_map/ppermute | solution.py:441
  23.9 0.0 collective-permute-start
  23.9 0.0 copy-done.6
  23.9 0.0 copy-done.7
  23.9 1.9 collective-permute-start.3
  25.7 1.3 collective-permute-start.2
  27.0 23.6 %collective-permute-done.3.mb_ref = f32[8,128]{1,0:T(8,128)S(1)} collective-permute-done((f32[8,128]{1,0:T(8,128)S(1)}, f32[8,128]{1,0:T(8,128)S(1)}, u32[]{:S(2)}, u32[]{:S(2)}) %collective-permute-start.3) | collective-permute-done | bytes 4128 | tf_op jit(solution)/shard_map/ppermute | solution.py:441
  50.6 81.3 %collective-permute-done.2.ma_ref = f32[8,128]{1,0:T(8,128)S(1)} collective-permute-done((f32[8,128]{1,0:T(8,128)S(1)}, f32[8,128]{1,0:T(8,128)S(1)}, u32[]{:S(2)}, u32[]{:S(2)}) %collective-permute-start.2) | collective-permute-done | bytes 4128 | tf_op jit(solution)/shard_map/ppermute | solution.py:441
  131.9 0.0 collective-permute-done.1.pb_ref
  131.9 0.0 collective-permute-done.pa_ref
  131.9 0.0 copy-done.8
  131.9 0.6 copy-done.9
  132.5 0.4 copy-done.4
  132.9 8.1 %pack_other.1 = bf16[32,8,8,1536]{3,2,1,0:T(8,128)(2,1)} custom-call(s32[1]{0:T(128)} %bitcast.10.zl_ref, bf16[4320,128]{1,0:T(8,128)(2,1)} %collective-permute-done.pa_ref, bf16[4320,128]{1,0:T(8,128)(2,1)} %copy-done.4, f32[8,128]{1,0:T(8,128)} %copy-done.9, f32[8,128]{1,0:T(8,128)} %copy-done.8), custom_call_target="tpu_custom_call" | custom-call | tf_op jit(solution)/shard_map/pack_other/pallas_call | solution.py:185
  141.0 0.0 all-to-all-done.slab
  141.0 7.7 %all-to-all-start.2 = ((bf16[32,8,8,1536]{3,2,1,0:T(8,128)(2,1)}), bf16[32,8,8,1536]{3,2,1,0:T(8,128)(2,1)}, u32[]{:S(2)}, u32[]{:S(2)}) async-start(bf16[32,8,8,1536]{3,2,1,0:T(8,128)(2,1)} %pack_other.1), calls=%async_computation.2 | async-start | bytes 12582912 | tf_op jit(solution)/shard_map/all_to_all | solution.py:451
  148.7 41.2 %expert.1 = (bf16[64,5,8,768]{3,2,1,0:T(8,128)(2,1)}, bf16[640,1440]{1,0:T(8,128)(2,1)}, bf16[640,720]{1,0:T(8,128)(2,1)}, bf16[640,720]{1,0:T(8,128)(2,1)}, bf1...) custom-call(s32[1]{0:T(128)} %bitcast.4.dp_ref, bf16[64,5,8,1536]{3,2,1,0:T(8,128)(2,1)} %all-to-all-done.slab, ...), custom_call_target="tpu_custom_call" | custom-call | flops 15925248000 | bytes 40000000 | tf_op jit(solution)/shard_map/expert/pallas_call | solution.py:295
  189.9 32.2 %all-to-all-done.2.slab = bf16[32,8,8,1536]{3,2,1,0:T(8,128)(2,1)} async-done(((bf16[32,8,8,1536]{3,2,1,0:T(8,128)(2,1)}), bf16[32,8,8,1536]{3,2,1,0:T(8,128)(2,1)}, u32[]{:S(2)}, u32[]{:S(2)}) %all-to-all-start.2) | async-done | bytes 6291488 | tf_op jit(solution)/shard_map/all_to_all | solution.py:451
  222.1 9.5 %all-to-all-start.1 = ((bf16[64,5,8,768]{3,2,1,0:T(8,128)(2,1)}), bf16[64,5,8,768]{3,2,1,0:T(8,128)(2,1)}, u32[]{:S(2)}, u32[]{:S(2)}) async-start(bf16[64,5,8,768]{3,2,1,0:T(8,128)(2,1)} %get-tuple-element.15), calls=%async_computation.1 | async-start | bytes 7864320 | tf_op jit(solution)/shard_map/all_to_all | solution.py:454
  231.6 0.0 copy-start.2
  231.7 6.1 %unpack_other.1 = (bf16[80,8,2880]{2,1,0:T(8,128)(2,1)}, bf16[80,8,1440]{2,1,0:T(8,128)(2,1)}) custom-call(s32[1]{0:T(128)} %bitcast.10.zl_ref, bf16[32,8,8,1536]{3,2,1,0:T(8,128)(2,1)} %all-to-all-done.2.slab), custom_call_target="tpu_custom_call" | custom-call | tf_op jit(solution)/shard_map/unpack_other/pallas_call | solution.py:381
  237.8 1.9 copy.10
  239.7 0.1 collective-permute-start.5
  239.8 0.0 copy-done.2
  239.8 2.2 copy.9
  242.1 2.9 collective-permute-start.4
  245.0 5.4 %fusion.7 = f32[1440,1440]{1,0:T(8,128)S(1)} fusion(bf16[640,1440]{1,0:T(8,128)(2,1)S(1)} %copy-done.2, bf16[80,8,1440]{2,1,0:T(8,128)(2,1)} %get-tuple-element.16), kind=kOutput, calls=%fused_computation.9 | convolution fusion | flops 2654208000 | bytes 11980800 | tf_op jit(solution)/shard_map/dot_general | solution.py:39
  250.4 0.0 copy-done
  250.4 0.0 copy-done.5
  250.4 0.0 copy-start.10
  250.4 3.6 %fusion.4 = f32[720,2880]{1,0:T(8,128)S(1)} fusion(bf16[640,720]{1,0:T(8,128)(2,1)S(1)} %copy-done.5, bf16[80,8,2880]{2,1,0:T(8,128)(2,1)S(1)} %copy-done), kind=kOutput, calls=%fused_computation.6 | convolution fusion | flops 2654208000 | bytes 12902400 | tf_op jit(solution)/shard_map/dot_general | solution.py:39
  254.1 41.7 %collective-permute-done.5 = bf16[640,720]{0,1:T(8,128)(2,1)} collective-permute-done((bf16[640,720]{0,1:T(8,128)(2,1)S(1)}, bf16[640,720]{0,1:T(8,128)(2,1)}, u32[]{:S(2)}, u32[]{:S(2)}) %collective-permute-start.5) | collective-permute-done | bytes 921632 | tf_op jit(solution)/shard_map/ppermute | solution.py:441
  295.7 0.0 copy-done.10
  295.7 6.5 %fusion.2 = bf16[1,720,2880]{2,1,0:T(8,128)(2,1)} fusion(f32[720,2880]{1,0:T(8,128)S(1)} %fusion.4, bf16[640,720]{0,1:T(8,128)(2,1)} %collective-permute-done.5, bf16[80,8,2880]{2,1,0:T(8,128)(2,1)S(1)} %copy-done.10), kind=kOutput, calls=%fused_computation.4 | convolution fusion | flops 2658355200 | bytes 17049600 | tf_op jit(solution)/shard_map/dot_general | solution.py:39
  302.2 32.9 %collective-permute-done.4 = bf16[640,1440]{0,1:T(8,128)(2,1)S(1)} collective-permute-done((bf16[640,1440]{0,1:T(8,128)(2,1)}, bf16[640,1440]{0,1:T(8,128)(2,1)S(1)}, u32[]{:S(2)}, u32[]{:S(2)}) %collective-permute-start.4) | collective-permute-done | bytes 1843232 | tf_op jit(solution)/shard_map/ppermute | solution.py:441
  335.1 0.0 copy-done.11
  335.1 5.4 %fusion.1 = bf16[1,1440,1440]{2,1,0:T(8,128)(2,1)} fusion(f32[1440,1440]{1,0:T(8,128)S(1)} %fusion.7, bf16[640,1440]{0,1:T(8,128)(2,1)S(1)} %collective-permute-done.4, bf16[80,8,1440]{2,1,0:T(8,128)(2,1)S(1)} %copy-done.11), kind=kOutput, calls=%fused_computation.3 | convolution fusion | flops 2658355200 | bytes 16128000 | tf_op jit(solution)/shard_map/dot_general | solution.py:39
  340.6 0.0 all-to-all-done.1.ret_ref
  340.6 4.2 %combine.1 = bf16[2880,128]{1,0:T(8,128)(2,1)} custom-call(f32[512,128]{1,0:T(8,128)} %get-tuple-element.13.rank_ref, bf16[64,5,8,768]{3,2,1,0:T(8,128)(2,1)} %all-to-all-done.1.ret_ref), custom_call_target="tpu_custom_call" | custom-call | tf_op jit(solution)/shard_map/combine/pallas_call | solution.py:416
  (9 shorter events, 0.1 us)
Async XLA Ops:
  8.5 10.7 %copy-start.3 = (bf16[128,2880]{0,1:T(8,128)(2,1)S(1)}, bf16[128,2880]{0,1:T(8,128)(2,1)}, u32[]{:S(2)}) copy-start(bf16[128,2880]{0,1:T(8,128)(2,1)} %param.6) | copy-start | bytes 2211844
  8.5 10.7 %copy-start.1 = (bf16[128,2880]{0,1:T(8,128)(2,1)S(1)}, bf16[128,2880]{0,1:T(8,128)(2,1)}, u32[]{:S(2)}) copy-start(bf16[128,2880]{0,1:T(8,128)(2,1)} %param.7) | copy-start | bytes 2211844
  8.5 15.4 %copy-start.6 = (s32[128,4]{0,1:T(4,128)S(1)}, s32[128,4]{0,1:T(4,128)}, u32[]{:S(2)}) copy-start(s32[128,4]{0,1:T(4,128)} %param.8) | copy-start | bytes 6148
  8.5 15.4 %copy-start.7 = (f32[128,4]{0,1:T(4,128)S(1)}, f32[128,4]{0,1:T(4,128)}, u32[]{:S(2)}) copy-start(f32[128,4]{0,1:T(4,128)} %param.9) | copy-start | bytes 6148
  8.5 132.5 %all-to-all-start = ((bf16[64,5,8,1536]{3,2,1,0:T(8,128)(2,1)}), bf16[64,5,8,1536]{3,2,1,0:T(8,128)(2,1)}, u32[]{:S(2)}, u32[]{:S(2)}) async-start(bf16[64,5,8,1536]{3,2,1,0:T(8,128)(2,1)} %get-tuple-element.14), calls=%async_computation | async-start | bytes 15728640 | tf_op jit(solution)/shard_map/all_to_all | solution.py:449
  20.3 111.6 %collective-permute-start.1 = (bf16[4320,128]{1,0:T(8,128)(2,1)}, bf16[4320,128]{1,0:T(8,128)(2,1)S(1)}, u32[]{:S(2)}, u32[]{:S(2)}) collective-permute-start(bf16[4320,128]{1,0:T(8,128)(2,1)} %pad_maximum_fusion), channel_id=1, source_target_pairs={{0,96},{1,97},{2,98},{3,99},{4,100},{5,101},{6,102},{7,103},{8,104... | collective-permute-start | bytes 3317768 | tf_op jit(solution)/shard_map/ppermute | solution.py:441
  23.9 108.1 %collective-permute-start = (bf16[4320,128]{1,0:T(8,128)(2,1)}, bf16[4320,128]{1,0:T(8,128)(2,1)}, u32[]{:S(2)}, u32[]{:S(2)}) collective-permute-start(bf16[4320,128]{1,0:T(8,128)(2,1)} %pad_maximum_fusion), channel_id=1, source_target_pairs={{0,64},{1,65},{2,66},{3,67},{4,68},{5,69},{6,70},{7,71},{8,72},{9,... | collective-permute-start | bytes 3317768 | tf_op jit(solution)/shard_map/ppermute | solution.py:441
  23.9 26.7 %collective-permute-start.3 = (f32[8,128]{1,0:T(8,128)S(1)}, f32[8,128]{1,0:T(8,128)S(1)}, u32[]{:S(2)}, u32[]{:S(2)}) collective-permute-start(f32[8,128]{1,0:T(8,128)S(1)} %pad_maximum_fusion.1), channel_id=1, source_target_pairs={{0,96},{1,97},{2,98},{3,99},{4,100},{5,101},{6,102},{7,103},{8,104... | collective-permute-start | bytes 12296 | tf_op jit(solution)/shard_map/ppermute | solution.py:441
  25.7 106.2 %collective-permute-start.2 = (f32[8,128]{1,0:T(8,128)S(1)}, f32[8,128]{1,0:T(8,128)S(1)}, u32[]{:S(2)}, u32[]{:S(2)}) collective-permute-start(f32[8,128]{1,0:T(8,128)S(1)} %pad_maximum_fusion.1), channel_id=1, source_target_pairs={{0,64},{1,65},{2,66},{3,67},{4,68},{5,69},{6,70},{7,71},{8,72},{9,... | collective-permute-start | bytes 12296 | tf_op jit(solution)/shard_map/ppermute | solution.py:441
  50.6 81.3 %copy-start.8 = (f32[8,128]{1,0:T(8,128)}, f32[8,128]{1,0:T(8,128)S(1)}, u32[]{:S(2)}) copy-start(f32[8,128]{1,0:T(8,128)S(1)} %collective-permute-done.3.mb_ref) | copy-start | bytes 12292
  131.9 0.6 copy-start.9
  131.9 1.0 copy-start.4
  141.0 81.1 %all-to-all-start.2 = ((bf16[32,8,8,1536]{3,2,1,0:T(8,128)(2,1)}), bf16[32,8,8,1536]{3,2,1,0:T(8,128)(2,1)}, u32[]{:S(2)}, u32[]{:S(2)}) async-start(bf16[32,8,8,1536]{3,2,1,0:T(8,128)(2,1)} %pack_other.1), calls=%async_computation.2 | async-start | bytes 12582912 | tf_op jit(solution)/shard_map/all_to_all | solution.py:451
  222.1 118.5 %all-to-all-start.1 = ((bf16[64,5,8,768]{3,2,1,0:T(8,128)(2,1)}), bf16[64,5,8,768]{3,2,1,0:T(8,128)(2,1)}, u32[]{:S(2)}, u32[]{:S(2)}) async-start(bf16[64,5,8,768]{3,2,1,0:T(8,128)(2,1)} %get-tuple-element.15), calls=%async_computation.1 | async-start | bytes 7864320 | tf_op jit(solution)/shard_map/all_to_all | solution.py:454
  231.6 8.2 %copy-start.2 = (bf16[640,1440]{1,0:T(8,128)(2,1)S(1)}, bf16[640,1440]{1,0:T(8,128)(2,1)}, u32[]{:S(2)}) copy-start(bf16[640,1440]{1,0:T(8,128)(2,1)} %get-tuple-element.17) | copy-start | bytes 5529604
  239.7 56.0 %collective-permute-start.5 = (bf16[640,720]{0,1:T(8,128)(2,1)S(1)}, bf16[640,720]{0,1:T(8,128)(2,1)}, u32[]{:S(2)}, u32[]{:S(2)}) collective-permute-start(bf16[640,720]{0,1:T(8,128)(2,1)S(1)} %copy.10), channel_id=1, source_target_pairs={{0,64},{1,65},{2,66},{3,67},{4,68},{5,69},{6,70},{7,71},{8,72},{9,... | collective-permute-start | bytes 2764808 | tf_op jit(solution)/shard_map/ppermute | solution.py:441
  242.1 93.1 %collective-permute-start.4 = (bf16[640,1440]{0,1:T(8,128)(2,1)}, bf16[640,1440]{0,1:T(8,128)(2,1)S(1)}, u32[]{:S(2)}, u32[]{:S(2)}) collective-permute-start(bf16[640,1440]{0,1:T(8,128)(2,1)} %copy.9), channel_id=1, source_target_pairs={{0,64},{1,65},{2,66},{3,67},{4,68},{5,69},{6,70},{7,71},{8,72},{9,... | collective-permute-start | bytes 5529608 | tf_op jit(solution)/shard_map/ppermute | solution.py:441
  245.0 5.4 %copy-start = (bf16[80,8,2880]{2,1,0:T(8,128)(2,1)S(1)}, bf16[80,8,2880]{2,1,0:T(8,128)(2,1)}, u32[]{:S(2)}) copy-start(bf16[80,8,2880]{2,1,0:T(8,128)(2,1)} %get-tuple-element.20) | copy-start | bytes 11059204
  245.0 5.4 %copy-start.5 = (bf16[640,720]{1,0:T(8,128)(2,1)S(1)}, bf16[640,720]{1,0:T(8,128)(2,1)}, u32[]{:S(2)}) copy-start(bf16[640,720]{1,0:T(8,128)(2,1)} %get-tuple-element.19) | copy-start | bytes 2764804
  250.4 45.4 %copy-start.10 = (bf16[80,8,2880]{2,1,0:T(8,128)(2,1)S(1)}, bf16[80,8,2880]{2,1,0:T(8,128)(2,1)}, u32[]{:S(2)}) copy-start(bf16[80,8,2880]{2,1,0:T(8,128)(2,1)} %get-tuple-element.22) | copy-start | bytes 11059204
  295.7 39.4 %copy-start.11 = (bf16[80,8,1440]{2,1,0:T(8,128)(2,1)S(1)}, bf16[80,8,1440]{2,1,0:T(8,128)(2,1)}, u32[]{:S(2)}) copy-start(bf16[80,8,1440]{2,1,0:T(8,128)(2,1)} %get-tuple-element.18) | copy-start | bytes 5529604

commit v2 on v1

v2 whole, which is shorter than its diff:
```python
import functools

import jax
import jax.numpy as jnp
from jax import lax
from jax.experimental import pallas as pl
from jax.experimental.pallas import tpu as pltpu
from jax.sharding import Mesh, PartitionSpec as P


LW = 1536
QW = 768
BF = jnp.bfloat16
F32 = jnp.float32
ALL = ("dp", "zl", "y", "x", "core")
GROUP = ("zl", "y", "x", "core")
PLANE = ("y", "x", "core")
ANY = pl.BlockSpec(memory_space=pl.ANY)
SMEM = pl.BlockSpec(memory_space=pltpu.SMEM)
VLIMIT = 62 * 1024 * 1024


def iota(shape, dim):
    return lax.broadcasted_iota(jnp.int32, shape, dim)


def onehot(cond):
    return jnp.where(cond, 1.0, 0.0).astype(BF)


def dot_nn(left, right):
    return lax.dot_general(left, right, (((1,), (0,)), ((), ())), preferred_element_type=F32)


def dot_nt(left, right):
    return lax.dot_general(left, right, (((1,), (1,)), ((), ())), preferred_element_type=F32)


def dot_tn(left, right):
    return lax.dot_general(left, right, (((0,), (0,)), ((), ())), preferred_element_type=F32)


def rank_rows(ids, parts, first, experts):
    top, tokens = ids.shape
    index = iota((experts, tokens), 0) + first
    member = jnp.zeros((experts, tokens), F32)
    weight = [jnp.zeros((experts, tokens), F32) for _ in parts]
    for k in range(top):
        hit = ids[k : k + 1, :] == index
        member = member + jnp.where(hit, 1.0, 0.0)
        weight = [w + jnp.where(hit, part[k : k + 1, :], 0.0) for w, part in zip(weight, parts)]
    before = onehot(iota((tokens, tokens), 0) < iota((tokens, tokens), 1))
    rank = member * (dot_nn(member.astype(BF), before) + 1.0)
    spread = onehot(iota((experts * 8, experts), 0) // 8 == iota((experts * 8, experts), 1))
    total = None
    for w in reversed(weight):
        piece = dot_nn(spread, w.astype(BF))
        total = piece if total is None else piece + total
    return dot_nn(spread, rank.astype(BF)), total


def padded(piece, width):
    if piece.shape[0] == width:
        return piece
    return jnp.concatenate([piece, jnp.zeros((width - piece.shape[0], piece.shape[1]), piece.dtype)], axis=0)


def row_weight(hit, weight):
    return jnp.sum(jnp.where(hit, weight, 0.0), axis=1, keepdims=True)


def blocks(total, size):
    return [(start, min(size, total - start)) for start in range(0, total, size)]


def pack_x_body(ids_ref, w_ref, x_ref, out_ref, rank_ref, meta_ref):
    step = pl.program_id(0)
    rows, tokens = rank_ref.shape

    @pl.when(step == 0)
    def _():
        rank, _ = rank_rows(ids_ref[...], [], 0, rows // 8)
        rank_ref[...] = rank
        meta_ref[...] = jnp.concatenate([ids_ref[...].astype(F32), w_ref[...]], axis=0)

    slot = iota((rows, tokens), 0) % 8
    pieces = blocks(x_ref.shape[0], QW)
    for q, (start, size) in enumerate(pieces):

        @pl.when(step == q)
        def _(start=start, size=size):
            hit = rank_ref[...] == (slot + 1).astype(F32)
            value = dot_nt(onehot(hit), padded(x_ref[pl.ds(start, size), :], QW))
            out_ref[...] = value.reshape(rows // 8, 1, 8, QW).astype(BF)

    @pl.when(step == 4)
    def _():
        hit = rank_ref[...] == (slot % 2 + 9).astype(F32)
        picks = jnp.concatenate([onehot(hit & (slot // 2 == q)) for q in range(4)], axis=1)
        source = jnp.concatenate([padded(x_ref[pl.ds(start, size), :], QW) for start, size in pieces], axis=1)
        out_ref[...] = dot_nt(picks, source).reshape(rows // 8, 1, 8, QW).astype(BF)


def pack_x(ids, weights, x, peers):
    tokens = ids.shape[1]
    whole = lambda a: pl.BlockSpec(a.shape, lambda g: (0, 0))
    return pl.pallas_call(
        pack_x_body,
        grid=(5,),
        in_specs=[whole(ids), whole(weights), whole(x)],
        out_specs=[
            pl.BlockSpec((peers, 1, 8, QW), lambda g: (0, g, 0, 0)),
            pl.BlockSpec((peers * 8, tokens), lambda g: (0, 0)),
            pl.BlockSpec((2 * ids.shape[0], tokens), lambda g: (0, 0)),
        ],
        out_shape=[
            jax.ShapeDtypeStruct((peers, 5, 8, QW), BF),
            jax.ShapeDtypeStruct((peers * 8, tokens), F32),
            jax.ShapeDtypeStruct((2 * ids.shape[0], tokens), F32),
        ],
        compiler_params=pltpu.CompilerParams(vmem_limit_bytes=VLIMIT),
        name="pack_x",
    )(ids, weights, x)


def pack_dy_body(spans, zl_ref, pa_ref, pb_ref, ma_ref, mb_ref, out_ref, rank_s, weight_s):
    step = pl.program_id(0)
    _, rows, tokens = rank_s.shape
    pays = (pa_ref, pb_ref)
    top = ma_ref.shape[0] // 2

    @pl.when(step == 0)
    def _():
        for s, meta in enumerate((ma_ref, mb_ref)):
            ids = meta[pl.ds(0, top), :].astype(jnp.int32)
            weight = meta[pl.ds(top, top), :]
            w1 = weight.astype(BF)
            rest = weight - w1.astype(F32)
            w2 = rest.astype(BF)
            w3 = (rest - w2.astype(F32)).astype(BF)
            parts = [w.astype(F32) for w in (w1, w2, w3)]
            rank, weight = rank_rows(ids, parts, zl_ref[0] * (rows // 8), rows // 8)
            rank_s[s] = rank
            weight_s[s] = weight

    slot = iota((rows, tokens), 0) % 8
    for c, (start, size) in enumerate(spans):
        for s in range(2):

            @pl.when(step == c * 2 + s)
            def _(start=start, size=size, s=s):
                hit = rank_s[s] == (slot + 1).astype(F32)
                value = dot_nt(onehot(hit), padded(pays[s][pl.ds(start, size), :], LW))
                value = value * row_weight(hit, weight_s[s])
                out_ref[...] = value.reshape(rows // 8, 1, 8, LW).astype(BF)

    @pl.when(step == 4)
    def _():
        picks, source = [], []
        scale = jnp.zeros((rows, 1), F32)
        for s in range(2):
            hit = rank_s[s] == (slot % 2 + 9).astype(F32)
            scale = scale + jnp.where((slot[:, :1] // 2) % 2 == s, row_weight(hit, weight_s[s]), 0.0)
            for c, (start, size) in enumerate(spans):
                picks.append(onehot(hit & (slot // 2 == c * 2 + s)))
                source.append(padded(pays[s][pl.ds(start, size), :], LW))
        value = dot_nt(jnp.concatenate(picks, axis=1), jnp.concatenate(source, axis=1))
        out_ref[...] = (value * scale).reshape(rows // 8, 1, 8, LW).astype(BF)


def pack_dy(zl, dy_a, dy_b, meta_a, meta_b, peers):
    width, tokens = dy_a.shape
    spans = ((0, LW), (LW, width - LW))
    whole = lambda a: pl.BlockSpec(a.shape, lambda g: (0, 0))
    return pl.pallas_call(
        functools.partial(pack_dy_body, spans),
        grid=(5,),
        in_specs=[SMEM, whole(dy_a), whole(dy_b), whole(meta_a), whole(meta_b)],
        out_specs=pl.BlockSpec((peers, 1, 8, LW), lambda g: (0, g, 0, 0)),
        out_shape=jax.ShapeDtypeStruct((peers, 5, 8, LW), BF),
        scratch_shapes=[pltpu.VMEM((2, peers * 8, tokens), F32), pltpu.VMEM((2, peers * 8, tokens), F32)],
        compiler_params=pltpu.CompilerParams(vmem_limit_bytes=VLIMIT),
    )(zl, dy_a, dy_b, meta_a, meta_b)


def load_plane(zl, slab, first, dst, tmp, sems):
    plane = slab.shape[0]
    copies = []
    for z in range(2):
        rel = lax.bitwise_xor(zl, z)
        span = pl.ds(z * plane, plane)
        copies.append(pltpu.make_async_copy(slab.at[:, first + rel], dst.at[span, :, pl.ds(0, LW)], sems.at[2 * z]))
        copies.append(pltpu.make_async_copy(slab.at[:, first + 2 + rel], tmp.at[span], sems.at[2 * z + 1]))
    for copy in copies:
        copy.start()
    return copies


def rem_rows(zl, last, piece, size):
    plane = last.shape[0]
    peers = plane * 2
    r_i = iota((peers * 2, plane * 8), 0)
    c_i = iota((peers * 2, plane * 8), 1)
    rel = lax.bitwise_xor(r_i // peers, zl)
    base = ((r_i // 2) % plane) * 8 + piece * 4 + rel * 2 + r_i % 2
    value = dot_nn(onehot(c_i == base), last[...].reshape(plane * 8, LW)[:, :size])
    return value.reshape(peers // 4, 8, size).astype(BF)


def pre_body(dp_ref, slab, wup, act_o, slope_o, xh_o, xs_o, x3, xq, rem, wu, act_s, slope_s, xh_s, xs_s, sems, osems):
    peers = slab.shape[0]
    main = peers * 8
    rows = main + peers * 2
    hidden, width = wu.shape
    pieces = blocks(width, QW)
    copies = [pltpu.make_async_copy(wup, wu, sems.at[5])]
    for q, (start, size) in enumerate(pieces):
        dst = xq if size < QW else x3.at[pl.ds(0, peers), :, pl.ds(start, QW)]
        copies.append(pltpu.make_async_copy(slab.at[:, q], dst, sems.at[q]))
    copies.append(pltpu.make_async_copy(slab.at[:, 4], rem, sems.at[4]))
    for copy in copies:
        copy.start()
    for copy in copies[1:]:
        copy.wait()
    start, size = pieces[-1]
    x3[pl.ds(0, peers), :, pl.ds(start, size)] = xq[:, :, pl.ds(0, size)]
    last = rem[...].reshape(main, QW)
    r_i = iota((peers * 2, main), 0)
    c_i = iota((peers * 2, main), 1)
    for q, (start, size) in enumerate(pieces):
        pick = onehot(c_i == (r_i // 2) * 8 + 2 * q + r_i % 2)
        value = dot_nn(pick, last[:, :size])
        x3[pl.ds(peers, peers // 4), :, pl.ds(start, size)] = value.reshape(peers // 4, 8, size).astype(BF)
    copies[0].wait()
    first = dp_ref[0] == 0
    x0 = x3[:, :, pl.ds(0, width // 2)]
    x1 = x3[:, :, pl.ds(width // 2, width // 2)]
    xh_s[...] = jnp.where(first, x0, x1)
    xs_s[...] = jnp.where(first, x1, x0)
    outs = [pltpu.make_async_copy(xh_s, xh_o, osems.at[0]), pltpu.make_async_copy(xs_s, xs_o, osems.at[1])]
    outs[0].start()
    outs[1].start()
    for start, size in blocks(hidden, 512):
        pre = dot_nt(x3[...].reshape(rows, width), wu[pl.ds(start, size), :])
        s = jax.nn.sigmoid(pre)
        act_s[pl.ds(start, size), :] = (pre * s).T.astype(BF)
        slope_s[:, pl.ds(start, size)] = s * (1.0 + pre * (1.0 - s))
    copy = pltpu.make_async_copy(slope_s, slope_o, osems.at[3])
    copy.start()
    outs.append(copy)
    copy = pltpu.make_async_copy(act_s, act_o, osems.at[2])
    copy.start()
    outs.append(copy)
    for copy in outs:
        copy.wait()


def expert_pre(dp, slab, wup):
    peers = slab.shape[0]
    hidden, width = wup.shape
    rows = peers * 10
    tiles = rows // 8
    sds = jax.ShapeDtypeStruct
    return pl.pallas_call(
        pre_body,
        in_specs=[SMEM, ANY, ANY],
        out_specs=[ANY] * 4,
        out_shape=[sds((hidden, rows), BF), sds((rows, hidden), F32)] + [sds((tiles, 8, width // 2), BF)] * 2,
        scratch_shapes=[
            pltpu.VMEM((tiles, 8, width), BF),
            pltpu.VMEM((peers, 8, QW), BF),
            pltpu.VMEM((peers, 8, QW), BF),
            pltpu.VMEM((hidden, width), BF),
            pltpu.VMEM((hidden, rows), BF),
            pltpu.VMEM((rows, hidden), F32),
            pltpu.VMEM((tiles, 8, width // 2), BF),
            pltpu.VMEM((tiles, 8, width // 2), BF),
            pltpu.SemaphoreType.DMA((6,)),
            pltpu.SemaphoreType.DMA((4,)),
        ],
        compiler_params=pltpu.CompilerParams(vmem_limit_bytes=VLIMIT),
        cost_estimate=pl.CostEstimate(flops=2 * rows * hidden * width, transcendentals=rows * hidden, bytes_accessed=20_000_000),
        name="expert_pre",
    )(dp, slab, wup)


def grad_body(zl_ref, slab, slope, wup, wdn, ret_o, gp_o, dy_o, dy3, dyr, rem, wu, wd, slope_s, gp_s, gpt_s, ret, rest, sems, osems):
    plane = slab.shape[0]
    peers = plane * 2
    main = peers * 8
    rows = main + peers * 2
    hidden, width = wu.shape
    right = width - LW
    zl = zl_ref[0]
    copies = load_plane(zl, slab, 0, dy3, dyr, sems)
    more = [
        pltpu.make_async_copy(src, dst, sems.at[4 + i])
        for i, (src, dst) in enumerate(((slab.at[:, 4], rem), (wdn, wd), (slope, slope_s), (wup, wu)))
    ]
    for copy in more:
        copy.start()
    for copy in copies + more[:1]:
        copy.wait()
    dy3[pl.ds(0, peers), :, pl.ds(LW, right)] = dyr[:, :, pl.ds(0, right)]
    for c, (start, size) in enumerate(((0, LW), (LW, right))):
        dy3[pl.ds(peers, peers // 4), :, pl.ds(start, size)] = rem_rows(zl, rem, c, size)
    outs = [pltpu.make_async_copy(dy3, dy_o, osems.at[0])]
    outs[0].start()
    for copy in more[1:3]:
        copy.wait()
    for start, size in blocks(hidden, 512):
        grad = dot_nt(dy3[...].reshape(rows, width), wd[pl.ds(start, size), :])
        value = (grad * slope_s[:, pl.ds(start, size)]).astype(BF)
        gp_s[:, pl.ds(start, size)] = value
        gpt_s[pl.ds(start, size), :] = value.T
    copy = pltpu.make_async_copy(gpt_s, gp_o, osems.at[1])
    copy.start()
    outs.append(copy)
    more[3].wait()
    rest[...] = jnp.zeros(rest.shape, F32)
    r_j = iota((main, peers * 2), 0)
    c_j = iota((main, peers * 2), 1)

    def columns(q, start, size):
        value = dot_nn(gp_s[...], wu[:, pl.ds(start, size)]).astype(BF)
        ret[:, q, :, pl.ds(0, size)] = value[:main].reshape(peers, 8, size)
        place = onehot(((r_j % 8) // 2 == q) & (c_j == (r_j // 8) * 2 + r_j % 2))
        rest[:, pl.ds(0, size)] = rest[:, pl.ds(0, size)] + dot_nn(place, value[main:])
        pltpu.make_async_copy(ret.at[:, q], ret_o.at[:, q], osems.at[2 + q]).start()

    full = width // QW
    ret[:, full] = jnp.zeros((peers, 8, QW), BF)
    lax.fori_loop(0, full, lambda q, c: (columns(q, pl.multiple_of(q * QW, QW), QW), c)[1], 0)
    columns(full, full * QW, width - full * QW)
    outs += [pltpu.make_async_copy(ret.at[:, q], ret_o.at[:, q], osems.at[2 + q]) for q in range(full + 1)]
    ret[:, 4] = rest[...].reshape(peers, 8, QW).astype(BF)
    copy = pltpu.make_async_copy(ret.at[:, 4], ret_o.at[:, 4], osems.at[6])
    copy.start()
    outs.append(copy)
    for copy in outs:
        copy.wait()


def expert_grad(zl, slab, slope, wup, wdn):
    plane = slab.shape[0]
    peers = plane * 2
    hidden, width = wup.shape
    rows = peers * 10
    tiles = rows // 8
    sds = jax.ShapeDtypeStruct
    return pl.pallas_call(
        grad_body,
        in_specs=[SMEM, ANY, ANY, ANY, ANY],
        out_specs=[ANY] * 3,
        out_shape=[sds((peers, 5, 8, QW), BF), sds((hidden, rows), BF), sds((tiles, 8, width), BF)],
        scratch_shapes=[
            pltpu.VMEM((tiles, 8, width), BF),
            pltpu.VMEM((peers, 8, LW), BF),
            pltpu.VMEM((plane, 8, LW), BF),
            pltpu.VMEM((hidden, width), BF),
            pltpu.VMEM((hidden, width), BF),
            pltpu.VMEM(slope.shape, F32),
            pltpu.VMEM((rows, hidden), BF),
            pltpu.VMEM((hidden, rows), BF),
            pltpu.VMEM((peers, 5, 8, QW), BF),
            pltpu.VMEM((peers * 8, QW), F32),
            pltpu.SemaphoreType.DMA((8,)),
            pltpu.SemaphoreType.DMA((7,)),
        ],
        compiler_params=pltpu.CompilerParams(vmem_limit_bytes=VLIMIT),
        cost_estimate=pl.CostEstimate(flops=4 * rows * hidden * width, transcendentals=0, bytes_accessed=40_000_000),
        name="expert_grad",
    )(zl, slab, slope, wup, wdn)


def unpack_body(zl_ref, slab, dy_o, dy3, dyr, rem, sems):
    plane = slab.shape[0]
    peers = plane * 2
    width = dy3.shape[2]
    right = width - LW
    zl = zl_ref[0]
    copies = load_plane(zl, slab, 0, dy3, dyr, sems)
    copies.append(pltpu.make_async_copy(slab.at[:, 4], rem, sems.at[4]))
    copies[-1].start()
    for copy in copies:
        copy.wait()
    dy3[pl.ds(0, peers), :, pl.ds(LW, right)] = dyr[:, :, pl.ds(0, right)]
    for c, (start, size) in enumerate(((0, LW), (LW, right))):
        dy3[pl.ds(peers, peers // 4), :, pl.ds(start, size)] = rem_rows(zl, rem, c, size)
    copy = pltpu.make_async_copy(dy3, dy_o, sems.at[5])
    copy.start()
    copy.wait()


def unpack_other(zl, slab, width):
    plane = slab.shape[0]
    peers = plane * 2
    tiles = peers * 10 // 8
    return pl.pallas_call(
        unpack_body,
        in_specs=[SMEM, ANY],
        out_specs=ANY,
        out_shape=jax.ShapeDtypeStruct((tiles, 8, width), BF),
        scratch_shapes=[
            pltpu.VMEM((tiles, 8, width), BF),
            pltpu.VMEM((peers, 8, LW), BF),
            pltpu.VMEM((plane, 8, LW), BF),
            pltpu.SemaphoreType.DMA((6,)),
        ],
        compiler_params=pltpu.CompilerParams(vmem_limit_bytes=VLIMIT),
        name="unpack_other",
    )(zl, slab)


def combine_body(rank_ref, ret_ref, last_ref, out_ref, rem_s):
    step = pl.program_id(0)
    rows, tokens = rank_ref.shape
    slot = iota((rows, tokens), 0) % 8
    rank = rank_ref[...]

    @pl.when(step == 0)
    def _():
        last = rank == (slot % 2 + 9).astype(F32)
        picks = jnp.concatenate([onehot(last & (slot // 2 == q)) for q in range(4)], axis=1)
        rem_s[...] = dot_tn(picks, last_ref[...].reshape(rows, QW)).reshape(4, tokens, QW)

    value = dot_tn(onehot(rank == (slot + 1).astype(F32)), ret_ref[...].reshape(rows, QW)) + rem_s[step]
    out_ref[...] = value.T.astype(BF)


def combine(rank, ret, width):
    peers = ret.shape[0]
    return pl.pallas_call(
        combine_body,
        grid=(4,),
        in_specs=[
            pl.BlockSpec(rank.shape, lambda q: (0, 0)),
            pl.BlockSpec((peers, 1, 8, QW), lambda q: (0, q, 0, 0)),
            pl.BlockSpec((peers, 1, 8, QW), lambda q: (0, 4, 0, 0)),
        ],
        out_specs=pl.BlockSpec((QW, rank.shape[1]), lambda q: (q, 0)),
        out_shape=jax.ShapeDtypeStruct((width, rank.shape[1]), BF),
        scratch_shapes=[pltpu.VMEM((4, rank.shape[1], QW), F32)],
        compiler_params=pltpu.CompilerParams(vmem_limit_bytes=VLIMIT),
        name="combine",
    )(rank, ret, ret)


def local(sizes, tokens_in, grad_out, expert_ids, combine_weights, up_weight, down_weight):
    n_dp, n_zl, n_plane = sizes
    peers = n_zl * n_plane
    width = tokens_in.shape[1]
    x = tokens_in.T
    dy = grad_out.T
    ids = expert_ids.T
    weights = combine_weights.T
    wup = up_weight[0].T
    wdn = down_weight[0]
    dp = lax.axis_index("dp").astype(jnp.int32)
    zl = lax.axis_index("zl").astype(jnp.int32)

    def move(value, cross, flip):
        pairs = []
        for i in range(n_dp * peers):
            d, z, p = i // peers, (i // n_plane) % n_zl, i % n_plane
            pairs.append((i, ((d ^ cross) * n_zl + (z ^ flip)) * n_plane + p))
        return lax.ppermute(value, ALL, pairs)

    slab, rank, meta = pack_x(ids, weights, x, peers)
    dy_near = move(dy, 0, 1)
    meta_near = move(meta, 0, 1)
    dy_a, meta_a = move(dy, 1, 0), move(meta, 1, 0)
    dy_b, meta_b = move(dy, 1, 1), move(meta, 1, 1)

    got_x = lax.all_to_all(slab, GROUP, 0, 0, tiled=True)
    slab_dy = pack_dy(zl[None], dy, dy_near, meta, meta_near, n_plane)
    got_dy = lax.all_to_all(slab_dy, PLANE, 0, 0, tiled=True)
    slab_other = pack_dy(zl[None], dy_a, dy_b, meta_a, meta_b, n_plane)
    got_other = lax.all_to_all(slab_other, PLANE, 0, 0, tiled=True)

    act, slope, xh, x_send = expert_pre(dp[None], got_x, wup)
    xh_other = move(x_send, 1, 0)
    act_keep = lax.dynamic_slice_in_dim(act, dp * (act.shape[0] // 2), act.shape[0] // 2, 0)
    act_send = lax.dynamic_slice_in_dim(act, (1 - dp) * (act.shape[0] // 2), act.shape[0] // 2, 0)
    act_other = move(act_send, 1, 0)
    ret, gp, dyr = expert_grad(zl[None], got_dy, slope, wup, wdn)
    gp_other = move(gp, 1, 0)
    back = lax.all_to_all(ret, GROUP, 0, 0, tiled=True)
    dy_other = unpack_other(zl[None], got_other, width)

    flat = lambda a: a.reshape(-1, a.shape[-1])
    up = lambda a, b: lax.dot_general(a, b, (((0,), (1,)), ((), ())), preferred_element_type=F32)
    grad_down = (dot_nn(act_keep, flat(dyr)) + dot_nn(act_other, flat(dy_other))).astype(BF)[None]
    grad_up = (up(flat(xh_other), gp_other) + up(flat(xh), gp)).astype(BF)[None]
    grad_input = combine(rank, back, width).T
    return grad_input, grad_up, grad_down


def build(devices, shape):
    n_dp, n_zl, n_y, n_x, n_core = shape
    fine = Mesh(devices.reshape(shape), ALL)
    token = P(ALL, None)
    weight = P(GROUP, None, None)
    inner = functools.partial(local, (n_dp, n_zl, n_y * n_x * n_core))

    return jax.shard_map(
        inner,
        mesh=fine,
        in_specs=(token, token, token, token, weight, weight),
        out_specs=(token, P(GROUP, "dp", None), P(GROUP, "dp", None)),
        check_vma=False,
    )


def solution(mesh):
    return build(mesh.devices, (2, 2, 4, 4, 2))
```

time: 352 us -> 374 us (1.062)
  starting transfers between devices: 37.6 us -> 49.3 us
  matrix products: 20.9 us -> 28.9 us
  waiting for transfers between devices: 212 us -> 218 us
    ppermute x6 -> x9, waiting for transfers between devices: 179 us -> 205 us  [move(): return lax.ppermute(value, ALL, pairs)]
    all_to_all x1, waiting for transfers between devices: 32.2 us -> 9.42 us  [local(): got_other = lax.all_to_all(slab_other, PLANE, 0, 0, tiled=True)]
    dot_general x4, matrix products: 20.9 us -> 28.9 us  [the longest x2 14.7 us: dot_nn(): lax.dot_general(left, right, (((1,), (0,)), ((), ())), preferred_element_...]
    all_to_all x1 -> x2, starting transfers between devices: 10.6 us -> 18.3 us  [the longest x1 10.6 us: local(): got_x = lax.all_to_all(slab, GROUP, 0, 0, tiled=True)]
    ppermute x6 -> x9, starting transfers between devices: 9.73 us -> 14.1 us  [move(): return lax.ppermute(value, ALL, pairs)]
    pallas_call x2 -> x0, local copies, waits for them, and re-layouts: 4.17 us -> none  [expert(): pl.pallas_call(expert_body, in_specs=[SMEM, ANY, ANY, ANY], out_specs=[AN...]
    pallas_call x5 -> x7, Pallas kernels: 67.5 us -> 65.7 us  [the longest x1 23.5 us: expert_grad(): pl.pallas_call(grad_body, in_specs=[SMEM, ANY, ANY, ANY, ANY], out_specs=...]
  transfers between devices with their start and end apart: 9 -> 13, of which waited for: 5 -> 7; matrix products, arithmetic and copies ran while one was open for 8% -> 8% of each run, Pallas kernels for 16% -> 15%
where the time goes in v2:
time: 374 us; the launch traced here: 367 us
  waiting for transfers between devices  218 us (58%)
  Pallas kernels  65.7 us (18%)
  starting transfers between devices  49.3 us (13%)
  matrix products  28.9 us (8%)
  local copies, waits for them, and re-layouts  3.86 us (1%)
    ppermute x9, waiting for transfers between devices, move(): return lax.ppermute(value, ALL, pairs)  205 us
    pallas_call x1, Pallas kernels, expert_grad(): pl.pallas_call(grad_body, in_specs=[SMEM, ANY, ANY, ANY, ANY], out_specs=...  23.5 us
    dot_general x2, matrix products, dot_nn(): lax.dot_general(left, right, (((1,), (0,)), ((), ())), preferred_element_...  14.7 us
    pallas_call x1, Pallas kernels, expert_pre(): pl.pallas_call(pre_body, in_specs=[SMEM, ANY, ANY], out_specs=[ANY] * 4,...  14.7 us
    dot_general x2, matrix products, local(): lax.dot_general(a, b, (((0,), (1,)), ((), ())), preferred_element_type=F32)  14.2 us
    ppermute x9, starting transfers between devices, move(): return lax.ppermute(value, ALL, pairs)  14.1 us
    pallas_call x2, Pallas kernels, pack_dy(): pl.pallas_call(functools.partial(pack_dy_body, spans), grid=(5,), in_spec...  11.8 us
    all_to_all x1, starting transfers between devices, local(): got_x = lax.all_to_all(slab, GROUP, 0, 0, tiled=True)  10.6 us
  transfers between devices with their start and end apart: 13, of which 7 were waited for; matrix products, arithmetic and copies ran while one was open for 8% of the time, Pallas kernels for 15%

profile of v2, /device:TPU:1, one launch (start us, length us, event | category | flops | bytes accessed | tf_op | source)
XLA Modules:
  0.0 366.6 jit_solution(9807322969871253375)
XLA Ops:
  0.6 5.7 %pack_x.1 = (bf16[64,5,8,768]{3,2,1,0:T(8,128)(2,1)}, f32[512,128]{1,0:T(8,128)}, f32[8,128]{1,0:T(8,128)}) custom-call(s32[4,128]{1,0:T(4,128)} %bitcast.36, f32[4,128]{1,0:T(4,128)} %bitcast.37, bf16[2880,128]{1,0:T(8,128)(2,1)} %bitcast.30), custom_call_target="tpu_custom_call" | custom-call | tf_op jit(solution)/shard_map/pack_x/pallas_call | solution.py:107
  6.3 10.6 %all-to-all-start.1 = ((bf16[64,5,8,768]{3,2,1,0:T(8,128)(2,1)}), bf16[64,5,8,768]{3,2,1,0:T(8,128)(2,1)}, u32[]{:S(2)}, u32[]{:S(2)}) async-start(bf16[64,5,8,768]{3,2,1,0:T(8,128)(2,1)} %get-tuple-element.15), calls=%async_computation.1 | async-start | bytes 7864320 | tf_op jit(solution)/shard_map/all_to_all | solution.py:475
  17.0 0.0 copy-done.1
  17.0 1.5 collective-permute-start
  18.5 0.0 copy-done.6
  18.5 0.1 collective-permute-start.1
  18.6 59.1 %collective-permute-done.1.mb_ref = f32[8,128]{1,0:T(8,128)S(1)} collective-permute-done((f32[8,128]{1,0:T(8,128)S(1)}, f32[8,128]{1,0:T(8,128)S(1)}, u32[]{:S(2)}, u32[]{:S(2)}) %collective-permute-start.1) | collective-permute-done | bytes 4128 | tf_op jit(solution)/shard_map/ppermute | solution.py:467
  77.7 0.0 collective-permute-done.pb_ref
  77.7 0.6 copy-done.10
  78.3 0.3 copy-done.5
  78.6 5.8 %shard_map.85 = bf16[32,5,8,1536]{3,2,1,0:T(8,128)(2,1)} custom-call(s32[1]{0:T(128)} %bitcast.3.zl_ref, bf16[2880,128]{1,0:T(8,128)(2,1)} %bitcast.31, bf16[2880,128]{1,0:T(8,128)(2,1)} %copy-done.5, f32[8,128]{1,0:T(8,128)} %get-tuple-element.14.ma_ref, f32[8,128]{1,0:T(8,128)} %copy-done.10), custom_call_target="tpu_custom_call" | custom-call | tf_op jit(solution)/shard_map/pallas_call | solution.py:175
  84.5 0.0 all-to-all-done.1.slab
  84.5 7.6 %all-to-all-start = ((bf16[32,5,8,1536]{3,2,1,0:T(8,128)(2,1)}), bf16[32,5,8,1536]{3,2,1,0:T(8,128)(2,1)}, u32[]{:S(2)}, u32[]{:S(2)}) async-start(bf16[32,5,8,1536]{3,2,1,0:T(8,128)(2,1)} %shard_map.85), calls=%async_computation | async-start | bytes 7864320 | tf_op jit(solution)/shard_map/all_to_all | solution.py:477
  92.1 0.0 copy-done.2
  92.1 3.4 collective-permute-start.5
  95.5 0.0 collective-permute-start.6
  95.5 0.0 copy-done.7
  95.5 1.2 collective-permute-start.7
  96.7 1.4 collective-permute-start.8
  98.2 14.1 %collective-permute-done.7.ma_ref = f32[8,128]{1,0:T(8,128)S(1)} collective-permute-done((f32[8,128]{1,0:T(8,128)S(1)}, f32[8,128]{1,0:T(8,128)S(1)}, u32[]{:S(2)}, u32[]{:S(2)}) %collective-permute-start.7) | collective-permute-done | bytes 4128 | tf_op jit(solution)/shard_map/ppermute | solution.py:467
  112.3 16.2 %collective-permute-done.8.mb_ref = f32[8,128]{1,0:T(8,128)S(1)} collective-permute-done((f32[8,128]{1,0:T(8,128)S(1)}, f32[8,128]{1,0:T(8,128)S(1)}, u32[]{:S(2)}, u32[]{:S(2)}) %collective-permute-start.8) | collective-permute-done | bytes 4128 | tf_op jit(solution)/shard_map/ppermute | solution.py:467
  128.5 0.0 collective-permute-done.5.pa_ref
  128.5 0.0 collective-permute-done.6.pb_ref
  128.5 0.6 copy-done.9
  129.1 0.3 copy-done.3
  129.4 0.9 copy-done.4
  130.3 6.0 %shard_map.86 = bf16[32,5,8,1536]{3,2,1,0:T(8,128)(2,1)} custom-call(s32[1]{0:T(128)} %bitcast.3.zl_ref, bf16[2880,128]{1,0:T(8,128)(2,1)} %copy-done.3, bf16[2880,128]{1,0:T(8,128)(2,1)} %copy-done.4, f32[8,128]{1,0:T(8,128)} %copy-done.8, f32[8,128]{1,0:T(8,128)} %copy-done.9), custom_call_target="tpu_custom_call" | custom-call | tf_op jit(solution)/shard_map/pallas_call | solution.py:175
  136.3 3.7 %all-to-all-done.slab = bf16[32,5,8,1536]{3,2,1,0:T(8,128)(2,1)} async-done(((bf16[32,5,8,1536]{3,2,1,0:T(8,128)(2,1)}), bf16[32,5,8,1536]{3,2,1,0:T(8,128)(2,1)}, u32[]{:S(2)}, u32[]{:S(2)}) %all-to-all-start) | async-done | bytes 3932192 | tf_op jit(solution)/shard_map/all_to_all | solution.py:477
  139.9 8.5 %all-to-all-start.3 = ((bf16[32,5,8,1536]{3,2,1,0:T(8,128)(2,1)}), bf16[32,5,8,1536]{3,2,1,0:T(8,128)(2,1)}, u32[]{:S(2)}, u32[]{:S(2)}) async-start(bf16[32,5,8,1536]{3,2,1,0:T(8,128)(2,1)} %shard_map.86), calls=%async_computation.3 | async-start | bytes 7864320 | tf_op jit(solution)/shard_map/all_to_all | solution.py:479
  148.4 14.7 %expert_pre.1 = (bf16[1440,640]{1,0:T(8,128)(2,1)}, f32[640,1440]{1,0:T(8,128)}, bf16[80,8,1440]{2,1,0:T(8,128)(2,1)}, bf16[80,8,1440]{2,1,0:T(8,128)(2,1)}) custom-call(s32[1]{0:T(128)} %bitcast.5.dp_ref, bf16[64,5,8,768]{3,2,1,0:T(8,128)(2,1)} %all-to-all-done.1.slab, bf16[1440,2880]{1,0:T(8,128)(2,1)} %bitcast.38), custom_call_target="tpu_custom_call" | custom-call | flops 5308416000 | bytes 20000000 | tf_op jit(solution)/shard_map/expert_pre/pallas_call | solution.py:264
  163.1 23.5 %expert_grad.1 = (bf16[64,5,8,768]{3,2,1,0:T(8,128)(2,1)}, bf16[1440,640]{1,0:T(8,128)(2,1)}, bf16[80,8,2880]{2,1,0:T(8,128)(2,1)}) custom-call(s32[1]{0:T(128)} %bitcast.3.zl_ref, bf16[32,5,8,1536]{3,2,1,0:T(8,128)(2,1)} %all-to-all-done.slab, f32[640,1440]{1,0:T(8,128)} %get-tuple-element.16.slope, bf16[1440,2880]{1,0:T(8,128)(2,1)} %bitcast.39, ...), custom_call_target="tpu_custom_call" | custom-call | flops 10616832000 | bytes 40000000 | tf_op jit(solution)/shard_map/expert_grad/pallas_call | solution.py:351
  186.6 9.4 %all-to-all-done.3.slab = bf16[32,5,8,1536]{3,2,1,0:T(8,128)(2,1)} async-done(((bf16[32,5,8,1536]{3,2,1,0:T(8,128)(2,1)}), bf16[32,5,8,1536]{3,2,1,0:T(8,128)(2,1)}, u32[]{:S(2)}, u32[]{:S(2)}) %all-to-all-start.3) | async-done | bytes 3932192 | tf_op jit(solution)/shard_map/all_to_all | solution.py:479
  196.0 8.5 %all-to-all-start.2 = ((bf16[64,5,8,768]{3,2,1,0:T(8,128)(2,1)}), bf16[64,5,8,768]{3,2,1,0:T(8,128)(2,1)}, u32[]{:S(2)}, u32[]{:S(2)}) async-start(bf16[64,5,8,768]{3,2,1,0:T(8,128)(2,1)} %get-tuple-element.17), calls=%async_computation.2 | async-start | bytes 7864320 | tf_op jit(solution)/shard_map/all_to_all | solution.py:488
  204.5 3.4 collective-permute-start.2
  207.9 1.3 constant_dynamic-slice_fusion
  209.1 0.1 collective-permute-start.4
  209.2 3.0 collective-permute-start.3
  212.2 9.2 %fusion.4 = f32[720,2880]{1,0:T(8,128)} fusion(bf16[80,8,2880]{2,1,0:T(8,128)(2,1)} %get-tuple-element.22, bf16[1440,640]{1,0:T(8,128)(2,1)} %get-tuple-element.21, s32[]{:T(128)S(6)} %select_n.6), kind=kOutput, calls=%fused_computation.6 | convolution fusion | flops 2654208000 | bytes 12984324 | tf_op jit(solution)/shard_map/dot_general | solution.py:32
  221.4 4.4 %unpack_other.1 = bf16[80,8,2880]{2,1,0:T(8,128)(2,1)} custom-call(s32[1]{0:T(128)} %bitcast.3.zl_ref, bf16[32,5,8,1536]{3,2,1,0:T(8,128)(2,1)} %all-to-all-done.3.slab), custom_call_target="tpu_custom_call" | custom-call | tf_op jit(solution)/shard_map/unpack_other/pallas_call | solution.py:399
  225.9 0.0 copy-start
  225.9 6.0 %fusion.6 = f32[1440,1440]{1,0:T(8,128)S(1)} fusion(bf16[1440,640]{1,0:T(8,128)(2,1)} %get-tuple-element.19, bf16[80,8,1440]{2,1,0:T(8,128)(2,1)} %get-tuple-element.20), kind=kOutput, calls=%fused_computation.8 | convolution fusion | flops 2654208000 | bytes 11980800 | tf_op jit(solution)/shard_map/dot_general | solution.py:492
  231.9 81.1 %collective-permute-done.4 = bf16[720,640]{1,0:T(8,128)(2,1)S(1)} collective-permute-done((bf16[720,640]{1,0:T(8,128)(2,1)S(1)}, bf16[720,640]{1,0:T(8,128)(2,1)S(1)}, u32[]{:S(2)}, u32[]{:S(2)}) %collective-permute-start.4) | collective-permute-done | bytes 921632 | tf_op jit(solution)/shard_map/ppermute | solution.py:467
  313.0 5.4 %fusion.2 = bf16[1,720,2880]{2,1,0:T(8,128)(2,1)} fusion(f32[720,2880]{1,0:T(8,128)S(1)} %copy-done.11, bf16[720,640]{1,0:T(8,128)(2,1)S(1)} %collective-permute-done.4, bf16[80,8,2880]{2,1,0:T(8,128)(2,1)S(1)} %copy-done), kind=kOutput, calls=%fused_computation.4 | convolution fusion | flops 2658355200 | bytes 17049600 | tf_op jit(solution)/shard_map/dot_general | solution.py:32
  318.4 0.0 collective-permute-done.2
  318.4 34.2 %collective-permute-done.3 = bf16[1440,640]{1,0:T(8,128)(2,1)} collective-permute-done((bf16[1440,640]{1,0:T(8,128)(2,1)}, bf16[1440,640]{1,0:T(8,128)(2,1)}, u32[]{:S(2)}, u32[]{:S(2)}) %collective-permute-start.3) | collective-permute-done | bytes 1843232 | tf_op jit(solution)/shard_map/ppermute | solution.py:467
  352.6 8.2 %fusion.1 = bf16[1,1440,1440]{2,1,0:T(8,128)(2,1)} fusion(f32[1440,1440]{1,0:T(8,128)S(1)} %fusion.6, bf16[1440,640]{1,0:T(8,128)(2,1)} %collective-permute-done.3, bf16[80,8,1440]{2,1,0:T(8,128)(2,1)} %collective-permute-done.2), kind=kOutput, calls=%fused_computation.3 | convolution fusion | flops 2658355200 | bytes 16128000 | tf_op jit(solution)/shard_map/dot_general | solution.py:492
  360.8 0.0 all-to-all-done.2.ret_ref.last_ref
  360.8 5.6 %combine.1 = bf16[2880,128]{1,0:T(8,128)(2,1)} custom-call(f32[512,128]{1,0:T(8,128)} %get-tuple-element.13.rank_ref, bf16[64,5,8,768]{3,2,1,0:T(8,128)(2,1)} %all-to-all-done.2.ret_ref.last_ref, bf16[64,5,8,768]{3,2,1,0:T(8,128)(2,1)} %all-to-all-done.2.ret_ref.last_ref), custom_call_target="tpu_custom_call" | custom-call | tf_op jit(solution)/shard_map/combine/pallas_call | solution.py:433
  (14 shorter events, 0.0 us)
Async XLA Ops:
  6.3 10.7 %copy-start.1 = (bf16[128,2880]{0,1:T(8,128)(2,1)S(1)}, bf16[128,2880]{0,1:T(8,128)(2,1)}, u32[]{:S(2)}) copy-start(bf16[128,2880]{0,1:T(8,128)(2,1)} %param.7) | copy-start | bytes 2211844
  6.3 12.2 %copy-start.6 = (f32[8,128]{1,0:T(8,128)S(1)}, f32[8,128]{1,0:T(8,128)}, u32[]{:S(2)}) copy-start(f32[8,128]{1,0:T(8,128)} %get-tuple-element.14.ma_ref) | copy-start | bytes 12292
  6.3 78.1 %all-to-all-start.1 = ((bf16[64,5,8,768]{3,2,1,0:T(8,128)(2,1)}), bf16[64,5,8,768]{3,2,1,0:T(8,128)(2,1)}, u32[]{:S(2)}, u32[]{:S(2)}) async-start(bf16[64,5,8,768]{3,2,1,0:T(8,128)(2,1)} %get-tuple-element.15), calls=%async_computation.1 | async-start | bytes 7864320 | tf_op jit(solution)/shard_map/all_to_all | solution.py:475
  17.0 60.8 %collective-permute-start = (bf16[2880,128]{1,0:T(8,128)(2,1)S(1)}, bf16[2880,128]{1,0:T(8,128)(2,1)S(1)}, u32[]{:S(2)}, u32[]{:S(2)}) collective-permute-start(bf16[2880,128]{1,0:T(8,128)(2,1)S(1)} %bitcast.32), channel_id=1, source_target_pairs={{0,32},{1,33},{2,34},{3,35},{4,36},{5,37},{6,38},{7,39},{8,40},{9,... | collective-permute-start | bytes 2211848 | tf_op jit(solution)/shard_map/ppermute | solution.py:467
  18.5 59.2 %collective-permute-start.1 = (f32[8,128]{1,0:T(8,128)S(1)}, f32[8,128]{1,0:T(8,128)S(1)}, u32[]{:S(2)}, u32[]{:S(2)}) collective-permute-start(f32[8,128]{1,0:T(8,128)S(1)} %copy-done.6), channel_id=1, source_target_pairs={{0,32},{1,33},{2,34},{3,35},{4,36},{5,37},{6,38},{7,39},{8,40},{9,... | collective-permute-start | bytes 12296 | tf_op jit(solution)/shard_map/ppermute | solution.py:467
  77.7 0.6 copy-start.10
  77.7 0.9 copy-start.5
  84.5 7.6 %copy-start.2 = (bf16[128,2880]{0,1:T(8,128)(2,1)S(1)}, bf16[128,2880]{0,1:T(8,128)(2,1)}, u32[]{:S(2)}) copy-start(bf16[128,2880]{0,1:T(8,128)(2,1)} %param.7) | copy-start | bytes 2211844
  84.5 11.0 %copy-start.7 = (f32[8,128]{1,0:T(8,128)S(1)}, f32[8,128]{1,0:T(8,128)}, u32[]{:S(2)}) copy-start(f32[8,128]{1,0:T(8,128)} %get-tuple-element.14.ma_ref) | copy-start | bytes 12292
  84.5 55.5 %all-to-all-start = ((bf16[32,5,8,1536]{3,2,1,0:T(8,128)(2,1)}), bf16[32,5,8,1536]{3,2,1,0:T(8,128)(2,1)}, u32[]{:S(2)}, u32[]{:S(2)}) async-start(bf16[32,5,8,1536]{3,2,1,0:T(8,128)(2,1)} %shard_map.85), calls=%async_computation | async-start | bytes 7864320 | tf_op jit(solution)/shard_map/all_to_all | solution.py:477
  92.1 36.4 %collective-permute-start.5 = (bf16[2880,128]{1,0:T(8,128)(2,1)S(1)}, bf16[2880,128]{1,0:T(8,128)(2,1)S(1)}, u32[]{:S(2)}, u32[]{:S(2)}) collective-permute-start(bf16[2880,128]{1,0:T(8,128)(2,1)S(1)} %bitcast.33), channel_id=1, source_target_pairs={{0,64},{1,65},{2,66},{3,67},{4,68},{5,69},{6,70},{7,71},{8,72},{9,... | collective-permute-start | bytes 2211848 | tf_op jit(solution)/shard_map/ppermute | solution.py:467
  95.5 33.0 %collective-permute-start.6 = (bf16[2880,128]{1,0:T(8,128)(2,1)S(1)}, bf16[2880,128]{1,0:T(8,128)(2,1)S(1)}, u32[]{:S(2)}, u32[]{:S(2)}) collective-permute-start(bf16[2880,128]{1,0:T(8,128)(2,1)S(1)} %bitcast.34), channel_id=1, source_target_pairs={{0,96},{1,97},{2,98},{3,99},{4,100},{5,101},{6,102},{7,103},{8,104... | collective-permute-start | bytes 2211848 | tf_op jit(solution)/shard_map/ppermute | solution.py:467
  95.5 16.8 %collective-permute-start.7 = (f32[8,128]{1,0:T(8,128)S(1)}, f32[8,128]{1,0:T(8,128)S(1)}, u32[]{:S(2)}, u32[]{:S(2)}) collective-permute-start(f32[8,128]{1,0:T(8,128)S(1)} %copy-done.7), channel_id=1, source_target_pairs={{0,64},{1,65},{2,66},{3,67},{4,68},{5,69},{6,70},{7,71},{8,72},{9,... | collective-permute-start | bytes 12296 | tf_op jit(solution)/shard_map/ppermute | solution.py:467
  96.7 31.8 %collective-permute-start.8 = (f32[8,128]{1,0:T(8,128)S(1)}, f32[8,128]{1,0:T(8,128)S(1)}, u32[]{:S(2)}, u32[]{:S(2)}) collective-permute-start(f32[8,128]{1,0:T(8,128)S(1)} %copy-done.7), channel_id=1, source_target_pairs={{0,96},{1,97},{2,98},{3,99},{4,100},{5,101},{6,102},{7,103},{8,104... | collective-permute-start | bytes 12296 | tf_op jit(solution)/shard_map/ppermute | solution.py:467
  112.3 16.2 %copy-start.8 = (f32[8,128]{1,0:T(8,128)}, f32[8,128]{1,0:T(8,128)S(1)}, u32[]{:S(2)}) copy-start(f32[8,128]{1,0:T(8,128)S(1)} %collective-permute-done.7.ma_ref) | copy-start | bytes 12292
  128.5 0.6 copy-start.9
  128.5 0.9 copy-start.3
  129.4 0.9 copy-start.4
  139.9 56.1 %all-to-all-start.3 = ((bf16[32,5,8,1536]{3,2,1,0:T(8,128)(2,1)}), bf16[32,5,8,1536]{3,2,1,0:T(8,128)(2,1)}, u32[]{:S(2)}, u32[]{:S(2)}) async-start(bf16[32,5,8,1536]{3,2,1,0:T(8,128)(2,1)} %shard_map.86), calls=%async_computation.3 | async-start | bytes 7864320 | tf_op jit(solution)/shard_map/all_to_all | solution.py:479
  196.0 164.8 %all-to-all-start.2 = ((bf16[64,5,8,768]{3,2,1,0:T(8,128)(2,1)}), bf16[64,5,8,768]{3,2,1,0:T(8,128)(2,1)}, u32[]{:S(2)}, u32[]{:S(2)}) async-start(bf16[64,5,8,768]{3,2,1,0:T(8,128)(2,1)} %get-tuple-element.17), calls=%async_computation.2 | async-start | bytes 7864320 | tf_op jit(solution)/shard_map/all_to_all | solution.py:488
  204.5 113.9 %collective-permute-start.2 = (bf16[80,8,1440]{2,1,0:T(8,128)(2,1)}, bf16[80,8,1440]{2,1,0:T(8,128)(2,1)}, u32[]{:S(2)}, u32[]{:S(2)}) collective-permute-start(bf16[80,8,1440]{2,1,0:T(8,128)(2,1)} %get-tuple-element.18), channel_id=1, source_target_pairs={{0,64},{1,65},{2,66},{3,67},{4,68},{5,69},{6,70},{7,71},{8,72},{9,... | collective-permute-start | bytes 5529608 | tf_op jit(solution)/shard_map/ppermute | solution.py:467
  209.1 103.9 %collective-permute-start.4 = (bf16[720,640]{1,0:T(8,128)(2,1)S(1)}, bf16[720,640]{1,0:T(8,128)(2,1)S(1)}, u32[]{:S(2)}, u32[]{:S(2)}) collective-permute-start(bf16[720,640]{1,0:T(8,128)(2,1)S(1)} %constant_dynamic-slice_fusion), channel_id=1, source_target_pairs={{0,64},{1,65},{2,66},{3,67},{4,68},{5,69},{6,70},{7,71},{8,72},{9,... | collective-permute-start | bytes 2764808 | tf_op jit(solution)/shard_map/ppermute | solution.py:467
  209.2 143.4 %collective-permute-start.3 = (bf16[1440,640]{1,0:T(8,128)(2,1)}, bf16[1440,640]{1,0:T(8,128)(2,1)}, u32[]{:S(2)}, u32[]{:S(2)}) collective-permute-start(bf16[1440,640]{1,0:T(8,128)(2,1)} %get-tuple-element.19), channel_id=1, source_target_pairs={{0,64},{1,65},{2,66},{3,67},{4,68},{5,69},{6,70},{7,71},{8,72},{9,... | collective-permute-start | bytes 5529608 | tf_op jit(solution)/shard_map/ppermute | solution.py:467
  225.9 87.1 %copy-start = (bf16[80,8,2880]{2,1,0:T(8,128)(2,1)S(1)}, bf16[80,8,2880]{2,1,0:T(8,128)(2,1)}, u32[]{:S(2)}) copy-start(bf16[80,8,2880]{2,1,0:T(8,128)(2,1)} %unpack_other.1) | copy-start | bytes 11059204
  225.9 87.1 %copy-start.11 = (f32[720,2880]{1,0:T(8,128)S(1)}, f32[720,2880]{1,0:T(8,128)}, u32[]{:S(2)}) copy-start(f32[720,2880]{1,0:T(8,128)} %fusion.4) | copy-start | bytes 24883204

commit v3 on v2

v3 whole, which is shorter than its diff:
```python
import functools

import jax
import jax.numpy as jnp
from jax import lax
from jax.experimental import pallas as pl
from jax.experimental.pallas import tpu as pltpu
from jax.sharding import Mesh, PartitionSpec as P


LW = 1536
QW = 768
LANES = 128
BF = jnp.bfloat16
F32 = jnp.float32
ALL = ("dp", "zl", "y", "x", "core")
GROUP = ("zl", "y", "x", "core")
PLANE = ("y", "x", "core")
ANY = pl.BlockSpec(memory_space=pl.ANY)
SMEM = pl.BlockSpec(memory_space=pltpu.SMEM)
VLIMIT = 62 * 1024 * 1024


def iota(shape, dim):
    return lax.broadcasted_iota(jnp.int32, shape, dim)


def onehot(cond):
    return jnp.where(cond, 1.0, 0.0).astype(BF)


def dot_nn(left, right):
    return lax.dot_general(left, right, (((1,), (0,)), ((), ())), preferred_element_type=F32)


def dot_nt(left, right):
    return lax.dot_general(left, right, (((1,), (1,)), ((), ())), preferred_element_type=F32)


def dot_tn(left, right):
    return lax.dot_general(left, right, (((0,), (0,)), ((), ())), preferred_element_type=F32)


def rank_rows(ids, parts, first, experts):
    top, tokens = ids.shape
    index = iota((experts, tokens), 0) + first
    member = jnp.zeros((experts, tokens), F32)
    weight = [jnp.zeros((experts, tokens), F32) for _ in parts]
    for k in range(top):
        hit = ids[k : k + 1, :] == index
        member = member + jnp.where(hit, 1.0, 0.0)
        weight = [w + jnp.where(hit, part[k : k + 1, :], 0.0) for w, part in zip(weight, parts)]
    before = onehot(iota((tokens, tokens), 0) < iota((tokens, tokens), 1))
    rank = member * (dot_nn(member.astype(BF), before) + 1.0)
    spread = onehot(iota((experts * 8, experts), 0) // 8 == iota((experts * 8, experts), 1))
    total = None
    for w in reversed(weight):
        piece = dot_nn(spread, w.astype(BF))
        total = piece if total is None else piece + total
    return dot_nn(spread, rank.astype(BF)), total


def padded(piece, width):
    if piece.shape[0] == width:
        return piece
    return jnp.concatenate([piece, jnp.zeros((width - piece.shape[0], piece.shape[1]), piece.dtype)], axis=0)


def row_weight(hit, weight):
    return jnp.sum(jnp.where(hit, weight, 0.0), axis=1, keepdims=True)


def blocks(total, size):
    return [(start, min(size, total - start)) for start in range(0, total, size)]


def tiles(width):
    return -(-width // LANES)


def from_tiles(ref, first, count):
    peers = ref.shape[0]
    return jnp.concatenate([ref[:, first + i].reshape(peers * 8, LANES) for i in range(count)], axis=1)


def to_tiles(ref, first, value):
    rows, width = value.shape
    for i in range(tiles(width)):
        part = value[:, i * LANES : min(width, (i + 1) * LANES)]
        ref[:, first + i, :, pl.ds(0, part.shape[1])] = part.reshape(rows // 8, 8, part.shape[1]).astype(BF)


def pack_x_body(ids_ref, w_ref, x_ref, out_o, rank_ref, meta_ref, out_s, sems):
    rows, tokens = rank_ref.shape
    rank, _ = rank_rows(ids_ref[...], [], 0, rows // 8)
    rank_ref[...] = rank
    meta_ref[...] = jnp.concatenate([ids_ref[...].astype(F32), w_ref[...]], axis=0)
    slot = iota((rows, tokens), 0) % 8
    width = x_ref.shape[0]
    pieces = blocks(width, QW)
    spans = [(start // LANES, tiles(size)) for start, size in pieces] + [(tiles(width), tiles(QW))]
    copies = [
        pltpu.make_async_copy(out_s.at[:, pl.ds(c, n)], out_o.at[:, pl.ds(c, n)], sems.at[g])
        for g, (c, n) in enumerate(spans)
    ]
    main = onehot(rank == (slot + 1).astype(F32))
    for q, (start, size) in enumerate(pieces):
        to_tiles(out_s, spans[q][0], dot_nt(main, padded(x_ref[pl.ds(start, size), :], spans[q][1] * LANES)))
        copies[q].start()
    hit = rank == (slot % 2 + 9).astype(F32)
    picks = jnp.concatenate([onehot(hit & (slot // 2 == q)) for q in range(4)], axis=1)
    source = jnp.concatenate([padded(x_ref[pl.ds(start, size), :], QW) for start, size in pieces], axis=1)
    to_tiles(out_s, spans[4][0], dot_nt(picks, source))
    copies[4].start()
    for copy in copies:
        copy.wait()


def pack_x(ids, weights, x, peers):
    tokens = ids.shape[1]
    count = tiles(x.shape[0]) + tiles(QW)
    vmem = pl.BlockSpec(memory_space=pltpu.VMEM)
    return pl.pallas_call(
        pack_x_body,
        in_specs=[vmem, vmem, vmem],
        out_specs=[ANY, vmem, vmem],
        out_shape=[
            jax.ShapeDtypeStruct((peers, count, 8, LANES), BF),
            jax.ShapeDtypeStruct((peers * 8, tokens), F32),
            jax.ShapeDtypeStruct((2 * ids.shape[0], tokens), F32),
        ],
        scratch_shapes=[pltpu.VMEM((peers, count, 8, LANES), BF), pltpu.SemaphoreType.DMA((5,))],
        compiler_params=pltpu.CompilerParams(vmem_limit_bytes=VLIMIT),
        name="pack_x",
    )(ids, weights, x)


def pack_dy_body(zl_ref, pa_ref, pb_ref, ma_ref, mb_ref, out_o, out_s, sems):
    width, tokens = pa_ref.shape
    peers = out_s.shape[0]
    rows = peers * 8
    top = ma_ref.shape[0] // 2
    pays = (pa_ref, pb_ref)
    slot = iota((rows, tokens), 0) % 8
    spans = blocks(width, LW)
    ranks, scales = [], []
    for meta in (ma_ref, mb_ref):
        ids = meta[pl.ds(0, top), :].astype(jnp.int32)
        weight = meta[pl.ds(top, top), :]
        w1 = weight.astype(BF)
        rest = weight - w1.astype(F32)
        w2 = rest.astype(BF)
        w3 = (rest - w2.astype(F32)).astype(BF)
        parts = [w.astype(F32) for w in (w1, w2, w3)]
        rank, weight = rank_rows(ids, parts, zl_ref[0] * peers, peers)
        ranks.append(rank)
        scales.append(weight)
    copies = []

    def send(first, value):
        to_tiles(out_s, first, value)
        part = pl.ds(first, tiles(value.shape[1]))
        copies.append(pltpu.make_async_copy(out_s.at[:, part], out_o.at[:, part], sems.at[len(copies)]))
        copies[-1].start()

    for s in range(2):
        hit = ranks[s] == (slot + 1).astype(F32)
        scale = row_weight(hit, scales[s])
        for start, size in spans:
            count = tiles(size)
            first = 2 * (start // LANES) + s * count
            send(first, dot_nt(onehot(hit), padded(pays[s][pl.ds(start, size), :], count * LANES)) * scale)
    picks, source = [], []
    scale = jnp.zeros((rows, 1), F32)
    for s in range(2):
        hit = ranks[s] == (slot % 2 + 9).astype(F32)
        scale = scale + jnp.where((slot[:, :1] // 2) % 2 == s, row_weight(hit, scales[s]), 0.0)
        for c, (start, size) in enumerate(spans):
            picks.append(onehot(hit & (slot // 2 == c * 2 + s)))
            source.append(padded(pays[s][pl.ds(start, size), :], LW))
    send(2 * tiles(width), dot_nt(jnp.concatenate(picks, axis=1), jnp.concatenate(source, axis=1)) * scale)
    for copy in copies:
        copy.wait()


def pack_dy(zl, dy_a, dy_b, meta_a, meta_b, peers):
    width = dy_a.shape[0]
    shape = (peers, 2 * tiles(width) + tiles(LW), 8, LANES)
    vmem = pl.BlockSpec(memory_space=pltpu.VMEM)
    return pl.pallas_call(
        pack_dy_body,
        in_specs=[SMEM, vmem, vmem, vmem, vmem],
        out_specs=ANY,
        out_shape=jax.ShapeDtypeStruct(shape, BF),
        scratch_shapes=[pltpu.VMEM(shape, BF), pltpu.SemaphoreType.DMA((5,))],
        compiler_params=pltpu.CompilerParams(vmem_limit_bytes=VLIMIT),
    )(zl, dy_a, dy_b, meta_a, meta_b)


def load_plane(zl, slab, main, rem, sems):
    plane = slab.shape[0]
    count = main.shape[1]
    left = tiles(LW)
    right = count - left
    copies = []
    for z in range(2):
        rel = lax.bitwise_xor(zl, z)
        span = pl.ds(z * plane, plane)
        for i, (first, n) in enumerate(((rel * left, left), (2 * left + rel * right, right))):
            copies.append(
                pltpu.make_async_copy(
                    slab.at[:, pl.ds(first, n)], main.at[span, pl.ds(i * left, n)], sems.at[2 * z + i]
                )
            )
    copies.append(pltpu.make_async_copy(slab.at[:, pl.ds(2 * count, left)], rem, sems.at[4]))
    for copy in copies:
        copy.start()
    return copies


def place_main(main, dst):
    peers = main.shape[0]
    width = dst.shape[2]
    for c, (start, size) in enumerate(blocks(width, LANES)):
        dst[pl.ds(0, peers), :, pl.ds(start, size)] = main[:, c, :, pl.ds(0, size)]


def place_rem(zl, rem, dst):
    plane = rem.shape[0]
    peers = plane * 2
    last = from_tiles(rem, 0, rem.shape[1])
    r_i = iota((peers * 2, plane * 8), 0)
    c_i = iota((peers * 2, plane * 8), 1)
    rel = lax.bitwise_xor(r_i // peers, zl)
    base = ((r_i // 2) % plane) * 8 + rel * 2 + r_i % 2
    for c, (start, size) in enumerate(blocks(dst.shape[2], LW)):
        value = dot_nn(onehot(c_i == base + 4 * c), last[:, :size])
        dst[pl.ds(peers, peers // 4), :, pl.ds(start, size)] = value.reshape(peers // 4, 8, size).astype(BF)


def split_body(dp_ref, slab, x_o, xh_o, xs_o, got, x3, xh_s, xs_s, sems, osems):
    peers = slab.shape[0]
    main = peers * 8
    width = x3.shape[2]
    copy = pltpu.make_async_copy(slab, got, sems.at[0])
    copy.start()
    copy.wait()
    place_main(got, x3)
    last = from_tiles(got, tiles(width), tiles(QW))
    r_i = iota((peers * 2, main), 0)
    c_i = iota((peers * 2, main), 1)
    for q, (start, size) in enumerate(blocks(width, QW)):
        pick = onehot(c_i == (r_i // 2) * 8 + 2 * q + r_i % 2)
        value = dot_nn(pick, last[:, :size])
        x3[pl.ds(peers, peers // 4), :, pl.ds(start, size)] = value.reshape(peers // 4, 8, size).astype(BF)
    first = dp_ref[0] == 0
    x0 = x3[:, :, pl.ds(0, width // 2)]
    x1 = x3[:, :, pl.ds(width // 2, width // 2)]
    xs_s[...] = jnp.where(first, x1, x0)
    outs = [pltpu.make_async_copy(xs_s, xs_o, osems.at[0])]
    outs[0].start()
    outs.append(pltpu.make_async_copy(x3, x_o, osems.at[1]))
    outs[1].start()
    xh_s[...] = jnp.where(first, x0, x1)
    outs.append(pltpu.make_async_copy(xh_s, xh_o, osems.at[2]))
    outs[2].start()
    for copy in outs:
        copy.wait()


def split_x(dp, slab, width):
    peers = slab.shape[0]
    groups = peers * 10 // 8
    sds = jax.ShapeDtypeStruct
    half = (groups, 8, width // 2)
    return pl.pallas_call(
        split_body,
        in_specs=[SMEM, ANY],
        out_specs=[ANY] * 3,
        out_shape=[sds((groups, 8, width), BF), sds(half, BF), sds(half, BF)],
        scratch_shapes=[
            pltpu.VMEM(slab.shape, BF),
            pltpu.VMEM((groups, 8, width), BF),
            pltpu.VMEM(half, BF),
            pltpu.VMEM(half, BF),
            pltpu.SemaphoreType.DMA((1,)),
            pltpu.SemaphoreType.DMA((3,)),
        ],
        compiler_params=pltpu.CompilerParams(vmem_limit_bytes=VLIMIT),
        name="split_x",
    )(dp, slab)


def pre_body(x, wup, act_o, slope_o, x3, wu, act_s, slope_s, sems, osems):
    groups, _, width = x.shape
    rows = groups * 8
    hidden = wup.shape[0]
    spans = blocks(hidden, 512)
    copies = [pltpu.make_async_copy(x, x3, sems.at[0])]
    for n, (start, size) in enumerate(spans):
        copies.append(pltpu.make_async_copy(wup.at[pl.ds(start, size)], wu.at[pl.ds(start, size)], sems.at[1 + n]))
    for copy in copies:
        copy.start()
    copies[0].wait()
    for n, (start, size) in enumerate(spans):
        copies[1 + n].wait()
        pre = dot_nt(x3[...].reshape(rows, width), wu[pl.ds(start, size), :])
        s = jax.nn.sigmoid(pre)
        act_s[pl.ds(start, size), :] = (pre * s).T.astype(BF)
        slope_s[:, pl.ds(start, size)] = s * (1.0 + pre * (1.0 - s))
    outs = [
        pltpu.make_async_copy(act_s, act_o, osems.at[0]),
        pltpu.make_async_copy(slope_s, slope_o, osems.at[1]),
    ]
    for copy in outs:
        copy.start()
    for copy in outs:
        copy.wait()


def expert_pre(x, wup):
    groups, _, width = x.shape
    rows = groups * 8
    hidden = wup.shape[0]
    sds = jax.ShapeDtypeStruct
    return pl.pallas_call(
        pre_body,
        in_specs=[ANY, ANY],
        out_specs=[ANY] * 2,
        out_shape=[sds((hidden, rows), BF), sds((rows, hidden), F32)],
        scratch_shapes=[
            pltpu.VMEM((groups, 8, width), BF),
            pltpu.VMEM((hidden, width), BF),
            pltpu.VMEM((hidden, rows), BF),
            pltpu.VMEM((rows, hidden), F32),
            pltpu.SemaphoreType.DMA((1 + len(blocks(hidden, 512)),)),
            pltpu.SemaphoreType.DMA((2,)),
        ],
        compiler_params=pltpu.CompilerParams(vmem_limit_bytes=VLIMIT),
        cost_estimate=pl.CostEstimate(flops=2 * rows * hidden * width, transcendentals=rows * hidden, bytes_accessed=20_000_000),
        name="expert_pre",
    )(x, wup)


def grad_body(zl_ref, slab, slope, wup, wdn, ret_o, gp_o, dy_o, got, rem, dy3, wu, wd, slope_s, gp_s, gpt_s, ret, rest, sems, osems):
    plane = slab.shape[0]
    peers = plane * 2
    main = peers * 8
    rows = main + peers * 2
    hidden, width = wu.shape
    zl = zl_ref[0]
    copies = load_plane(zl, slab, got, rem, sems)
    more = [
        pltpu.make_async_copy(src, dst, sems.at[5 + i])
        for i, (src, dst) in enumerate(((wdn, wd), (slope, slope_s), (wup, wu)))
    ]
    for copy in more:
        copy.start()
    for copy in copies:
        copy.wait()
    place_main(got, dy3)
    place_rem(zl, rem, dy3)
    outs = [pltpu.make_async_copy(dy3, dy_o, osems.at[0])]
    outs[0].start()
    for copy in more[:2]:
        copy.wait()
    for start, size in blocks(hidden, 512):
        grad = dot_nt(dy3[...].reshape(rows, width), wd[pl.ds(start, size), :])
        value = (grad * slope_s[:, pl.ds(start, size)]).astype(BF)
        gp_s[:, pl.ds(start, size)] = value
        gpt_s[pl.ds(start, size), :] = value.T
    copy = pltpu.make_async_copy(gpt_s, gp_o, osems.at[1])
    copy.start()
    outs.append(copy)
    more[2].wait()
    rest[...] = jnp.zeros(rest.shape, F32)
    r_j = iota((main, peers * 2), 0)
    c_j = iota((main, peers * 2), 1)

    def columns(q, start, size):
        value = dot_nn(gp_s[...], wu[:, pl.ds(start, size)]).astype(BF)
        to_tiles(ret, q * tiles(QW), value[:main])
        place = onehot(((r_j % 8) // 2 == q) & (c_j == (r_j // 8) * 2 + r_j % 2))
        rest[:, pl.ds(0, size)] = rest[:, pl.ds(0, size)] + dot_nn(place, value[main:])

    def send(q, first, count):
        part = pl.ds(first, count)
        return pltpu.make_async_copy(ret.at[:, part], ret_o.at[:, part], osems.at[2 + q])

    def step(q, carry):
        columns(q, pl.multiple_of(q * QW, QW), QW)
        send(q, q * tiles(QW), tiles(QW)).start()
        return carry

    full = width // QW
    end = width - full * QW
    ret[:, tiles(width) - 1] = jnp.zeros((peers, 8, LANES), BF)
    lax.fori_loop(0, full, step, 0)
    columns(full, full * QW, end)
    send(full, full * tiles(QW), tiles(end)).start()
    to_tiles(ret, tiles(width), rest[...])
    send(full + 1, tiles(width), tiles(QW)).start()
    outs += [send(q, q * tiles(QW), tiles(QW)) for q in range(full)]
    outs += [send(full, full * tiles(QW), tiles(end)), send(full + 1, tiles(width), tiles(QW))]
    for copy in outs:
        copy.wait()


def expert_grad(zl, slab, slope, wup, wdn):
    plane = slab.shape[0]
    peers = plane * 2
    hidden, width = wup.shape
    rows = peers * 10
    groups = rows // 8
    count = tiles(width) + tiles(QW)
    sds = jax.ShapeDtypeStruct
    return pl.pallas_call(
        grad_body,
        in_specs=[SMEM, ANY, ANY, ANY, ANY],
        out_specs=[ANY] * 3,
        out_shape=[sds((peers, count, 8, LANES), BF), sds((hidden, rows), BF), sds((groups, 8, width), BF)],
        scratch_shapes=[
            pltpu.VMEM((peers, tiles(width), 8, LANES), BF),
            pltpu.VMEM((plane, tiles(LW), 8, LANES), BF),
            pltpu.VMEM((groups, 8, width), BF),
            pltpu.VMEM((hidden, width), BF),
            pltpu.VMEM((hidden, width), BF),
            pltpu.VMEM(slope.shape, F32),
            pltpu.VMEM((rows, hidden), BF),
            pltpu.VMEM((hidden, rows), BF),
            pltpu.VMEM((peers, count, 8, LANES), BF),
            pltpu.VMEM((peers * 8, QW), F32),
            pltpu.SemaphoreType.DMA((8,)),
            pltpu.SemaphoreType.DMA((7,)),
        ],
        compiler_params=pltpu.CompilerParams(vmem_limit_bytes=VLIMIT),
        cost_estimate=pl.CostEstimate(flops=4 * rows * hidden * width, transcendentals=0, bytes_accessed=40_000_000),
        name="expert_grad",
    )(zl, slab, slope, wup, wdn)


def unpack_body(zl_ref, slab, dy_o, got, rem, dy3, sems):
    for copy in load_plane(zl_ref[0], slab, got, rem, sems):
        copy.wait()
    place_main(got, dy3)
    place_rem(zl_ref[0], rem, dy3)
    copy = pltpu.make_async_copy(dy3, dy_o, sems.at[5])
    copy.start()
    copy.wait()


def unpack_other(zl, slab, width):
    plane = slab.shape[0]
    peers = plane * 2
    groups = peers * 10 // 8
    return pl.pallas_call(
        unpack_body,
        in_specs=[SMEM, ANY],
        out_specs=ANY,
        out_shape=jax.ShapeDtypeStruct((groups, 8, width), BF),
        scratch_shapes=[
            pltpu.VMEM((peers, tiles(width), 8, LANES), BF),
            pltpu.VMEM((plane, tiles(LW), 8, LANES), BF),
            pltpu.VMEM((groups, 8, width), BF),
            pltpu.SemaphoreType.DMA((6,)),
        ],
        compiler_params=pltpu.CompilerParams(vmem_limit_bytes=VLIMIT),
        name="unpack_other",
    )(zl, slab)


def combine_body(rank_ref, ret_ref, out_ref, got, sems):
    rows, tokens = rank_ref.shape
    width = out_ref.shape[0]
    spans = [(tiles(width), tiles(QW))] + [(start // LANES, tiles(size)) for start, size in blocks(width, QW)]
    copies = [
        pltpu.make_async_copy(ret_ref.at[:, pl.ds(c, n)], got.at[:, pl.ds(c, n)], sems.at[i])
        for i, (c, n) in enumerate(spans)
    ]
    for copy in copies:
        copy.start()
    slot = iota((rows, tokens), 0) % 8
    rank = rank_ref[...]
    last = rank == (slot % 2 + 9).astype(F32)
    picks = jnp.concatenate([onehot(last & (slot // 2 == q)) for q in range(4)], axis=1)
    main = onehot(rank == (slot + 1).astype(F32))
    copies[0].wait()
    rem = dot_tn(picks, from_tiles(got, *spans[0]))
    for q, (start, size) in enumerate(blocks(width, QW)):
        copies[1 + q].wait()
        value = dot_tn(main, from_tiles(got, *spans[1 + q]))[:, :size]
        value = value + rem[q * tokens : (q + 1) * tokens, :size]
        out_ref[pl.ds(start, size), :] = value.T.astype(BF)


def combine(rank, ret, width):
    vmem = pl.BlockSpec(memory_space=pltpu.VMEM)
    return pl.pallas_call(
        combine_body,
        in_specs=[vmem, ANY],
        out_specs=vmem,
        out_shape=jax.ShapeDtypeStruct((width, rank.shape[1]), BF),
        scratch_shapes=[pltpu.VMEM(ret.shape, BF), pltpu.SemaphoreType.DMA((5,))],
        compiler_params=pltpu.CompilerParams(vmem_limit_bytes=VLIMIT),
        name="combine",
    )(rank, ret)


def local(sizes, tokens_in, grad_out, expert_ids, combine_weights, up_weight, down_weight):
    n_dp, n_zl, n_plane = sizes
    peers = n_zl * n_plane
    width = tokens_in.shape[1]
    x = tokens_in.T
    dy = grad_out.T
    ids = expert_ids.T
    weights = combine_weights.T
    wup = up_weight[0].T
    wdn = down_weight[0]
    dp = lax.axis_index("dp").astype(jnp.int32)
    zl = lax.axis_index("zl").astype(jnp.int32)

    def move(value, cross, flip):
        pairs = []
        for i in range(n_dp * peers):
            d, z, p = i // peers, (i // n_plane) % n_zl, i % n_plane
            pairs.append((i, ((d ^ cross) * n_zl + (z ^ flip)) * n_plane + p))
        return lax.ppermute(value, ALL, pairs)

    slab, rank, meta = pack_x(ids, weights, x, peers)
    dy_near = move(dy, 0, 1)
    meta_near = move(meta, 0, 1)
    dy_a, meta_a = move(dy, 1, 0), move(meta, 1, 0)
    dy_b, meta_b = move(dy, 1, 1), move(meta, 1, 1)

    got_x = lax.all_to_all(slab, GROUP, 0, 0, tiled=True)
    slab_dy = pack_dy(zl[None], dy, dy_near, meta, meta_near, n_plane)
    got_dy = lax.all_to_all(slab_dy, PLANE, 0, 0, tiled=True)
    slab_other = pack_dy(zl[None], dy_a, dy_b, meta_a, meta_b, n_plane)
    got_other = lax.all_to_all(slab_other, PLANE, 0, 0, tiled=True)

    x_rows, xh, x_send = split_x(dp[None], got_x, width)
    act, slope = expert_pre(x_rows, wup)
    xh_other = move(x_send, 1, 0)
    act_keep = lax.dynamic_slice_in_dim(act, dp * (act.shape[0] // 2), act.shape[0] // 2, 0)
    act_send = lax.dynamic_slice_in_dim(act, (1 - dp) * (act.shape[0] // 2), act.shape[0] // 2, 0)
    act_other = move(act_send, 1, 0)
    ret, gp, dyr = expert_grad(zl[None], got_dy, slope, wup, wdn)
    gp_other = move(gp, 1, 0)
    back = lax.all_to_all(ret, GROUP, 0, 0, tiled=True)
    dy_other = unpack_other(zl[None], got_other, width)

    flat = lambda a: a.reshape(-1, a.shape[-1])
    up = lambda a, b: lax.dot_general(a, b, (((0,), (1,)), ((), ())), preferred_element_type=F32)
    grad_down = (dot_nn(act_keep, flat(dyr)) + dot_nn(act_other, flat(dy_other))).astype(BF)[None]
    grad_up = (up(flat(xh_other), gp_other) + up(flat(xh), gp)).astype(BF)[None]
    grad_input = combine(rank, back, width).T
    return grad_input, grad_up, grad_down


def build(devices, shape):
    n_dp, n_zl, n_y, n_x, n_core = shape
    fine = Mesh(devices.reshape(shape), ALL)
    token = P(ALL, None)
    weight = P(GROUP, None, None)
    inner = functools.partial(local, (n_dp, n_zl, n_y * n_x * n_core))

    return jax.shard_map(
        inner,
        mesh=fine,
        in_specs=(token, token, token, token, weight, weight),
        out_specs=(token, P(GROUP, "dp", None), P(GROUP, "dp", None)),
        check_vma=False,
    )


def solution(mesh):
    return build(mesh.devices, (2, 2, 4, 4, 2))
```

time: 374 us -> 364 us (0.973)
  waiting for transfers between devices: 218 us -> 209 us
    all_to_all x1, waiting for transfers between devices: 9.42 us -> 2.99 us  [local(): got_other = lax.all_to_all(slab_other, PLANE, 0, 0, tiled=True)]
    pallas_call x5 -> x6, Pallas kernels: 37.8 us -> 37.3 us  [the longest x1 13.1 us: expert_pre(): pl.pallas_call(pre_body, in_specs=[ANY, ANY], out_specs=[ANY] * 2, out_sh...]
  transfers between devices with their start and end apart: 13 -> 13, of which waited for: 7 -> 7; matrix products, arithmetic and copies ran while one was open for 8% -> 8% of each run, Pallas kernels for 15% -> 16%
where the time goes in v3:
time: 364 us; the launch traced here: 357 us
  waiting for transfers between devices  209 us (57%)
  Pallas kernels  65.3 us (18%)
  starting transfers between devices  48.7 us (13%)
  matrix products  28.9 us (8%)
  local copies, waits for them, and re-layouts  3.87 us (1%)
    ppermute x9, waiting for transfers between devices, move(): return lax.ppermute(value, ALL, pairs)  202 us
    pallas_call x1, Pallas kernels, expert_grad(): pl.pallas_call(grad_body, in_specs=[SMEM, ANY, ANY, ANY, ANY], out_specs=...  23.5 us
    dot_general x2, matrix products, dot_nn(): lax.dot_general(left, right, (((1,), (0,)), ((), ())), preferred_element_...  14.7 us
    dot_general x2, matrix products, local(): lax.dot_general(a, b, (((0,), (1,)), ((), ())), preferred_element_type=F32)  14.2 us
    ppermute x9, starting transfers between devices, move(): return lax.ppermute(value, ALL, pairs)  14.1 us
    pallas_call x1, Pallas kernels, expert_pre(): pl.pallas_call(pre_body, in_specs=[ANY, ANY], out_specs=[ANY] * 2, out_sh...  13.1 us
    all_to_all x1, starting transfers between devices, local(): got_x = lax.all_to_all(slab, GROUP, 0, 0, tiled=True)  10.6 us
    all_to_all x1, starting transfers between devices, local(): back = lax.all_to_all(ret, GROUP, 0, 0, tiled=True)  8.33 us
  transfers between devices with their start and end apart: 13, of which 7 were waited for; matrix products, arithmetic and copies ran while one was open for 8% of the time, Pallas kernels for 16%

profile of v3, /device:TPU:1, one launch (start us, length us, event | category | flops | bytes accessed | tf_op | source)
XLA Modules:
  0.0 357.3 jit_solution(17368943157338978845)
XLA Ops:
  0.6 4.5 %pack_x.1 = (bf16[64,29,8,128]{3,2,1,0:T(8,128)(2,1)}, f32[512,128]{1,0:T(8,128)}, f32[8,128]{1,0:T(8,128)}) custom-call(s32[4,128]{1,0:T(4,128)} %bitcast.36, f32[4,128]{1,0:T(4,128)} %bitcast.37, bf16[2880,128]{1,0:T(8,128)(2,1)} %bitcast.31), custom_call_target="tpu_custom_call" | custom-call | tf_op jit(solution)/shard_map/pack_x/pallas_call | solution.py:123
  5.2 0.0 copy-start.1
  5.2 10.6 %all-to-all-start.1 = ((bf16[64,29,8,128]{3,2,1,0:T(8,128)(2,1)}), bf16[64,29,8,128]{3,2,1,0:T(8,128)(2,1)}, u32[]{:S(2)}, u32[]{:S(2)}) async-start(bf16[64,29,8,128]{3,2,1,0:T(8,128)(2,1)} %get-tuple-element.16), calls=%async_computation.1 | async-start | bytes 7602176 | tf_op jit(solution)/shard_map/all_to_all | solution.py:535
  15.8 1.5 collective-permute-start
  17.4 0.1 collective-permute-start.1
  17.5 57.7 %collective-permute-done.1.mb_ref = f32[8,128]{1,0:T(8,128)S(1)} collective-permute-done((f32[8,128]{1,0:T(8,128)S(1)}, f32[8,128]{1,0:T(8,128)S(1)}, u32[]{:S(2)}, u32[]{:S(2)}) %collective-permute-start.1) | collective-permute-done | bytes 4128 | tf_op jit(solution)/shard_map/ppermute | solution.py:527
  75.2 0.0 collective-permute-done.pb_ref
  75.2 0.6 copy-done.10
  75.8 0.3 copy-done.5
  76.1 4.0 %shard_map.85 = bf16[32,58,8,128]{3,2,1,0:T(8,128)(2,1)} custom-call(s32[1]{0:T(128)} %bitcast.3.zl_ref, bf16[2880,128]{1,0:T(8,128)(2,1)} %bitcast.32, bf16[2880,128]{1,0:T(8,128)(2,1)} %copy-done.5, f32[8,128]{1,0:T(8,128)} %get-tuple-element.15.ma_ref, f32[8,128]{1,0:T(8,128)} %copy-done.10), custom_call_target="tpu_custom_call" | custom-call | tf_op jit(solution)/shard_map/pallas_call | solution.py:190
  80.1 0.0 copy-start.2
  80.1 0.0 copy-start.7
  80.1 0.0 all-to-all-done.1.slab
  80.1 7.6 %all-to-all-start = ((bf16[32,58,8,128]{3,2,1,0:T(8,128)(2,1)}), bf16[32,58,8,128]{3,2,1,0:T(8,128)(2,1)}, u32[]{:S(2)}, u32[]{:S(2)}) async-start(bf16[32,58,8,128]{3,2,1,0:T(8,128)(2,1)} %shard_map.85), calls=%async_computation | async-start | bytes 7602176 | tf_op jit(solution)/shard_map/all_to_all | solution.py:537
  87.7 3.4 collective-permute-start.5
  91.1 0.0 collective-permute-start.6
  91.1 1.2 collective-permute-start.7
  92.4 1.4 collective-permute-start.8
  93.8 14.1 %collective-permute-done.7.ma_ref = f32[8,128]{1,0:T(8,128)S(1)} collective-permute-done((f32[8,128]{1,0:T(8,128)S(1)}, f32[8,128]{1,0:T(8,128)S(1)}, u32[]{:S(2)}, u32[]{:S(2)}) %collective-permute-start.7) | collective-permute-done | bytes 4128 | tf_op jit(solution)/shard_map/ppermute | solution.py:527
  107.9 16.2 %collective-permute-done.8.mb_ref = f32[8,128]{1,0:T(8,128)S(1)} collective-permute-done((f32[8,128]{1,0:T(8,128)S(1)}, f32[8,128]{1,0:T(8,128)S(1)}, u32[]{:S(2)}, u32[]{:S(2)}) %collective-permute-start.8) | collective-permute-done | bytes 4128 | tf_op jit(solution)/shard_map/ppermute | solution.py:527
  124.1 0.0 collective-permute-done.5.pa_ref
  124.2 0.0 collective-permute-done.6.pb_ref
  124.2 0.6 copy-done.9
  124.7 0.3 copy-done.3
  125.0 0.9 copy-done.4
  125.9 4.0 %shard_map.86 = bf16[32,58,8,128]{3,2,1,0:T(8,128)(2,1)} custom-call(s32[1]{0:T(128)} %bitcast.3.zl_ref, bf16[2880,128]{1,0:T(8,128)(2,1)} %copy-done.3, bf16[2880,128]{1,0:T(8,128)(2,1)} %copy-done.4, f32[8,128]{1,0:T(8,128)} %copy-done.8, f32[8,128]{1,0:T(8,128)} %copy-done.9), custom_call_target="tpu_custom_call" | custom-call | tf_op jit(solution)/shard_map/pallas_call | solution.py:190
  129.9 4.6 %all-to-all-done.slab = bf16[32,58,8,128]{3,2,1,0:T(8,128)(2,1)} async-done(((bf16[32,58,8,128]{3,2,1,0:T(8,128)(2,1)}), bf16[32,58,8,128]{3,2,1,0:T(8,128)(2,1)}, u32[]{:S(2)}, u32[]{:S(2)}) %all-to-all-start) | async-done | bytes 3801120 | tf_op jit(solution)/shard_map/all_to_all | solution.py:537
  134.5 8.0 %all-to-all-start.3 = ((bf16[32,58,8,128]{3,2,1,0:T(8,128)(2,1)}), bf16[32,58,8,128]{3,2,1,0:T(8,128)(2,1)}, u32[]{:S(2)}, u32[]{:S(2)}) async-start(bf16[32,58,8,128]{3,2,1,0:T(8,128)(2,1)} %shard_map.86), calls=%async_computation.3 | async-start | bytes 7602176 | tf_op jit(solution)/shard_map/all_to_all | solution.py:539
  142.5 6.5 %split_x.1 = (bf16[80,8,2880]{2,1,0:T(8,128)(2,1)}, bf16[80,8,1440]{2,1,0:T(8,128)(2,1)}, bf16[80,8,1440]{2,1,0:T(8,128)(2,1)}) custom-call(s32[1]{0:T(128)} %bitcast.5.dp_ref, bf16[64,29,8,128]{3,2,1,0:T(8,128)(2,1)} %all-to-all-done.1.slab), custom_call_target="tpu_custom_call" | custom-call | tf_op jit(solution)/shard_map/split_x/pallas_call | solution.py:276
  149.0 13.1 %expert_pre.1 = (bf16[1440,640]{1,0:T(8,128)(2,1)}, f32[640,1440]{1,0:T(8,128)}) custom-call(bf16[80,8,2880]{2,1,0:T(8,128)(2,1)} %get-tuple-element.17.x, bf16[1440,2880]{1,0:T(8,128)(2,1)} %bitcast.38), custom_call_target="tpu_custom_call" | custom-call | flops 5308416000 | bytes 20000000 | tf_op jit(solution)/shard_map/expert_pre/pallas_call | solution.py:326
  162.2 23.5 %expert_grad.1 = (bf16[64,29,8,128]{3,2,1,0:T(8,128)(2,1)}, bf16[1440,640]{1,0:T(8,128)(2,1)}, bf16[80,8,2880]{2,1,0:T(8,128)(2,1)}) custom-call(s32[1]{0:T(128)} %bitcast.3.zl_ref, bf16[32,58,8,128]{3,2,1,0:T(8,128)(2,1)} %all-to-all-done.slab, f32[640,1440]{1,0:T(8,128)} %get-tuple-element.18.slope, bf16[1440,2880]{1,0:T(8,128)(2,1)} %bitcast.39, ...), custom_call_target="tpu_custom_call" | custom-call | flops 10616832000 | bytes 40000000 | tf_op jit(solution)/shard_map/expert_grad/pallas_call | solution.py:417
  185.7 3.0 all-to-all-done.3.slab
  188.7 8.3 %all-to-all-start.2 = ((bf16[64,29,8,128]{3,2,1,0:T(8,128)(2,1)}), bf16[64,29,8,128]{3,2,1,0:T(8,128)(2,1)}, u32[]{:S(2)}, u32[]{:S(2)}) async-start(bf16[64,29,8,128]{3,2,1,0:T(8,128)(2,1)} %get-tuple-element.19), calls=%async_computation.2 | async-start | bytes 7602176 | tf_op jit(solution)/shard_map/all_to_all | solution.py:549
  197.1 3.4 collective-permute-start.2
  200.4 1.3 constant_dynamic-slice_fusion
  201.7 0.1 collective-permute-start.4
  201.8 3.0 collective-permute-start.3
  204.8 9.2 %fusion.4 = f32[720,2880]{1,0:T(8,128)} fusion(bf16[80,8,2880]{2,1,0:T(8,128)(2,1)} %get-tuple-element.24, bf16[1440,640]{1,0:T(8,128)(2,1)} %get-tuple-element.23, s32[]{:T(128)S(6)} %select_n.6), kind=kOutput, calls=%fused_computation.6 | convolution fusion | flops 2654208000 | bytes 12984324 | tf_op jit(solution)/shard_map/dot_general | solution.py:33
  214.0 4.5 %unpack_other.1 = bf16[80,8,2880]{2,1,0:T(8,128)(2,1)} custom-call(s32[1]{0:T(128)} %bitcast.3.zl_ref, bf16[32,58,8,128]{3,2,1,0:T(8,128)(2,1)} %all-to-all-done.3.slab), custom_call_target="tpu_custom_call" | custom-call | tf_op jit(solution)/shard_map/unpack_other/pallas_call | solution.py:456
  218.5 0.0 copy-start
  218.5 6.0 %fusion.6 = f32[1440,1440]{1,0:T(8,128)S(1)} fusion(bf16[1440,640]{1,0:T(8,128)(2,1)} %get-tuple-element.21, bf16[80,8,1440]{2,1,0:T(8,128)(2,1)} %get-tuple-element.22), kind=kOutput, calls=%fused_computation.8 | convolution fusion | flops 2654208000 | bytes 11980800 | tf_op jit(solution)/shard_map/dot_general | solution.py:553
  224.6 79.6 %collective-permute-done.4 = bf16[720,640]{1,0:T(8,128)(2,1)S(1)} collective-permute-done((bf16[720,640]{1,0:T(8,128)(2,1)S(1)}, bf16[720,640]{1,0:T(8,128)(2,1)S(1)}, u32[]{:S(2)}, u32[]{:S(2)}) %collective-permute-start.4) | collective-permute-done | bytes 921632 | tf_op jit(solution)/shard_map/ppermute | solution.py:527
  304.2 5.4 %fusion.2 = bf16[1,720,2880]{2,1,0:T(8,128)(2,1)} fusion(f32[720,2880]{1,0:T(8,128)S(1)} %copy-done.11, bf16[720,640]{1,0:T(8,128)(2,1)S(1)} %collective-permute-done.4, bf16[80,8,2880]{2,1,0:T(8,128)(2,1)S(1)} %copy-done), kind=kOutput, calls=%fused_computation.4 | convolution fusion | flops 2658355200 | bytes 17049600 | tf_op jit(solution)/shard_map/dot_general | solution.py:33
  309.6 0.0 collective-permute-done.2
  309.6 34.2 %collective-permute-done.3 = bf16[1440,640]{1,0:T(8,128)(2,1)} collective-permute-done((bf16[1440,640]{1,0:T(8,128)(2,1)}, bf16[1440,640]{1,0:T(8,128)(2,1)}, u32[]{:S(2)}, u32[]{:S(2)}) %collective-permute-start.3) | collective-permute-done | bytes 1843232 | tf_op jit(solution)/shard_map/ppermute | solution.py:527
  343.8 8.2 %fusion.1 = bf16[1,1440,1440]{2,1,0:T(8,128)(2,1)} fusion(f32[1440,1440]{1,0:T(8,128)S(1)} %fusion.6, bf16[1440,640]{1,0:T(8,128)(2,1)} %collective-permute-done.3, bf16[80,8,1440]{2,1,0:T(8,128)(2,1)} %collective-permute-done.2), kind=kOutput, calls=%fused_computation.3 | convolution fusion | flops 2658355200 | bytes 16128000 | tf_op jit(solution)/shard_map/dot_general | solution.py:553
  352.0 0.0 all-to-all-done.2.ret_ref
  352.0 5.0 %combine.1 = bf16[2880,128]{1,0:T(8,128)(2,1)} custom-call(f32[512,128]{1,0:T(8,128)} %get-tuple-element.14.rank_ref, bf16[64,29,8,128]{3,2,1,0:T(8,128)(2,1)} %all-to-all-done.2.ret_ref), custom_call_target="tpu_custom_call" | custom-call | tf_op jit(solution)/shard_map/combine/pallas_call | solution.py:498
  (15 shorter events, 0.0 us)
Async XLA Ops:
  5.2 10.7 %copy-start.1 = (bf16[128,2880]{0,1:T(8,128)(2,1)S(1)}, bf16[128,2880]{0,1:T(8,128)(2,1)}, u32[]{:S(2)}) copy-start(bf16[128,2880]{0,1:T(8,128)(2,1)} %param.7) | copy-start | bytes 2211844
  5.2 12.2 %copy-start.6 = (f32[8,128]{1,0:T(8,128)S(1)}, f32[8,128]{1,0:T(8,128)}, u32[]{:S(2)}) copy-start(f32[8,128]{1,0:T(8,128)} %get-tuple-element.15.ma_ref) | copy-start | bytes 12292
  5.2 74.9 %all-to-all-start.1 = ((bf16[64,29,8,128]{3,2,1,0:T(8,128)(2,1)}), bf16[64,29,8,128]{3,2,1,0:T(8,128)(2,1)}, u32[]{:S(2)}, u32[]{:S(2)}) async-start(bf16[64,29,8,128]{3,2,1,0:T(8,128)(2,1)} %get-tuple-element.16), calls=%async_computation.1 | async-start | bytes 7602176 | tf_op jit(solution)/shard_map/all_to_all | solution.py:535
  15.8 59.4 %collective-permute-start = (bf16[2880,128]{1,0:T(8,128)(2,1)S(1)}, bf16[2880,128]{1,0:T(8,128)(2,1)S(1)}, u32[]{:S(2)}, u32[]{:S(2)}) collective-permute-start(bf16[2880,128]{1,0:T(8,128)(2,1)S(1)} %bitcast.33), channel_id=1, source_target_pairs={{0,32},{1,33},{2,34},{3,35},{4,36},{5,37},{6,38},{7,39},{8,40},{9,... | collective-permute-start | bytes 2211848 | tf_op jit(solution)/shard_map/ppermute | solution.py:527
  17.4 57.8 %collective-permute-start.1 = (f32[8,128]{1,0:T(8,128)S(1)}, f32[8,128]{1,0:T(8,128)S(1)}, u32[]{:S(2)}, u32[]{:S(2)}) collective-permute-start(f32[8,128]{1,0:T(8,128)S(1)} %copy-done.6), channel_id=1, source_target_pairs={{0,32},{1,33},{2,34},{3,35},{4,36},{5,37},{6,38},{7,39},{8,40},{9,... | collective-permute-start | bytes 12296 | tf_op jit(solution)/shard_map/ppermute | solution.py:527
  75.2 0.6 copy-start.10
  75.2 0.9 copy-start.5
  80.1 7.7 %copy-start.2 = (bf16[128,2880]{0,1:T(8,128)(2,1)S(1)}, bf16[128,2880]{0,1:T(8,128)(2,1)}, u32[]{:S(2)}) copy-start(bf16[128,2880]{0,1:T(8,128)(2,1)} %param.7) | copy-start | bytes 2211844
  80.1 11.0 %copy-start.7 = (f32[8,128]{1,0:T(8,128)S(1)}, f32[8,128]{1,0:T(8,128)}, u32[]{:S(2)}) copy-start(f32[8,128]{1,0:T(8,128)} %get-tuple-element.15.ma_ref) | copy-start | bytes 12292
  80.1 54.4 %all-to-all-start = ((bf16[32,58,8,128]{3,2,1,0:T(8,128)(2,1)}), bf16[32,58,8,128]{3,2,1,0:T(8,128)(2,1)}, u32[]{:S(2)}, u32[]{:S(2)}) async-start(bf16[32,58,8,128]{3,2,1,0:T(8,128)(2,1)} %shard_map.85), calls=%async_computation | async-start | bytes 7602176 | tf_op jit(solution)/shard_map/all_to_all | solution.py:537
  87.7 36.4 %collective-permute-start.5 = (bf16[2880,128]{1,0:T(8,128)(2,1)S(1)}, bf16[2880,128]{1,0:T(8,128)(2,1)S(1)}, u32[]{:S(2)}, u32[]{:S(2)}) collective-permute-start(bf16[2880,128]{1,0:T(8,128)(2,1)S(1)} %bitcast.34), channel_id=1, source_target_pairs={{0,64},{1,65},{2,66},{3,67},{4,68},{5,69},{6,70},{7,71},{8,72},{9,... | collective-permute-start | bytes 2211848 | tf_op jit(solution)/shard_map/ppermute | solution.py:527
  91.1 33.0 %collective-permute-start.6 = (bf16[2880,128]{1,0:T(8,128)(2,1)S(1)}, bf16[2880,128]{1,0:T(8,128)(2,1)S(1)}, u32[]{:S(2)}, u32[]{:S(2)}) collective-permute-start(bf16[2880,128]{1,0:T(8,128)(2,1)S(1)} %bitcast.35), channel_id=1, source_target_pairs={{0,96},{1,97},{2,98},{3,99},{4,100},{5,101},{6,102},{7,103},{8,104... | collective-permute-start | bytes 2211848 | tf_op jit(solution)/shard_map/ppermute | solution.py:527
  91.1 16.8 %collective-permute-start.7 = (f32[8,128]{1,0:T(8,128)S(1)}, f32[8,128]{1,0:T(8,128)S(1)}, u32[]{:S(2)}, u32[]{:S(2)}) collective-permute-start(f32[8,128]{1,0:T(8,128)S(1)} %copy-done.7), channel_id=1, source_target_pairs={{0,64},{1,65},{2,66},{3,67},{4,68},{5,69},{6,70},{7,71},{8,72},{9,... | collective-permute-start | bytes 12296 | tf_op jit(solution)/shard_map/ppermute | solution.py:527
  92.4 31.8 %collective-permute-start.8 = (f32[8,128]{1,0:T(8,128)S(1)}, f32[8,128]{1,0:T(8,128)S(1)}, u32[]{:S(2)}, u32[]{:S(2)}) collective-permute-start(f32[8,128]{1,0:T(8,128)S(1)} %copy-done.7), channel_id=1, source_target_pairs={{0,96},{1,97},{2,98},{3,99},{4,100},{5,101},{6,102},{7,103},{8,104... | collective-permute-start | bytes 12296 | tf_op jit(solution)/shard_map/ppermute | solution.py:527
  107.9 16.2 %copy-start.8 = (f32[8,128]{1,0:T(8,128)}, f32[8,128]{1,0:T(8,128)S(1)}, u32[]{:S(2)}) copy-start(f32[8,128]{1,0:T(8,128)S(1)} %collective-permute-done.7.ma_ref) | copy-start | bytes 12292
  124.1 0.6 copy-start.9
  124.2 0.9 copy-start.3
  125.0 0.9 copy-start.4
  134.5 54.2 %all-to-all-start.3 = ((bf16[32,58,8,128]{3,2,1,0:T(8,128)(2,1)}), bf16[32,58,8,128]{3,2,1,0:T(8,128)(2,1)}, u32[]{:S(2)}, u32[]{:S(2)}) async-start(bf16[32,58,8,128]{3,2,1,0:T(8,128)(2,1)} %shard_map.86), calls=%async_computation.3 | async-start | bytes 7602176 | tf_op jit(solution)/shard_map/all_to_all | solution.py:539
  188.7 163.2 %all-to-all-start.2 = ((bf16[64,29,8,128]{3,2,1,0:T(8,128)(2,1)}), bf16[64,29,8,128]{3,2,1,0:T(8,128)(2,1)}, u32[]{:S(2)}, u32[]{:S(2)}) async-start(bf16[64,29,8,128]{3,2,1,0:T(8,128)(2,1)} %get-tuple-element.19), calls=%async_computation.2 | async-start | bytes 7602176 | tf_op jit(solution)/shard_map/all_to_all | solution.py:549
  197.1 112.5 %collective-permute-start.2 = (bf16[80,8,1440]{2,1,0:T(8,128)(2,1)}, bf16[80,8,1440]{2,1,0:T(8,128)(2,1)}, u32[]{:S(2)}, u32[]{:S(2)}) collective-permute-start(bf16[80,8,1440]{2,1,0:T(8,128)(2,1)} %get-tuple-element.20), channel_id=1, source_target_pairs={{0,64},{1,65},{2,66},{3,67},{4,68},{5,69},{6,70},{7,71},{8,72},{9,... | collective-permute-start | bytes 5529608 | tf_op jit(solution)/shard_map/ppermute | solution.py:527
  201.7 102.4 %collective-permute-start.4 = (bf16[720,640]{1,0:T(8,128)(2,1)S(1)}, bf16[720,640]{1,0:T(8,128)(2,1)S(1)}, u32[]{:S(2)}, u32[]{:S(2)}) collective-permute-start(bf16[720,640]{1,0:T(8,128)(2,1)S(1)} %constant_dynamic-slice_fusion), channel_id=1, source_target_pairs={{0,64},{1,65},{2,66},{3,67},{4,68},{5,69},{6,70},{7,71},{8,72},{9,... | collective-permute-start | bytes 2764808 | tf_op jit(solution)/shard_map/ppermute | solution.py:527
  201.8 142.0 %collective-permute-start.3 = (bf16[1440,640]{1,0:T(8,128)(2,1)}, bf16[1440,640]{1,0:T(8,128)(2,1)}, u32[]{:S(2)}, u32[]{:S(2)}) collective-permute-start(bf16[1440,640]{1,0:T(8,128)(2,1)} %get-tuple-element.21), channel_id=1, source_target_pairs={{0,64},{1,65},{2,66},{3,67},{4,68},{5,69},{6,70},{7,71},{8,72},{9,... | collective-permute-start | bytes 5529608 | tf_op jit(solution)/shard_map/ppermute | solution.py:527
  218.5 85.7 %copy-start = (bf16[80,8,2880]{2,1,0:T(8,128)(2,1)S(1)}, bf16[80,8,2880]{2,1,0:T(8,128)(2,1)}, u32[]{:S(2)}) copy-start(bf16[80,8,2880]{2,1,0:T(8,128)(2,1)} %unpack_other.1) | copy-start | bytes 11059204
  218.5 85.7 %copy-start.11 = (f32[720,2880]{1,0:T(8,128)S(1)}, f32[720,2880]{1,0:T(8,128)}, u32[]{:S(2)}) copy-start(f32[720,2880]{1,0:T(8,128)} %fusion.4) | copy-start | bytes 24883204

commit v4 on v3

--- a/solution.py
+++ b/solution.py
@@ -11,6 +11,7 @@
 LW = 1536
 QW = 768
 LANES = 128
+HB = 480
 BF = jnp.bfloat16
 F32 = jnp.float32
 ALL = ("dp", "zl", "y", "x", "core")
@@ -72,6 +73,10 @@
 
 def blocks(total, size):
     return [(start, min(size, total - start)) for start in range(0, total, size)]
+
+
+def parts(rows):
+    return rows * 3 // 5
 
 
 def tiles(width):
@@ -135,64 +140,80 @@
     )(ids, weights, x)
 
 
-def pack_dy_body(zl_ref, pa_ref, pb_ref, ma_ref, mb_ref, out_o, out_s, sems):
-    width, tokens = pa_ref.shape
+def pack_dy_body(zl_ref, pa_ref, pb_ref, ma_ref, mb_ref, out_o, pay, meta, ranks, scales, out_s, sems, isems):
+    _, width, tokens = pay.shape
     peers = out_s.shape[0]
     rows = peers * 8
-    top = ma_ref.shape[0] // 2
-    pays = (pa_ref, pb_ref)
+    top = meta.shape[1] // 2
+    loads = [
+        pltpu.make_async_copy(src, dst.at[i % 2], isems.at[i])
+        for i, (src, dst) in enumerate(((ma_ref, meta), (mb_ref, meta), (pa_ref, pay), (pb_ref, pay)))
+    ]
+    for copy in loads:
+        copy.start()
+    for copy in loads:
+        copy.wait()
     slot = iota((rows, tokens), 0) % 8
     spans = blocks(width, LW)
-    ranks, scales = [], []
-    for meta in (ma_ref, mb_ref):
-        ids = meta[pl.ds(0, top), :].astype(jnp.int32)
-        weight = meta[pl.ds(top, top), :]
+
+    def send(i, first, count):
+        part = pl.ds(first, count)
+        return pltpu.make_async_copy(out_s.at[:, part], out_o.at[:, part], sems.at[i])
+
+    def source(s, carry):
+        ids = meta[s, pl.ds(0, top), :].astype(jnp.int32)
+        weight = meta[s, pl.ds(top, top), :]
         w1 = weight.astype(BF)
         rest = weight - w1.astype(F32)
         w2 = rest.astype(BF)
         w3 = (rest - w2.astype(F32)).astype(BF)
-        parts = [w.astype(F32) for w in (w1, w2, w3)]
-        rank, weight = rank_rows(ids, parts, zl_ref[0] * peers, peers)
-        ranks.append(rank)
-        scales.append(weight)
-    copies = []
-
-    def send(first, value):
-        to_tiles(out_s, first, value)
-        part = pl.ds(first, tiles(value.shape[1]))
-        copies.append(pltpu.make_async_copy(out_s.at[:, part], out_o.at[:, part], sems.at[len(copies)]))
-        copies[-1].start()
-
-    for s in range(2):
-        hit = ranks[s] == (slot + 1).astype(F32)
-        scale = row_weight(hit, scales[s])
-        for start, size in spans:
+        rank, weight = rank_rows(ids, [w.astype(F32) for w in (w1, w2, w3)], zl_ref[0] * peers, peers)
+        ranks[s] = rank
+        scales[s] = weight
+        hit = rank == (slot + 1).astype(F32)
+        scale = row_weight(hit, weight)
+        for i, (start, size) in enumerate(spans):
             count = tiles(size)
             first = 2 * (start // LANES) + s * count
-            send(first, dot_nt(onehot(hit), padded(pays[s][pl.ds(start, size), :], count * LANES)) * scale)
-    picks, source = [], []
+            to_tiles(out_s, first, dot_nt(onehot(hit), padded(pay[s, pl.ds(start, size), :], count * LANES)) * scale)
+            send(2 * s + i, first, count).start()
+        return carry
+
+    lax.fori_loop(0, 2, source, 0)
+    picks, pieces = [], []
     scale = jnp.zeros((rows, 1), F32)
     for s in range(2):
         hit = ranks[s] == (slot % 2 + 9).astype(F32)
         scale = scale + jnp.where((slot[:, :1] // 2) % 2 == s, row_weight(hit, scales[s]), 0.0)
         for c, (start, size) in enumerate(spans):
             picks.append(onehot(hit & (slot // 2 == c * 2 + s)))
-            source.append(padded(pays[s][pl.ds(start, size), :], LW))
-    send(2 * tiles(width), dot_nt(jnp.concatenate(picks, axis=1), jnp.concatenate(source, axis=1)) * scale)
-    for copy in copies:
-        copy.wait()
+            pieces.append(padded(pay[s, pl.ds(start, size), :], LW))
+    last = 2 * tiles(width)
+    to_tiles(out_s, last, dot_nt(jnp.concatenate(picks, axis=1), jnp.concatenate(pieces, axis=1)) * scale)
+    send(4, last, tiles(LW)).start()
+    for s in range(2):
+        for i, (start, size) in enumerate(spans):
+            send(2 * s + i, 2 * (start // LANES) + s * tiles(size), tiles(size)).wait()
+    send(4, last, tiles(LW)).wait()
 
 
 def pack_dy(zl, dy_a, dy_b, meta_a, meta_b, peers):
-    width = dy_a.shape[0]
+    width, tokens = dy_a.shape
     shape = (peers, 2 * tiles(width) + tiles(LW), 8, LANES)
-    vmem = pl.BlockSpec(memory_space=pltpu.VMEM)
     return pl.pallas_call(
         pack_dy_body,
-        in_specs=[SMEM, vmem, vmem, vmem, vmem],
+        in_specs=[SMEM, ANY, ANY, ANY, ANY],
         out_specs=ANY,
         out_shape=jax.ShapeDtypeStruct(shape, BF),
-        scratch_shapes=[pltpu.VMEM(shape, BF), pltpu.SemaphoreType.DMA((5,))],
+        scratch_shapes=[
+            pltpu.VMEM((2,) + dy_a.shape, BF),
+            pltpu.VMEM((2,) + meta_a.shape, F32),
+            pltpu.VMEM((2, peers * 8, tokens), F32),
+            pltpu.VMEM((2, peers * 8, tokens), F32),
+            pltpu.VMEM(shape, BF),
+            pltpu.SemaphoreType.DMA((5,)),
+            pltpu.SemaphoreType.DMA((4,)),
+        ],
         compiler_params=pltpu.CompilerParams(vmem_limit_bytes=VLIMIT),
     )(zl, dy_a, dy_b, meta_a, meta_b)
 
@@ -295,19 +316,21 @@
     groups, _, width = x.shape
     rows = groups * 8
     hidden = wup.shape[0]
-    spans = blocks(hidden, 512)
-    copies = [pltpu.make_async_copy(x, x3, sems.at[0])]
-    for n, (start, size) in enumerate(spans):
-        copies.append(pltpu.make_async_copy(wup.at[pl.ds(start, size)], wu.at[pl.ds(start, size)], sems.at[1 + n]))
+    copies = [pltpu.make_async_copy(x, x3, sems.at[0]), pltpu.make_async_copy(wup, wu, sems.at[1])]
     for copy in copies:
         copy.start()
-    copies[0].wait()
-    for n, (start, size) in enumerate(spans):
-        copies[1 + n].wait()
-        pre = dot_nt(x3[...].reshape(rows, width), wu[pl.ds(start, size), :])
+    for copy in copies:
+        copy.wait()
+
+    def block(n, carry):
+        span = pl.ds(pl.multiple_of(n * HB, HB), HB)
+        pre = dot_nt(x3[...].reshape(rows, width), wu[span, :])
         s = jax.nn.sigmoid(pre)
-        act_s[pl.ds(start, size), :] = (pre * s).T.astype(BF)
-        slope_s[:, pl.ds(start, size)] = s * (1.0 + pre * (1.0 - s))
+        act_s[span, :] = (pre * s).T.astype(BF)
+        slope_s[n] = s * (1.0 + pre * (1.0 - s))
+        return carry
+
+    lax.fori_loop(0, hidden // HB, block, 0)
     outs = [
         pltpu.make_async_copy(act_s, act_o, osems.at[0]),
         pltpu.make_async_copy(slope_s, slope_o, osems.at[1]),
@@ -327,13 +350,13 @@
         pre_body,
         in_specs=[ANY, ANY],
         out_specs=[ANY] * 2,
-        out_shape=[sds((hidden, rows), BF), sds((rows, hidden), F32)],
+        out_shape=[sds((hidden, rows), BF), sds((hidden // HB, rows, HB), F32)],
         scratch_shapes=[
             pltpu.VMEM((groups, 8, width), BF),
             pltpu.VMEM((hidden, width), BF),
             pltpu.VMEM((hidden, rows), BF),
-            pltpu.VMEM((rows, hidden), F32),
-            pltpu.SemaphoreType.DMA((1 + len(blocks(hidden, 512)),)),
+            pltpu.VMEM((hidden // HB, rows, HB), F32),
+            pltpu.SemaphoreType.DMA((2,)),
             pltpu.SemaphoreType.DMA((2,)),
         ],
         compiler_params=pltpu.CompilerParams(vmem_limit_bytes=VLIMIT),
@@ -342,7 +365,7 @@
     )(x, wup)
 
 
-def grad_body(zl_ref, slab, slope, wup, wdn, ret_o, gp_o, dy_o, got, rem, dy3, wu, wd, slope_s, gp_s, gpt_s, ret, rest, sems, osems):
+def grad_body(zl_ref, slab, slope, wup, wdn, ret_o, gp_o, gpa_o, gpb_o, dy_o, got, rem, dy3, wu, wd, slope_s, gp_n, gp_s, gpt_s, ret, rest, sems, osems):
     plane = slab.shape[0]
     peers = plane * 2
     main = peers * 8
@@ -364,14 +387,28 @@
     outs[0].start()
     for copy in more[:2]:
         copy.wait()
-    for start, size in blocks(hidden, 512):
-        grad = dot_nt(dy3[...].reshape(rows, width), wd[pl.ds(start, size), :])
-        value = (grad * slope_s[:, pl.ds(start, size)]).astype(BF)
-        gp_s[:, pl.ds(start, size)] = value
-        gpt_s[pl.ds(start, size), :] = value.T
-    copy = pltpu.make_async_copy(gpt_s, gp_o, osems.at[1])
-    copy.start()
-    outs.append(copy)
+
+    def block(n, carry):
+        span = pl.ds(pl.multiple_of(n * HB, HB), HB)
+        grad = dot_nt(dy3[...].reshape(rows, width), wd[span, :])
+        value = (grad * slope_s[n]).astype(BF)
+        gp_n[n] = value
+        gpt_s[span, :] = value.T
+        return carry
+
+    lax.fori_loop(0, hidden // HB, block, 0)
+    for n in range(hidden // HB):
+        gp_s[:, pl.ds(n * HB, HB)] = gp_n[n]
+    cut = gpa_o.shape[1]
+    for i, (src, dst) in enumerate(
+        (
+            (gpt_s.at[:, pl.ds(0, cut)], gpa_o),
+            (gpt_s.at[:, pl.ds(cut, rows - cut)], gpb_o),
+            (gpt_s, gp_o),
+        )
+    ):
+        outs.append(pltpu.make_async_copy(src, dst, osems.at[7 + i]))
+        outs[-1].start()
     more[2].wait()
     rest[...] = jnp.zeros(rest.shape, F32)
     r_j = iota((main, peers * 2), 0)
@@ -412,13 +449,14 @@
     hidden, width = wup.shape
     rows = peers * 10
     groups = rows // 8
+    cut = parts(rows)
     count = tiles(width) + tiles(QW)
     sds = jax.ShapeDtypeStruct
     return pl.pallas_call(
         grad_body,
         in_specs=[SMEM, ANY, ANY, ANY, ANY],
-        out_specs=[ANY] * 3,
-        out_shape=[sds((peers, count, 8, LANES), BF), sds((hidden, rows), BF), sds((groups, 8, width), BF)],
+        out_specs=[ANY] * 5,
+        out_shape=[sds((peers, count, 8, LANES), BF), sds((hidden, rows), BF)] + [sds((hidden, n), BF) for n in (cut, rows - cut)] + [sds((groups, 8, width), BF)],
         scratch_shapes=[
             pltpu.VMEM((peers, tiles(width), 8, LANES), BF),
             pltpu.VMEM((plane, tiles(LW), 8, LANES), BF),
@@ -426,12 +464,13 @@
             pltpu.VMEM((hidden, width), BF),
             pltpu.VMEM((hidden, width), BF),
             pltpu.VMEM(slope.shape, F32),
+            pltpu.VMEM(slope.shape, BF),
             pltpu.VMEM((rows, hidden), BF),
             pltpu.VMEM((hidden, rows), BF),
             pltpu.VMEM((peers, count, 8, LANES), BF),
             pltpu.VMEM((peers * 8, QW), F32),
             pltpu.SemaphoreType.DMA((8,)),
-            pltpu.SemaphoreType.DMA((7,)),
+            pltpu.SemaphoreType.DMA((10,)),
         ],
         compiler_params=pltpu.CompilerParams(vmem_limit_bytes=VLIMIT),
         cost_estimate=pl.CostEstimate(flops=4 * rows * hidden * width, transcendentals=0, bytes_accessed=40_000_000),
@@ -469,9 +508,10 @@
     )(zl, slab)
 
 
-def combine_body(rank_ref, ret_ref, out_ref, got, sems):
+def combine_body(rank_ref, ret_ref, out_o, got, out_ref, sems, osems):
     rows, tokens = rank_ref.shape
     width = out_ref.shape[0]
+    outs = []
     spans = [(tiles(width), tiles(QW))] + [(start // LANES, tiles(size)) for start, size in blocks(width, QW)]
     copies = [
         pltpu.make_async_copy(ret_ref.at[:, pl.ds(c, n)], got.at[:, pl.ds(c, n)], sems.at[i])
@@ -491,6 +531,10 @@
         value = dot_tn(main, from_tiles(got, *spans[1 + q]))[:, :size]
         value = value + rem[q * tokens : (q + 1) * tokens, :size]
         out_ref[pl.ds(start, size), :] = value.T.astype(BF)
+        outs.append(pltpu.make_async_copy(out_ref.at[pl.ds(start, size)], out_o.at[pl.ds(start, size)], osems.at[q]))
+        outs[-1].start()
+    for copy in outs:
+        copy.wait()
 
 
 def combine(rank, ret, width):
@@ -498,9 +542,14 @@
     return pl.pallas_call(
         combine_body,
         in_specs=[vmem, ANY],
-        out_specs=vmem,
+        out_specs=ANY,
         out_shape=jax.ShapeDtypeStruct((width, rank.shape[1]), BF),
-        scratch_shapes=[pltpu.VMEM(ret.shape, BF), pltpu.SemaphoreType.DMA((5,))],
+        scratch_shapes=[
+            pltpu.VMEM(ret.shape, BF),
+            pltpu.VMEM((width, rank.shape[1]), BF),
+            pltpu.SemaphoreType.DMA((5,)),
+            pltpu.SemaphoreType.DMA((4,)),
+        ],
         compiler_params=pltpu.CompilerParams(vmem_limit_bytes=VLIMIT),
         name="combine",
     )(rank, ret)
@@ -544,15 +593,19 @@
     act_keep = lax.dynamic_slice_in_dim(act, dp * (act.shape[0] // 2), act.shape[0] // 2, 0)
     act_send = lax.dynamic_slice_in_dim(act, (1 - dp) * (act.shape[0] // 2), act.shape[0] // 2, 0)
     act_other = move(act_send, 1, 0)
-    ret, gp, dyr = expert_grad(zl[None], got_dy, slope, wup, wdn)
-    gp_other = move(gp, 1, 0)
+    ret, gp, gpa, gpb, dyr = expert_grad(zl[None], got_dy, slope, wup, wdn)
+    gpa_other = move(gpa, 1, 0)
+    gpb_other = move(gpb, 1, 0)
     back = lax.all_to_all(ret, GROUP, 0, 0, tiled=True)
     dy_other = unpack_other(zl[None], got_other, width)
 
     flat = lambda a: a.reshape(-1, a.shape[-1])
     up = lambda a, b: lax.dot_general(a, b, (((0,), (1,)), ((), ())), preferred_element_type=F32)
     grad_down = (dot_nn(act_keep, flat(dyr)) + dot_nn(act_other, flat(dy_other))).astype(BF)[None]
-    grad_up = (up(flat(xh_other), gp_other) + up(flat(xh), gp)).astype(BF)[None]
+    cut = gpa.shape[1]
+    xo = flat(xh_other)
+    early = up(xo[:cut], gpa_other) + up(flat(xh), gp)
+    grad_up = (up(xo[cut:], gpb_other) + early).astype(BF)[None]
     grad_input = combine(rank, back, width).T
     return grad_input, grad_up, grad_down
 

time: 364 us -> 355 us (0.975); the launches traced: 357 us -> 354 us
  waiting for transfers between devices: 209 us -> 198 us
  matrix products: 28.9 us -> 34.5 us
    ppermute x9 -> x10, waiting for transfers between devices: 202 us -> 193 us  [move(): return lax.ppermute(value, ALL, pairs)]
    dot_general x2 -> x3, matrix products: 14.2 us -> 18.3 us  [local(): lax.dot_general(a, b, (((0,), (1,)), ((), ())), preferred_element_type=F32)]
    ppermute x9 -> x10, starting transfers between devices: 14.1 us -> 14.1 us  [move(): return lax.ppermute(value, ALL, pairs)]
  transfers between devices with their start and end apart: 13 -> 14, of which waited for: 7 -> 8; matrix products, arithmetic and copies ran while one was open for 8% -> 10% of each run, Pallas kernels for 16% -> 17%
where the time goes in v4:
time: 355 us; the launch traced here: 354 us
  waiting for transfers between devices  198 us (56%)
  Pallas kernels  68.7 us (19%)
  starting transfers between devices  48.1 us (14%)
  matrix products  34.5 us (10%)
  local copies, waits for them, and re-layouts  3.62 us (1%)
    ppermute x10, waiting for transfers between devices, move(): return lax.ppermute(value, ALL, pairs)  193 us
    pallas_call x1, Pallas kernels, expert_grad(): pl.pallas_call(grad_body, in_specs=[SMEM, ANY, ANY, ANY, ANY], out_specs=...  24.3 us
    dot_general x3, matrix products, local(): lax.dot_general(a, b, (((0,), (1,)), ((), ())), preferred_element_type=F32)  18.3 us
    dot_general x2, matrix products, dot_nn(): lax.dot_general(left, right, (((1,), (0,)), ((), ())), preferred_element_...  16.2 us
    pallas_call x1, Pallas kernels, expert_pre(): pl.pallas_call(pre_body, in_specs=[ANY, ANY], out_specs=[ANY] * 2, out_sh...  14.7 us
    ppermute x10, starting transfers between devices, move(): return lax.ppermute(value, ALL, pairs)  14.1 us
    all_to_all x1, starting transfers between devices, local(): got_x = lax.all_to_all(slab, GROUP, 0, 0, tiled=True)  10.6 us
    pallas_call x2, Pallas kernels, pack_dy(): pl.pallas_call(pack_dy_body, in_specs=[SMEM, ANY, ANY, ANY, ANY], out_spe...  9.13 us
  transfers between devices with their start and end apart: 14, of which 8 were waited for; matrix products, arithmetic and copies ran while one was open for 10% of the time, Pallas kernels for 17%

profile of v4, /device:TPU:1, one launch (start us, length us, event | category | flops | bytes accessed | tf_op | source)
XLA Modules:
  0.0 354.1 jit_solution(5545223203734298553)
XLA Ops:
  0.6 4.5 %pack_x.1 = (bf16[64,29,8,128]{3,2,1,0:T(8,128)(2,1)}, f32[512,128]{1,0:T(8,128)}, f32[8,128]{1,0:T(8,128)}) custom-call(s32[4,128]{1,0:T(4,128)} %bitcast.42, f32[4,128]{1,0:T(4,128)} %bitcast.43, bf16[2880,128]{1,0:T(8,128)(2,1)} %bitcast.37), custom_call_target="tpu_custom_call" | custom-call | tf_op jit(solution)/shard_map/pack_x/pallas_call | solution.py:128
  5.2 0.0 copy-start
  5.2 10.6 %all-to-all-start.1 = ((bf16[64,29,8,128]{3,2,1,0:T(8,128)(2,1)}), bf16[64,29,8,128]{3,2,1,0:T(8,128)(2,1)}, u32[]{:S(2)}, u32[]{:S(2)}) async-start(bf16[64,29,8,128]{3,2,1,0:T(8,128)(2,1)} %get-tuple-element.18), calls=%async_computation.1 | async-start | bytes 7602176 | tf_op jit(solution)/shard_map/all_to_all | solution.py:584
  15.9 1.5 collective-permute-start
  17.4 0.1 collective-permute-start.1
  17.5 57.7 %collective-permute-done.1.mb_ref = f32[8,128]{1,0:T(8,128)S(1)} collective-permute-done((f32[8,128]{1,0:T(8,128)S(1)}, f32[8,128]{1,0:T(8,128)S(1)}, u32[]{:S(2)}, u32[]{:S(2)}) %collective-permute-start.1) | collective-permute-done | bytes 4128 | tf_op jit(solution)/shard_map/ppermute | solution.py:576
  75.2 0.0 collective-permute-done.pb_ref
  75.2 0.6 copy-done.10
  75.8 0.3 copy-done.4
  76.1 4.5 %shard_map.85 = bf16[32,58,8,128]{3,2,1,0:T(8,128)(2,1)} custom-call(s32[1]{0:T(128)} %bitcast.3.zl_ref, bf16[2880,128]{1,0:T(8,128)(2,1)} %bitcast.38, bf16[2880,128]{1,0:T(8,128)(2,1)} %copy-done.4, f32[8,128]{1,0:T(8,128)} %get-tuple-element.17.ma_ref, f32[8,128]{1,0:T(8,128)} %copy-done.10), custom_call_target="tpu_custom_call" | custom-call | tf_op jit(solution)/shard_map/pallas_call | solution.py:203
  80.6 0.0 copy-start.1
  80.7 0.0 all-to-all-done.1.slab
  80.7 7.6 %all-to-all-start = ((bf16[32,58,8,128]{3,2,1,0:T(8,128)(2,1)}), bf16[32,58,8,128]{3,2,1,0:T(8,128)(2,1)}, u32[]{:S(2)}, u32[]{:S(2)}) async-start(bf16[32,58,8,128]{3,2,1,0:T(8,128)(2,1)} %shard_map.85), calls=%async_computation | async-start | bytes 7602176 | tf_op jit(solution)/shard_map/all_to_all | solution.py:586
  88.3 3.4 collective-permute-start.6
  91.7 1.2 collective-permute-start.8
  92.9 1.4 collective-permute-start.9
  94.4 14.1 %collective-permute-done.8.ma_ref = f32[8,128]{1,0:T(8,128)S(1)} collective-permute-done((f32[8,128]{1,0:T(8,128)S(1)}, f32[8,128]{1,0:T(8,128)S(1)}, u32[]{:S(2)}, u32[]{:S(2)}) %collective-permute-start.8) | collective-permute-done | bytes 4128 | tf_op jit(solution)/shard_map/ppermute | solution.py:576
  108.5 16.2 %collective-permute-done.9.mb_ref = f32[8,128]{1,0:T(8,128)S(1)} collective-permute-done((f32[8,128]{1,0:T(8,128)S(1)}, f32[8,128]{1,0:T(8,128)S(1)}, u32[]{:S(2)}, u32[]{:S(2)}) %collective-permute-start.9) | collective-permute-done | bytes 4128 | tf_op jit(solution)/shard_map/ppermute | solution.py:576
  124.7 0.0 collective-permute-done.6.pa_ref
  124.8 0.6 copy-done.9
  125.3 0.3 copy-done.2
  125.6 0.9 copy-done.3
  126.5 4.6 %shard_map.86 = bf16[32,58,8,128]{3,2,1,0:T(8,128)(2,1)} custom-call(s32[1]{0:T(128)} %bitcast.3.zl_ref, bf16[2880,128]{1,0:T(8,128)(2,1)} %copy-done.2, bf16[2880,128]{1,0:T(8,128)(2,1)} %copy-done.3, f32[8,128]{1,0:T(8,128)} %copy-done.8, f32[8,128]{1,0:T(8,128)} %copy-done.9), custom_call_target="tpu_custom_call" | custom-call | tf_op jit(solution)/shard_map/pallas_call | solution.py:203
  131.1 4.0 %all-to-all-done.slab = bf16[32,58,8,128]{3,2,1,0:T(8,128)(2,1)} async-done(((bf16[32,58,8,128]{3,2,1,0:T(8,128)(2,1)}), bf16[32,58,8,128]{3,2,1,0:T(8,128)(2,1)}, u32[]{:S(2)}, u32[]{:S(2)}) %all-to-all-start) | async-done | bytes 3801120 | tf_op jit(solution)/shard_map/all_to_all | solution.py:586
  135.1 7.4 %all-to-all-start.3 = ((bf16[32,58,8,128]{3,2,1,0:T(8,128)(2,1)}), bf16[32,58,8,128]{3,2,1,0:T(8,128)(2,1)}, u32[]{:S(2)}, u32[]{:S(2)}) async-start(bf16[32,58,8,128]{3,2,1,0:T(8,128)(2,1)} %shard_map.86), calls=%async_computation.3 | async-start | bytes 7602176 | tf_op jit(solution)/shard_map/all_to_all | solution.py:588
  142.5 6.6 %split_x.1 = (bf16[80,8,2880]{2,1,0:T(8,128)(2,1)}, bf16[80,8,1440]{2,1,0:T(8,128)(2,1)}, bf16[80,8,1440]{2,1,0:T(8,128)(2,1)}) custom-call(s32[1]{0:T(128)} %bitcast.5.dp_ref, bf16[64,29,8,128]{3,2,1,0:T(8,128)(2,1)} %all-to-all-done.1.slab), custom_call_target="tpu_custom_call" | custom-call | tf_op jit(solution)/shard_map/split_x/pallas_call | solution.py:297
  149.1 14.7 %expert_pre.1 = (bf16[1440,640]{1,0:T(8,128)(2,1)}, f32[3,640,480]{2,1,0:T(8,128)}) custom-call(bf16[80,8,2880]{2,1,0:T(8,128)(2,1)} %get-tuple-element.19.x, bf16[1440,2880]{1,0:T(8,128)(2,1)} %bitcast.44), custom_call_target="tpu_custom_call" | custom-call | flops 5308416000 | bytes 20000000 | tf_op jit(solution)/shard_map/expert_pre/pallas_call | solution.py:349
  163.8 24.3 %expert_grad.1 = (bf16[64,29,8,128]{3,2,1,0:T(8,128)(2,1)}, bf16[1440,640]{1,0:T(8,128)(2,1)}, bf16[1440,384]{1,0:T(8,128)(2,1)}, bf16[1440,256]{1,0:T(8,128)(2,1)}, bf16[80,8,2880]{2,1,0:T(8,128)(2,1)}) custom-call(s32[1]{0:T(128)} %bitcast.3.zl_ref, bf16[32,58,8,128]{3,2,1,0:T(8,128)(2,1)} %all-to-all-done.slab, f32[3,640,480]{2,1,0:T(8,128)} %get-tuple-element.20.slope, ...), custom_call_target="tpu_custom_call" | custom-call | flops 10616832000 | bytes 40000000 | tf_op jit(solution)/shard_map/expert_grad/pallas_call | solution.py:455
  188.1 0.9 all-to-all-done.3.slab
  189.0 8.4 %all-to-all-start.2 = ((bf16[64,29,8,128]{3,2,1,0:T(8,128)(2,1)}), bf16[64,29,8,128]{3,2,1,0:T(8,128)(2,1)}, u32[]{:S(2)}, u32[]{:S(2)}) async-start(bf16[64,29,8,128]{3,2,1,0:T(8,128)(2,1)} %get-tuple-element.21), calls=%async_computation.2 | async-start | bytes 7602176 | tf_op jit(solution)/shard_map/all_to_all | solution.py:599
  197.4 3.4 collective-permute-start.2
  200.7 1.0 constant_dynamic-slice_fusion
  201.7 0.0 collective-permute-start.5
  201.8 2.9 collective-permute-start.4
  204.7 0.0 collective-permute-start.3
  204.7 9.4 %fusion.6 = f32[1440,1440]{1,0:T(8,128)} fusion(bf16[1440,640]{1,0:T(8,128)(2,1)} %get-tuple-element.26, bf16[80,8,1440]{2,1,0:T(8,128)(2,1)} %get-tuple-element.25), kind=kOutput, calls=%fused_computation.9 | convolution fusion | flops 2654208000 | bytes 11980800 | tf_op jit(solution)/shard_map/dot_general | solution.py:603
  214.2 5.7 %fusion.4 = f32[720,2880]{1,0:T(8,128)} fusion(bf16[80,8,2880]{2,1,0:T(8,128)(2,1)S(1)} %copy-done.11, bf16[1440,640]{1,0:T(8,128)(2,1)S(1)} %copy-done.5, s32[]{:T(128)S(6)} %select_n.6), kind=kOutput, calls=%fused_computation.7 | convolution fusion | flops 2654208000 | bytes 12984324 | tf_op jit(solution)/shard_map/dot_general | solution.py:34
  219.9 4.5 %unpack_other.1 = bf16[80,8,2880]{2,1,0:T(8,128)(2,1)} custom-call(s32[1]{0:T(128)} %bitcast.3.zl_ref, bf16[32,58,8,128]{3,2,1,0:T(8,128)(2,1)} %all-to-all-done.3.slab), custom_call_target="tpu_custom_call" | custom-call | tf_op jit(solution)/shard_map/unpack_other/pallas_call | solution.py:495
  224.4 0.0 slice-start.1
  224.4 0.0 slice-start.2
  224.5 80.1 %collective-permute-done.5 = bf16[720,640]{1,0:T(8,128)(2,1)} collective-permute-done((bf16[720,640]{1,0:T(8,128)(2,1)}, bf16[720,640]{1,0:T(8,128)(2,1)}, u32[]{:S(2)}, u32[]{:S(2)}) %collective-permute-start.5) | collective-permute-done | bytes 921632 | tf_op jit(solution)/shard_map/ppermute | solution.py:576
  304.6 10.5 %fusion.2 = bf16[1,720,2880]{2,1,0:T(8,128)(2,1)} fusion(f32[720,2880]{1,0:T(8,128)} %fusion.4, bf16[720,640]{1,0:T(8,128)(2,1)} %collective-permute-done.5, bf16[80,8,2880]{2,1,0:T(8,128)(2,1)} %unpack_other.1), kind=kOutput, calls=%fused_computation.5 | convolution fusion | flops 2658355200 | bytes 17049600 | tf_op jit(solution)/shard_map/dot_general | solution.py:34
  315.0 13.1 %collective-permute-done.4 = bf16[1440,384]{1,0:T(8,128)(2,1)S(1)} collective-permute-done((bf16[1440,384]{1,0:T(8,128)(2,1)}, bf16[1440,384]{1,0:T(8,128)(2,1)S(1)}, u32[]{:S(2)}, u32[]{:S(2)}) %collective-permute-start.4) | collective-permute-done | bytes 1105952 | tf_op jit(solution)/shard_map/ppermute | solution.py:576
  328.2 3.9 %convolution_add_fusion = f32[1440,1440]{1,0:T(8,128)S(1)} fusion(f32[1440,1440]{1,0:T(8,128)S(1)} %bitcast.35, bf16[1440,384]{1,0:T(8,128)(2,1)S(1)} %collective-permute-done.4, bf16[80,8,1440]{2,1,0:T(8,128)(2,1)} %collective-permute-done.2), kind=kOutput, calls=%fused_computation | convolution fusion | flops 1594598400 | bytes 18874368 | tf_op jit(solution)/shard_map/dot_general | solution.py:603
  332.1 12.0 %collective-permute-done.3 = bf16[1440,256]{1,0:T(8,128)(2,1)} collective-permute-done((bf16[1440,256]{1,0:T(8,128)(2,1)}, bf16[1440,256]{1,0:T(8,128)(2,1)}, u32[]{:S(2)}, u32[]{:S(2)}) %collective-permute-start.3) | collective-permute-done | bytes 737312 | tf_op jit(solution)/shard_map/ppermute | solution.py:576
  344.1 5.0 %fusion.1 = bf16[1,1440,1440]{2,1,0:T(8,128)(2,1)} fusion(f32[1440,1440]{1,0:T(8,128)S(1)} %convolution_add_fusion, bf16[1440,256]{1,0:T(8,128)(2,1)} %collective-permute-done.3, bf16[80,8,1440]{2,1,0:T(8,128)(2,1)} %collective-permute-done.2), kind=kOutput, calls=%fused_computation.4 | convolution fusion | flops 1065830400 | bytes 13965312 | tf_op jit(solution)/shard_map/dot_general | solution.py:603
  349.1 0.0 all-to-all-done.2.ret_ref
  349.1 4.9 %combine.1 = bf16[2880,128]{1,0:T(8,128)(2,1)} custom-call(f32[512,128]{1,0:T(8,128)} %get-tuple-element.16.rank_ref, bf16[64,29,8,128]{3,2,1,0:T(8,128)(2,1)} %all-to-all-done.2.ret_ref), custom_call_target="tpu_custom_call" | custom-call | tf_op jit(solution)/shard_map/combine/pallas_call | solution.py:542
  (25 shorter events, 0.0 us)
Async XLA Ops:
  5.2 10.7 %copy-start = (bf16[128,2880]{0,1:T(8,128)(2,1)S(1)}, bf16[128,2880]{0,1:T(8,128)(2,1)}, u32[]{:S(2)}) copy-start(bf16[128,2880]{0,1:T(8,128)(2,1)} %param.7) | copy-start | bytes 2211844
  5.2 12.2 %copy-start.6 = (f32[8,128]{1,0:T(8,128)S(1)}, f32[8,128]{1,0:T(8,128)}, u32[]{:S(2)}) copy-start(f32[8,128]{1,0:T(8,128)} %get-tuple-element.17.ma_ref) | copy-start | bytes 12292
  5.2 75.5 %all-to-all-start.1 = ((bf16[64,29,8,128]{3,2,1,0:T(8,128)(2,1)}), bf16[64,29,8,128]{3,2,1,0:T(8,128)(2,1)}, u32[]{:S(2)}, u32[]{:S(2)}) async-start(bf16[64,29,8,128]{3,2,1,0:T(8,128)(2,1)} %get-tuple-element.18), calls=%async_computation.1 | async-start | bytes 7602176 | tf_op jit(solution)/shard_map/all_to_all | solution.py:584
  15.9 59.4 %collective-permute-start = (bf16[2880,128]{1,0:T(8,128)(2,1)S(1)}, bf16[2880,128]{1,0:T(8,128)(2,1)S(1)}, u32[]{:S(2)}, u32[]{:S(2)}) collective-permute-start(bf16[2880,128]{1,0:T(8,128)(2,1)S(1)} %bitcast.39), channel_id=1, source_target_pairs={{0,32},{1,33},{2,34},{3,35},{4,36},{5,37},{6,38},{7,39},{8,40},{9,... | collective-permute-start | bytes 2211848 | tf_op jit(solution)/shard_map/ppermute | solution.py:576
  17.4 57.8 %collective-permute-start.1 = (f32[8,128]{1,0:T(8,128)S(1)}, f32[8,128]{1,0:T(8,128)S(1)}, u32[]{:S(2)}, u32[]{:S(2)}) collective-permute-start(f32[8,128]{1,0:T(8,128)S(1)} %copy-done.6), channel_id=1, source_target_pairs={{0,32},{1,33},{2,34},{3,35},{4,36},{5,37},{6,38},{7,39},{8,40},{9,... | collective-permute-start | bytes 12296 | tf_op jit(solution)/shard_map/ppermute | solution.py:576
  75.2 0.6 copy-start.10
  75.2 0.9 copy-start.4
  80.6 7.7 %copy-start.1 = (bf16[128,2880]{0,1:T(8,128)(2,1)S(1)}, bf16[128,2880]{0,1:T(8,128)(2,1)}, u32[]{:S(2)}) copy-start(bf16[128,2880]{0,1:T(8,128)(2,1)} %param.7) | copy-start | bytes 2211844
  80.7 11.1 %copy-start.7 = (f32[8,128]{1,0:T(8,128)S(1)}, f32[8,128]{1,0:T(8,128)}, u32[]{:S(2)}) copy-start(f32[8,128]{1,0:T(8,128)} %get-tuple-element.17.ma_ref) | copy-start | bytes 12292
  80.7 54.4 %all-to-all-start = ((bf16[32,58,8,128]{3,2,1,0:T(8,128)(2,1)}), bf16[32,58,8,128]{3,2,1,0:T(8,128)(2,1)}, u32[]{:S(2)}, u32[]{:S(2)}) async-start(bf16[32,58,8,128]{3,2,1,0:T(8,128)(2,1)} %shard_map.85), calls=%async_computation | async-start | bytes 7602176 | tf_op jit(solution)/shard_map/all_to_all | solution.py:586
  88.3 36.4 %collective-permute-start.6 = (bf16[2880,128]{1,0:T(8,128)(2,1)S(1)}, bf16[2880,128]{1,0:T(8,128)(2,1)S(1)}, u32[]{:S(2)}, u32[]{:S(2)}) collective-permute-start(bf16[2880,128]{1,0:T(8,128)(2,1)S(1)} %bitcast.40), channel_id=1, source_target_pairs={{0,64},{1,65},{2,66},{3,67},{4,68},{5,69},{6,70},{7,71},{8,72},{9,... | collective-permute-start | bytes 2211848 | tf_op jit(solution)/shard_map/ppermute | solution.py:576
  91.7 33.0 %collective-permute-start.7 = (bf16[2880,128]{1,0:T(8,128)(2,1)S(1)}, bf16[2880,128]{1,0:T(8,128)(2,1)S(1)}, u32[]{:S(2)}, u32[]{:S(2)}) collective-permute-start(bf16[2880,128]{1,0:T(8,128)(2,1)S(1)} %bitcast.41), channel_id=1, source_target_pairs={{0,96},{1,97},{2,98},{3,99},{4,100},{5,101},{6,102},{7,103},{8,104... | collective-permute-start | bytes 2211848 | tf_op jit(solution)/shard_map/ppermute | solution.py:576
  91.7 16.8 %collective-permute-start.8 = (f32[8,128]{1,0:T(8,128)S(1)}, f32[8,128]{1,0:T(8,128)S(1)}, u32[]{:S(2)}, u32[]{:S(2)}) collective-permute-start(f32[8,128]{1,0:T(8,128)S(1)} %copy-done.7), channel_id=1, source_target_pairs={{0,64},{1,65},{2,66},{3,67},{4,68},{5,69},{6,70},{7,71},{8,72},{9,... | collective-permute-start | bytes 12296 | tf_op jit(solution)/shard_map/ppermute | solution.py:576
  92.9 31.8 %collective-permute-start.9 = (f32[8,128]{1,0:T(8,128)S(1)}, f32[8,128]{1,0:T(8,128)S(1)}, u32[]{:S(2)}, u32[]{:S(2)}) collective-permute-start(f32[8,128]{1,0:T(8,128)S(1)} %copy-done.7), channel_id=1, source_target_pairs={{0,96},{1,97},{2,98},{3,99},{4,100},{5,101},{6,102},{7,103},{8,104... | collective-permute-start | bytes 12296 | tf_op jit(solution)/shard_map/ppermute | solution.py:576
  108.5 16.2 %copy-start.8 = (f32[8,128]{1,0:T(8,128)}, f32[8,128]{1,0:T(8,128)S(1)}, u32[]{:S(2)}) copy-start(f32[8,128]{1,0:T(8,128)S(1)} %collective-permute-done.8.ma_ref) | copy-start | bytes 12292
  124.7 0.6 copy-start.9
  124.7 0.9 copy-start.2
  125.6 0.9 copy-start.3
  135.1 53.9 %all-to-all-start.3 = ((bf16[32,58,8,128]{3,2,1,0:T(8,128)(2,1)}), bf16[32,58,8,128]{3,2,1,0:T(8,128)(2,1)}, u32[]{:S(2)}, u32[]{:S(2)}) async-start(bf16[32,58,8,128]{3,2,1,0:T(8,128)(2,1)} %shard_map.86), calls=%async_computation.3 | async-start | bytes 7602176 | tf_op jit(solution)/shard_map/all_to_all | solution.py:588
  188.9 11.8 %copy-start.5 = (bf16[1440,640]{1,0:T(8,128)(2,1)S(1)}, bf16[1440,640]{1,0:T(8,128)(2,1)}, u32[]{:S(2)}) copy-start(bf16[1440,640]{1,0:T(8,128)(2,1)} %get-tuple-element.27) | copy-start | bytes 5529604
  189.0 160.1 %all-to-all-start.2 = ((bf16[64,29,8,128]{3,2,1,0:T(8,128)(2,1)}), bf16[64,29,8,128]{3,2,1,0:T(8,128)(2,1)}, u32[]{:S(2)}, u32[]{:S(2)}) async-start(bf16[64,29,8,128]{3,2,1,0:T(8,128)(2,1)} %get-tuple-element.21), calls=%async_computation.2 | async-start | bytes 7602176 | tf_op jit(solution)/shard_map/all_to_all | solution.py:599
  197.4 130.8 %collective-permute-start.2 = (bf16[80,8,1440]{2,1,0:T(8,128)(2,1)}, bf16[80,8,1440]{2,1,0:T(8,128)(2,1)}, u32[]{:S(2)}, u32[]{:S(2)}) collective-permute-start(bf16[80,8,1440]{2,1,0:T(8,128)(2,1)} %get-tuple-element.22), channel_id=1, source_target_pairs={{0,64},{1,65},{2,66},{3,67},{4,68},{5,69},{6,70},{7,71},{8,72},{9,... | collective-permute-start | bytes 5529608 | tf_op jit(solution)/shard_map/ppermute | solution.py:576
  201.7 102.8 %collective-permute-start.5 = (bf16[720,640]{1,0:T(8,128)(2,1)}, bf16[720,640]{1,0:T(8,128)(2,1)}, u32[]{:S(2)}, u32[]{:S(2)}) collective-permute-start(bf16[720,640]{1,0:T(8,128)(2,1)} %constant_dynamic-slice_fusion), channel_id=1, source_target_pairs={{0,64},{1,65},{2,66},{3,67},{4,68},{5,69},{6,70},{7,71},{8,72},{9,... | collective-permute-start | bytes 2764808 | tf_op jit(solution)/shard_map/ppermute | solution.py:576
  201.8 126.4 %collective-permute-start.4 = (bf16[1440,384]{1,0:T(8,128)(2,1)}, bf16[1440,384]{1,0:T(8,128)(2,1)S(1)}, u32[]{:S(2)}, u32[]{:S(2)}) collective-permute-start(bf16[1440,384]{1,0:T(8,128)(2,1)} %get-tuple-element.24), channel_id=1, source_target_pairs={{0,64},{1,65},{2,66},{3,67},{4,68},{5,69},{6,70},{7,71},{8,72},{9,... | collective-permute-start | bytes 3317768 | tf_op jit(solution)/shard_map/ppermute | solution.py:576
  204.7 139.3 %collective-permute-start.3 = (bf16[1440,256]{1,0:T(8,128)(2,1)}, bf16[1440,256]{1,0:T(8,128)(2,1)}, u32[]{:S(2)}, u32[]{:S(2)}) collective-permute-start(bf16[1440,256]{1,0:T(8,128)(2,1)} %get-tuple-element.23), channel_id=1, source_target_pairs={{0,64},{1,65},{2,66},{3,67},{4,68},{5,69},{6,70},{7,71},{8,72},{9,... | collective-permute-start | bytes 2211848 | tf_op jit(solution)/shard_map/ppermute | solution.py:576
  204.7 9.4 %copy-start.11 = (bf16[80,8,2880]{2,1,0:T(8,128)(2,1)S(1)}, bf16[80,8,2880]{2,1,0:T(8,128)(2,1)}, u32[]{:S(2)}) copy-start(bf16[80,8,2880]{2,1,0:T(8,128)(2,1)} %get-tuple-element.28) | copy-start | bytes 11059204
  219.9 108.3 %slice-start = ((s8[8847360]{0:T(1024)(128)(4,1)}), s8[458752]{0:T(1024)(128)(4,1)S(1)}, s32[]{:S(2)}) async-start(s8[8847360]{0:T(1024)(128)(4,1)} %bitcast.34), calls=%async_computation.4 | async-start | bytes 917504
  224.4 103.7 %slice-start.1 = ((s8[8847360]{0:T(1024)(128)(4,1)}), s8[4194304]{0:T(1024)(128)(4,1)S(1)}, s32[]{:S(2)}) async-start(s8[8847360]{0:T(1024)(128)(4,1)} %bitcast.34), calls=%async_computation.5 | async-start | bytes 8388608
  224.4 103.7 %slice-start.2 = ((s8[8847360]{0:T(1024)(128)(4,1)}), s8[4194304]{0:T(1024)(128)(4,1)S(1)}, s32[]{:S(2)}) async-start(s8[8847360]{0:T(1024)(128)(4,1)} %bitcast.34), calls=%async_computation.6 | async-start | bytes 8388608

commit v5 on v4

--- a/solution.py
+++ b/solution.py
@@ -277,7 +277,8 @@
     first = dp_ref[0] == 0
     x0 = x3[:, :, pl.ds(0, width // 2)]
     x1 = x3[:, :, pl.ds(width // 2, width // 2)]
-    xs_s[...] = jnp.where(first, x1, x0)
+    send = jnp.where(first, x1, x0)
+    xs_s[...] = send.reshape(main + peers * 2, width // 2).T
     outs = [pltpu.make_async_copy(xs_s, xs_o, osems.at[0])]
     outs[0].start()
     outs.append(pltpu.make_async_copy(x3, x_o, osems.at[1]))
@@ -298,12 +299,12 @@
         split_body,
         in_specs=[SMEM, ANY],
         out_specs=[ANY] * 3,
-        out_shape=[sds((groups, 8, width), BF), sds(half, BF), sds(half, BF)],
+        out_shape=[sds((groups, 8, width), BF), sds(half, BF), sds((width // 2, groups * 8), BF)],
         scratch_shapes=[
             pltpu.VMEM(slab.shape, BF),
             pltpu.VMEM((groups, 8, width), BF),
             pltpu.VMEM(half, BF),
-            pltpu.VMEM(half, BF),
+            pltpu.VMEM((width // 2, groups * 8), BF),
             pltpu.SemaphoreType.DMA((1,)),
             pltpu.SemaphoreType.DMA((3,)),
         ],
@@ -603,9 +604,8 @@
     up = lambda a, b: lax.dot_general(a, b, (((0,), (1,)), ((), ())), preferred_element_type=F32)
     grad_down = (dot_nn(act_keep, flat(dyr)) + dot_nn(act_other, flat(dy_other))).astype(BF)[None]
     cut = gpa.shape[1]
-    xo = flat(xh_other)
-    early = up(xo[:cut], gpa_other) + up(flat(xh), gp)
-    grad_up = (up(xo[cut:], gpb_other) + early).astype(BF)[None]
+    early = dot_nt(xh_other[:, :cut], gpa_other) + up(flat(xh), gp)
+    grad_up = (dot_nt(xh_other[:, cut:], gpb_other) + early).astype(BF)[None]
     grad_input = combine(rank, back, width).T
     return grad_input, grad_up, grad_down
 

time: 355 us -> 352 us (level)
    dot_general x3 -> x1, matrix products: 18.3 us -> 9.43 us  [local(): lax.dot_general(a, b, (((0,), (1,)), ((), ())), preferred_element_type=F32)]
    dot_general x0 -> x2, matrix products: none -> 8.67 us  [dot_nt(): lax.dot_general(left, right, (((1,), (1,)), ((), ())), preferred_element_...]
where the time goes in v5:
time: 352 us; the launch traced here: 351 us
  waiting for transfers between devices  195 us (55%)
  Pallas kernels  69.2 us (20%)
  starting transfers between devices  48.1 us (14%)
  matrix products  34.3 us (10%)
  local copies, waits for them, and re-layouts  3.62 us (1%)
    ppermute x10, waiting for transfers between devices, move(): return lax.ppermute(value, ALL, pairs)  191 us
    pallas_call x1, Pallas kernels, expert_grad(): pl.pallas_call(grad_body, in_specs=[SMEM, ANY, ANY, ANY, ANY], out_specs=...  24.3 us
    dot_general x2, matrix products, dot_nn(): lax.dot_general(left, right, (((1,), (0,)), ((), ())), preferred_element_...  16.2 us
    pallas_call x1, Pallas kernels, expert_pre(): pl.pallas_call(pre_body, in_specs=[ANY, ANY], out_specs=[ANY] * 2, out_sh...  14.7 us
    ppermute x10, starting transfers between devices, move(): return lax.ppermute(value, ALL, pairs)  14.1 us
    all_to_all x1, starting transfers between devices, local(): got_x = lax.all_to_all(slab, GROUP, 0, 0, tiled=True)  10.6 us
    dot_general x1, matrix products, local(): lax.dot_general(a, b, (((0,), (1,)), ((), ())), preferred_element_type=F32)  9.43 us
    pallas_call x2, Pallas kernels, pack_dy(): pl.pallas_call(pack_dy_body, in_specs=[SMEM, ANY, ANY, ANY, ANY], out_spe...  9.12 us
  transfers between devices with their start and end apart: 14, of which 8 were waited for; matrix products, arithmetic and copies ran while one was open for 10% of the time, Pallas kernels for 17%

profile of v5, /device:TPU:1, one launch (start us, length us, event | category | flops | bytes accessed | tf_op | source)
XLA Modules:
  0.0 351.3 jit_solution(3500799074003261193)
XLA Ops:
  0.6 4.5 %pack_x.1 = (bf16[64,29,8,128]{3,2,1,0:T(8,128)(2,1)}, f32[512,128]{1,0:T(8,128)}, f32[8,128]{1,0:T(8,128)}) custom-call(s32[4,128]{1,0:T(4,128)} %bitcast.36, f32[4,128]{1,0:T(4,128)} %bitcast.37, bf16[2880,128]{1,0:T(8,128)(2,1)} %bitcast.31), custom_call_target="tpu_custom_call" | custom-call | tf_op jit(solution)/shard_map/pack_x/pallas_call | solution.py:128
  5.2 0.0 copy-start
  5.2 10.6 %all-to-all-start.1 = ((bf16[64,29,8,128]{3,2,1,0:T(8,128)(2,1)}), bf16[64,29,8,128]{3,2,1,0:T(8,128)(2,1)}, u32[]{:S(2)}, u32[]{:S(2)}) async-start(bf16[64,29,8,128]{3,2,1,0:T(8,128)(2,1)} %get-tuple-element.18), calls=%async_computation.1 | async-start | bytes 7602176 | tf_op jit(solution)/shard_map/all_to_all | solution.py:585
  15.9 1.5 collective-permute-start
  17.4 0.1 collective-permute-start.1
  17.5 57.7 %collective-permute-done.1.mb_ref = f32[8,128]{1,0:T(8,128)S(1)} collective-permute-done((f32[8,128]{1,0:T(8,128)S(1)}, f32[8,128]{1,0:T(8,128)S(1)}, u32[]{:S(2)}, u32[]{:S(2)}) %collective-permute-start.1) | collective-permute-done | bytes 4128 | tf_op jit(solution)/shard_map/ppermute | solution.py:577
  75.2 0.0 collective-permute-done.pb_ref
  75.2 0.6 copy-done.10
  75.8 0.3 copy-done.4
  76.1 4.5 %shard_map.85 = bf16[32,58,8,128]{3,2,1,0:T(8,128)(2,1)} custom-call(s32[1]{0:T(128)} %bitcast.3.zl_ref, bf16[2880,128]{1,0:T(8,128)(2,1)} %bitcast.32, bf16[2880,128]{1,0:T(8,128)(2,1)} %copy-done.4, f32[8,128]{1,0:T(8,128)} %get-tuple-element.17.ma_ref, f32[8,128]{1,0:T(8,128)} %copy-done.10), custom_call_target="tpu_custom_call" | custom-call | tf_op jit(solution)/shard_map/pallas_call | solution.py:203
  80.6 0.0 copy-start.1
  80.6 0.0 all-to-all-done.1.slab
  80.7 7.6 %all-to-all-start = ((bf16[32,58,8,128]{3,2,1,0:T(8,128)(2,1)}), bf16[32,58,8,128]{3,2,1,0:T(8,128)(2,1)}, u32[]{:S(2)}, u32[]{:S(2)}) async-start(bf16[32,58,8,128]{3,2,1,0:T(8,128)(2,1)} %shard_map.85), calls=%async_computation | async-start | bytes 7602176 | tf_op jit(solution)/shard_map/all_to_all | solution.py:587
  88.3 3.4 collective-permute-start.6
  91.7 0.0 collective-permute-start.7
  91.7 1.2 collective-permute-start.8
  92.9 1.4 collective-permute-start.9
  94.4 14.1 %collective-permute-done.8.ma_ref = f32[8,128]{1,0:T(8,128)S(1)} collective-permute-done((f32[8,128]{1,0:T(8,128)S(1)}, f32[8,128]{1,0:T(8,128)S(1)}, u32[]{:S(2)}, u32[]{:S(2)}) %collective-permute-start.8) | collective-permute-done | bytes 4128 | tf_op jit(solution)/shard_map/ppermute | solution.py:577
  108.5 16.2 %collective-permute-done.9.mb_ref = f32[8,128]{1,0:T(8,128)S(1)} collective-permute-done((f32[8,128]{1,0:T(8,128)S(1)}, f32[8,128]{1,0:T(8,128)S(1)}, u32[]{:S(2)}, u32[]{:S(2)}) %collective-permute-start.9) | collective-permute-done | bytes 4128 | tf_op jit(solution)/shard_map/ppermute | solution.py:577
  124.7 0.0 collective-permute-done.6.pa_ref
  124.7 0.0 collective-permute-done.7.pb_ref
  124.7 0.6 copy-done.9
  125.3 0.3 copy-done.2
  125.6 0.9 copy-done.3
  126.5 4.6 %shard_map.86 = bf16[32,58,8,128]{3,2,1,0:T(8,128)(2,1)} custom-call(s32[1]{0:T(128)} %bitcast.3.zl_ref, bf16[2880,128]{1,0:T(8,128)(2,1)} %copy-done.2, bf16[2880,128]{1,0:T(8,128)(2,1)} %copy-done.3, f32[8,128]{1,0:T(8,128)} %copy-done.8, f32[8,128]{1,0:T(8,128)} %copy-done.9), custom_call_target="tpu_custom_call" | custom-call | tf_op jit(solution)/shard_map/pallas_call | solution.py:203
  131.0 4.0 %all-to-all-done.slab = bf16[32,58,8,128]{3,2,1,0:T(8,128)(2,1)} async-done(((bf16[32,58,8,128]{3,2,1,0:T(8,128)(2,1)}), bf16[32,58,8,128]{3,2,1,0:T(8,128)(2,1)}, u32[]{:S(2)}, u32[]{:S(2)}) %all-to-all-start) | async-done | bytes 3801120 | tf_op jit(solution)/shard_map/all_to_all | solution.py:587
  135.1 7.4 %all-to-all-start.3 = ((bf16[32,58,8,128]{3,2,1,0:T(8,128)(2,1)}), bf16[32,58,8,128]{3,2,1,0:T(8,128)(2,1)}, u32[]{:S(2)}, u32[]{:S(2)}) async-start(bf16[32,58,8,128]{3,2,1,0:T(8,128)(2,1)} %shard_map.86), calls=%async_computation.3 | async-start | bytes 7602176 | tf_op jit(solution)/shard_map/all_to_all | solution.py:589
  142.4 7.1 %split_x.1 = (bf16[80,8,2880]{2,1,0:T(8,128)(2,1)}, bf16[80,8,1440]{2,1,0:T(8,128)(2,1)}, bf16[1440,640]{1,0:T(8,128)(2,1)}) custom-call(s32[1]{0:T(128)} %bitcast.5.dp_ref, bf16[64,29,8,128]{3,2,1,0:T(8,128)(2,1)} %all-to-all-done.1.slab), custom_call_target="tpu_custom_call" | custom-call | tf_op jit(solution)/shard_map/split_x/pallas_call | solution.py:298
  149.5 14.7 %expert_pre.1 = (bf16[1440,640]{1,0:T(8,128)(2,1)}, f32[3,640,480]{2,1,0:T(8,128)}) custom-call(bf16[80,8,2880]{2,1,0:T(8,128)(2,1)} %get-tuple-element.19.x, bf16[1440,2880]{1,0:T(8,128)(2,1)} %bitcast.38), custom_call_target="tpu_custom_call" | custom-call | flops 5308416000 | bytes 20000000 | tf_op jit(solution)/shard_map/expert_pre/pallas_call | solution.py:350
  164.3 24.3 %expert_grad.1 = (bf16[64,29,8,128]{3,2,1,0:T(8,128)(2,1)}, bf16[1440,640]{1,0:T(8,128)(2,1)}, bf16[1440,384]{1,0:T(8,128)(2,1)}, bf16[1440,256]{1,0:T(8,128)(2,1)}, bf16[80,8,2880]{2,1,0:T(8,128)(2,1)}) custom-call(s32[1]{0:T(128)} %bitcast.3.zl_ref, bf16[32,58,8,128]{3,2,1,0:T(8,128)(2,1)} %all-to-all-done.slab, f32[3,640,480]{2,1,0:T(8,128)} %get-tuple-element.20.slope, ...), custom_call_target="tpu_custom_call" | custom-call | flops 10616832000 | bytes 40000000 | tf_op jit(solution)/shard_map/expert_grad/pallas_call | solution.py:456
  188.6 0.4 all-to-all-done.3.slab
  188.9 8.4 %all-to-all-start.2 = ((bf16[64,29,8,128]{3,2,1,0:T(8,128)(2,1)}), bf16[64,29,8,128]{3,2,1,0:T(8,128)(2,1)}, u32[]{:S(2)}, u32[]{:S(2)}) async-start(bf16[64,29,8,128]{3,2,1,0:T(8,128)(2,1)} %get-tuple-element.21), calls=%async_computation.2 | async-start | bytes 7602176 | tf_op jit(solution)/shard_map/all_to_all | solution.py:600
  197.3 3.4 collective-permute-start.2
  200.7 1.0 constant_dynamic-slice_fusion
  201.7 0.0 collective-permute-start.5
  201.8 2.9 collective-permute-start.4
  204.7 0.0 collective-permute-start.3
  204.7 9.4 %fusion.6 = f32[1440,1440]{1,0:T(8,128)} fusion(bf16[1440,640]{1,0:T(8,128)(2,1)} %get-tuple-element.26, bf16[80,8,1440]{2,1,0:T(8,128)(2,1)} %get-tuple-element.25), kind=kOutput, calls=%fused_computation.9 | convolution fusion | flops 2654208000 | bytes 11980800 | tf_op jit(solution)/shard_map/dot_general | solution.py:604
  214.2 5.7 %fusion.4 = f32[720,2880]{1,0:T(8,128)} fusion(bf16[80,8,2880]{2,1,0:T(8,128)(2,1)S(1)} %copy-done.11, bf16[1440,640]{1,0:T(8,128)(2,1)S(1)} %copy-done.5, s32[]{:T(128)S(6)} %select_n.6), kind=kOutput, calls=%fused_computation.7 | convolution fusion | flops 2654208000 | bytes 12984324 | tf_op jit(solution)/shard_map/dot_general | solution.py:34
  219.9 4.5 %unpack_other.1 = bf16[80,8,2880]{2,1,0:T(8,128)(2,1)} custom-call(s32[1]{0:T(128)} %bitcast.3.zl_ref, bf16[32,58,8,128]{3,2,1,0:T(8,128)(2,1)} %all-to-all-done.3.slab), custom_call_target="tpu_custom_call" | custom-call | tf_op jit(solution)/shard_map/unpack_other/pallas_call | solution.py:496
  224.4 0.0 slice-start.1
  224.4 77.5 %collective-permute-done.5 = bf16[720,640]{1,0:T(8,128)(2,1)} collective-permute-done((bf16[720,640]{1,0:T(8,128)(2,1)}, bf16[720,640]{1,0:T(8,128)(2,1)}, u32[]{:S(2)}, u32[]{:S(2)}) %collective-permute-start.5) | collective-permute-done | bytes 921632 | tf_op jit(solution)/shard_map/ppermute | solution.py:577
  301.9 10.5 %fusion.2 = bf16[1,720,2880]{2,1,0:T(8,128)(2,1)} fusion(f32[720,2880]{1,0:T(8,128)} %fusion.4, bf16[720,640]{1,0:T(8,128)(2,1)} %collective-permute-done.5, bf16[80,8,2880]{2,1,0:T(8,128)(2,1)} %unpack_other.1), kind=kOutput, calls=%fused_computation.5 | convolution fusion | flops 2658355200 | bytes 17049600 | tf_op jit(solution)/shard_map/dot_general | solution.py:34
  312.4 13.1 %collective-permute-done.4 = bf16[1440,384]{1,0:T(8,128)(2,1)S(1)} collective-permute-done((bf16[1440,384]{1,0:T(8,128)(2,1)}, bf16[1440,384]{1,0:T(8,128)(2,1)S(1)}, u32[]{:S(2)}, u32[]{:S(2)}) %collective-permute-start.4) | collective-permute-done | bytes 1105952 | tf_op jit(solution)/shard_map/ppermute | solution.py:577
  325.5 3.8 %convolution_add_fusion = f32[1440,1440]{1,0:T(8,128)S(1)} fusion(f32[1440,1440]{1,0:T(8,128)S(1)} %bitcast.29, bf16[1440,384]{1,0:T(8,128)(2,1)S(1)} %collective-permute-done.4, bf16[1440,640]{1,0:T(8,128)(2,1)} %collective-permute-done.2), kind=kOutput, calls=%fused_computation | convolution fusion | flops 1594598400 | bytes 18800640 | tf_op jit(solution)/shard_map/dot_general | solution.py:38
  329.4 12.0 %collective-permute-done.3 = bf16[1440,256]{1,0:T(8,128)(2,1)} collective-permute-done((bf16[1440,256]{1,0:T(8,128)(2,1)}, bf16[1440,256]{1,0:T(8,128)(2,1)}, u32[]{:S(2)}, u32[]{:S(2)}) %collective-permute-start.3) | collective-permute-done | bytes 737312 | tf_op jit(solution)/shard_map/ppermute | solution.py:577
  341.4 4.8 %fusion.1 = bf16[1,1440,1440]{2,1,0:T(8,128)(2,1)} fusion(f32[1440,1440]{1,0:T(8,128)S(1)} %convolution_add_fusion, bf16[1440,256]{1,0:T(8,128)(2,1)} %collective-permute-done.3, bf16[1440,640]{1,0:T(8,128)(2,1)} %collective-permute-done.2), kind=kOutput, calls=%fused_computation.4 | convolution fusion | flops 1065830400 | bytes 13916160 | tf_op jit(solution)/shard_map/dot_general | solution.py:38
  346.2 4.9 %combine.1 = bf16[2880,128]{1,0:T(8,128)(2,1)} custom-call(f32[512,128]{1,0:T(8,128)} %get-tuple-element.16.rank_ref, bf16[64,29,8,128]{3,2,1,0:T(8,128)(2,1)} %all-to-all-done.2.ret_ref), custom_call_target="tpu_custom_call" | custom-call | tf_op jit(solution)/shard_map/combine/pallas_call | solution.py:543
  (25 shorter events, 0.0 us)
Async XLA Ops:
  5.2 10.7 %copy-start = (bf16[128,2880]{0,1:T(8,128)(2,1)S(1)}, bf16[128,2880]{0,1:T(8,128)(2,1)}, u32[]{:S(2)}) copy-start(bf16[128,2880]{0,1:T(8,128)(2,1)} %param.7) | copy-start | bytes 2211844
  5.2 12.2 %copy-start.6 = (f32[8,128]{1,0:T(8,128)S(1)}, f32[8,128]{1,0:T(8,128)}, u32[]{:S(2)}) copy-start(f32[8,128]{1,0:T(8,128)} %get-tuple-element.17.ma_ref) | copy-start | bytes 12292
  5.2 75.4 %all-to-all-start.1 = ((bf16[64,29,8,128]{3,2,1,0:T(8,128)(2,1)}), bf16[64,29,8,128]{3,2,1,0:T(8,128)(2,1)}, u32[]{:S(2)}, u32[]{:S(2)}) async-start(bf16[64,29,8,128]{3,2,1,0:T(8,128)(2,1)} %get-tuple-element.18), calls=%async_computation.1 | async-start | bytes 7602176 | tf_op jit(solution)/shard_map/all_to_all | solution.py:585
  15.9 59.4 %collective-permute-start = (bf16[2880,128]{1,0:T(8,128)(2,1)S(1)}, bf16[2880,128]{1,0:T(8,128)(2,1)S(1)}, u32[]{:S(2)}, u32[]{:S(2)}) collective-permute-start(bf16[2880,128]{1,0:T(8,128)(2,1)S(1)} %bitcast.33), channel_id=1, source_target_pairs={{0,32},{1,33},{2,34},{3,35},{4,36},{5,37},{6,38},{7,39},{8,40},{9,... | collective-permute-start | bytes 2211848 | tf_op jit(solution)/shard_map/ppermute | solution.py:577
  17.4 57.8 %collective-permute-start.1 = (f32[8,128]{1,0:T(8,128)S(1)}, f32[8,128]{1,0:T(8,128)S(1)}, u32[]{:S(2)}, u32[]{:S(2)}) collective-permute-start(f32[8,128]{1,0:T(8,128)S(1)} %copy-done.6), channel_id=1, source_target_pairs={{0,32},{1,33},{2,34},{3,35},{4,36},{5,37},{6,38},{7,39},{8,40},{9,... | collective-permute-start | bytes 12296 | tf_op jit(solution)/shard_map/ppermute | solution.py:577
  75.2 0.6 copy-start.10
  75.2 0.9 copy-start.4
  80.6 7.7 %copy-start.1 = (bf16[128,2880]{0,1:T(8,128)(2,1)S(1)}, bf16[128,2880]{0,1:T(8,128)(2,1)}, u32[]{:S(2)}) copy-start(bf16[128,2880]{0,1:T(8,128)(2,1)} %param.7) | copy-start | bytes 2211844
  80.6 11.1 %copy-start.7 = (f32[8,128]{1,0:T(8,128)S(1)}, f32[8,128]{1,0:T(8,128)}, u32[]{:S(2)}) copy-start(f32[8,128]{1,0:T(8,128)} %get-tuple-element.17.ma_ref) | copy-start | bytes 12292
  80.7 54.4 %all-to-all-start = ((bf16[32,58,8,128]{3,2,1,0:T(8,128)(2,1)}), bf16[32,58,8,128]{3,2,1,0:T(8,128)(2,1)}, u32[]{:S(2)}, u32[]{:S(2)}) async-start(bf16[32,58,8,128]{3,2,1,0:T(8,128)(2,1)} %shard_map.85), calls=%async_computation | async-start | bytes 7602176 | tf_op jit(solution)/shard_map/all_to_all | solution.py:587
  88.3 36.4 %collective-permute-start.6 = (bf16[2880,128]{1,0:T(8,128)(2,1)S(1)}, bf16[2880,128]{1,0:T(8,128)(2,1)S(1)}, u32[]{:S(2)}, u32[]{:S(2)}) collective-permute-start(bf16[2880,128]{1,0:T(8,128)(2,1)S(1)} %bitcast.34), channel_id=1, source_target_pairs={{0,64},{1,65},{2,66},{3,67},{4,68},{5,69},{6,70},{7,71},{8,72},{9,... | collective-permute-start | bytes 2211848 | tf_op jit(solution)/shard_map/ppermute | solution.py:577
  91.7 33.0 %collective-permute-start.7 = (bf16[2880,128]{1,0:T(8,128)(2,1)S(1)}, bf16[2880,128]{1,0:T(8,128)(2,1)S(1)}, u32[]{:S(2)}, u32[]{:S(2)}) collective-permute-start(bf16[2880,128]{1,0:T(8,128)(2,1)S(1)} %bitcast.35), channel_id=1, source_target_pairs={{0,96},{1,97},{2,98},{3,99},{4,100},{5,101},{6,102},{7,103},{8,104... | collective-permute-start | bytes 2211848 | tf_op jit(solution)/shard_map/ppermute | solution.py:577
  91.7 16.8 %collective-permute-start.8 = (f32[8,128]{1,0:T(8,128)S(1)}, f32[8,128]{1,0:T(8,128)S(1)}, u32[]{:S(2)}, u32[]{:S(2)}) collective-permute-start(f32[8,128]{1,0:T(8,128)S(1)} %copy-done.7), channel_id=1, source_target_pairs={{0,64},{1,65},{2,66},{3,67},{4,68},{5,69},{6,70},{7,71},{8,72},{9,... | collective-permute-start | bytes 12296 | tf_op jit(solution)/shard_map/ppermute | solution.py:577
  92.9 31.8 %collective-permute-start.9 = (f32[8,128]{1,0:T(8,128)S(1)}, f32[8,128]{1,0:T(8,128)S(1)}, u32[]{:S(2)}, u32[]{:S(2)}) collective-permute-start(f32[8,128]{1,0:T(8,128)S(1)} %copy-done.7), channel_id=1, source_target_pairs={{0,96},{1,97},{2,98},{3,99},{4,100},{5,101},{6,102},{7,103},{8,104... | collective-permute-start | bytes 12296 | tf_op jit(solution)/shard_map/ppermute | solution.py:577
  108.5 16.2 %copy-start.8 = (f32[8,128]{1,0:T(8,128)}, f32[8,128]{1,0:T(8,128)S(1)}, u32[]{:S(2)}) copy-start(f32[8,128]{1,0:T(8,128)S(1)} %collective-permute-done.8.ma_ref) | copy-start | bytes 12292
  124.7 0.6 copy-start.9
  124.7 0.9 copy-start.2
  125.6 0.9 copy-start.3
  135.1 53.9 %all-to-all-start.3 = ((bf16[32,58,8,128]{3,2,1,0:T(8,128)(2,1)}), bf16[32,58,8,128]{3,2,1,0:T(8,128)(2,1)}, u32[]{:S(2)}, u32[]{:S(2)}) async-start(bf16[32,58,8,128]{3,2,1,0:T(8,128)(2,1)} %shard_map.86), calls=%async_computation.3 | async-start | bytes 7602176 | tf_op jit(solution)/shard_map/all_to_all | solution.py:589
  188.9 11.8 %copy-start.5 = (bf16[1440,640]{1,0:T(8,128)(2,1)S(1)}, bf16[1440,640]{1,0:T(8,128)(2,1)}, u32[]{:S(2)}) copy-start(bf16[1440,640]{1,0:T(8,128)(2,1)} %get-tuple-element.27) | copy-start | bytes 5529604
  188.9 157.3 %all-to-all-start.2 = ((bf16[64,29,8,128]{3,2,1,0:T(8,128)(2,1)}), bf16[64,29,8,128]{3,2,1,0:T(8,128)(2,1)}, u32[]{:S(2)}, u32[]{:S(2)}) async-start(bf16[64,29,8,128]{3,2,1,0:T(8,128)(2,1)} %get-tuple-element.21), calls=%async_computation.2 | async-start | bytes 7602176 | tf_op jit(solution)/shard_map/all_to_all | solution.py:600
  197.3 128.2 %collective-permute-start.2 = (bf16[1440,640]{1,0:T(8,128)(2,1)}, bf16[1440,640]{1,0:T(8,128)(2,1)}, u32[]{:S(2)}, u32[]{:S(2)}) collective-permute-start(bf16[1440,640]{1,0:T(8,128)(2,1)} %get-tuple-element.22), channel_id=1, source_target_pairs={{0,64},{1,65},{2,66},{3,67},{4,68},{5,69},{6,70},{7,71},{8,72},{9,... | collective-permute-start | bytes 5529608 | tf_op jit(solution)/shard_map/ppermute | solution.py:577
  201.7 100.2 %collective-permute-start.5 = (bf16[720,640]{1,0:T(8,128)(2,1)}, bf16[720,640]{1,0:T(8,128)(2,1)}, u32[]{:S(2)}, u32[]{:S(2)}) collective-permute-start(bf16[720,640]{1,0:T(8,128)(2,1)} %constant_dynamic-slice_fusion), channel_id=1, source_target_pairs={{0,64},{1,65},{2,66},{3,67},{4,68},{5,69},{6,70},{7,71},{8,72},{9,... | collective-permute-start | bytes 2764808 | tf_op jit(solution)/shard_map/ppermute | solution.py:577
  201.8 123.7 %collective-permute-start.4 = (bf16[1440,384]{1,0:T(8,128)(2,1)}, bf16[1440,384]{1,0:T(8,128)(2,1)S(1)}, u32[]{:S(2)}, u32[]{:S(2)}) collective-permute-start(bf16[1440,384]{1,0:T(8,128)(2,1)} %get-tuple-element.24), channel_id=1, source_target_pairs={{0,64},{1,65},{2,66},{3,67},{4,68},{5,69},{6,70},{7,71},{8,72},{9,... | collective-permute-start | bytes 3317768 | tf_op jit(solution)/shard_map/ppermute | solution.py:577
  204.7 136.7 %collective-permute-start.3 = (bf16[1440,256]{1,0:T(8,128)(2,1)}, bf16[1440,256]{1,0:T(8,128)(2,1)}, u32[]{:S(2)}, u32[]{:S(2)}) collective-permute-start(bf16[1440,256]{1,0:T(8,128)(2,1)} %get-tuple-element.23), channel_id=1, source_target_pairs={{0,64},{1,65},{2,66},{3,67},{4,68},{5,69},{6,70},{7,71},{8,72},{9,... | collective-permute-start | bytes 2211848 | tf_op jit(solution)/shard_map/ppermute | solution.py:577
  204.7 9.4 %copy-start.11 = (bf16[80,8,2880]{2,1,0:T(8,128)(2,1)S(1)}, bf16[80,8,2880]{2,1,0:T(8,128)(2,1)}, u32[]{:S(2)}) copy-start(bf16[80,8,2880]{2,1,0:T(8,128)(2,1)} %get-tuple-element.28) | copy-start | bytes 11059204
  219.9 105.6 %slice-start = ((s8[8847360]{0:T(1024)(128)(4,1)}), s8[458752]{0:T(1024)(128)(4,1)S(1)}, s32[]{:S(2)}) async-start(s8[8847360]{0:T(1024)(128)(4,1)} %bitcast.28), calls=%async_computation.4 | async-start | bytes 917504
  224.4 101.1 %slice-start.1 = ((s8[8847360]{0:T(1024)(128)(4,1)}), s8[4194304]{0:T(1024)(128)(4,1)S(1)}, s32[]{:S(2)}) async-start(s8[8847360]{0:T(1024)(128)(4,1)} %bitcast.28), calls=%async_computation.5 | async-start | bytes 8388608
  224.4 101.1 %slice-start.2 = ((s8[8847360]{0:T(1024)(128)(4,1)}), s8[4194304]{0:T(1024)(128)(4,1)S(1)}, s32[]{:S(2)}) async-start(s8[8847360]{0:T(1024)(128)(4,1)} %bitcast.28), calls=%async_computation.6 | async-start | bytes 8388608
